TPU v7x, 768 devices: a whole 4x8x12 slice. The times are simulated.
768 devices in a mesh: mem: 48 (over z, y_lo, core), slab: 16 (over x, y_hi).
Axes of the slice: x: 4, y: 8 (y_hi: 4, y_lo: 2; y = y_hi * 2 + y_lo), z: 12, core: 2. Of those that a mesh axis runs over, the one named last changes fastest.
Arguments:
- thickness: float32 [384, 1024, 384], P('mem', 'slab'), may hold values from 0.5 to 2.5
- face_u: float32 [1024, 384], P('slab'), may hold values from -0.4 to 0.4
- face_v: float32 [1024, 384], P('slab'), may hold values from -0.4 to 0.4
- obs_cells: int32 [2048, 4], P('slab'), may hold values from 0 to 393215, as said below
- obs_weights: int32 [2048, 4], P('slab'), may hold values from 1 to 4
- obs_values: float32 [2048], P('slab'), may hold values from -6 to 6
- obs_noise: float32 [384, 2048], P('mem', 'slab'), may hold values from -3 to 3
- cov_inverse: float32 [2048, 2048], P('slab'), may hold values from -0.1875 to 0.1875
- taper_mask: int32 [16, 16], replicated, may hold values from 0 to 1, as said below
Outputs:
- analysis: float32 [384, 1024, 384], P('mem', 'slab')
Inputs may be any that keep to these rules, and one draw needn't show every extreme that they name: `obs_cells`: observation o covers a 2 x 2 square of cells, all within the rows of slab o // 128. `taper_mask`: entries are 0 or 1 and the diagonal is 1.
All inputs are finite; a program needn't handle non-finite values.
Results may differ from a plain program's by a relative error of at most 0.0003.
Values sent between devices are 32-bit elements; how exact they have to be, the bound alone decides.
No kernel may reach another device: no remote copies, remote signals or barrier semaphores. Data moves between devices by JAX's collectives and lax.ppermute only.
A program may use at most 64 MiB of HBM per device.

v0:
```python
import jax
import jax.numpy as jnp
from jax import lax
from jax.sharding import PartitionSpec as P


def padded_2(block, sides, width):
    for axis, dim in sides:
        count = lax.axis_size(axis)
        forward = [(i, i + 1) for i in range(count - 1)]
        backward = [(target, source) for source, target in forward]
        low = lax.ppermute(
            lax.slice_in_dim(block, block.shape[dim] - width, None, axis=dim), axis, forward
        )
        high = lax.ppermute(lax.slice_in_dim(block, 0, width, axis=dim), axis, backward)
        block = jnp.concatenate([low, block, high], axis=dim)
    return block


def split_up(x, dim, peers):
    dims = x.shape
    pieces = x.reshape(*dims[:dim], peers, dims[dim] // peers, *dims[dim + 1 :])
    return jnp.moveaxis(pieces, dim, 0)


def sent_and_summed(x, axis, dim):
    pieces = split_up(x, dim, lax.axis_size(axis))
    arrived = lax.all_to_all(pieces, axis, split_axis=0, concat_axis=0, tiled=True)
    return arrived.sum(axis=0)


def in_one_piece(arrays, axis, dim, along):
    ends, at = ([], 0)
    for a in arrays[:-1]:
        at += a.shape[along]
        ends.append(at)
    both = jnp.concatenate(arrays, axis=along)
    return tuple(jnp.split(lax.all_gather(both, axis, axis=dim, tiled=True), ends, axis=along))


def joined_along(pieces, dim):
    dims = list(pieces.shape[1:])
    dims[dim] *= pieces.shape[0]
    return jnp.moveaxis(pieces, 0, dim).reshape(dims)


def copy_for_each(x, axis):
    peers = lax.axis_size(axis)
    return lax.all_to_all(jnp.broadcast_to(x[None], (peers, *x.shape)), axis, 0, 0, tiled=True)


def collect(x, axis, dim):
    return joined_along(copy_for_each(x, axis), dim)


def minmod(first_diff, second_diff):
    return (
        0.5
        * (jnp.sign(first_diff) + jnp.sign(second_diff))
        * jnp.minimum(jnp.abs(first_diff), jnp.abs(second_diff))
    )


def face_flux(padded, velocity, axis_dim):
    counted = padded.shape[axis_dim] - 3
    far_low = lax.slice_in_dim(padded, 0, counted, axis=axis_dim)
    near_low = lax.slice_in_dim(padded, 1, 1 + counted, axis=axis_dim)
    near_high = lax.slice_in_dim(padded, 2, 2 + counted, axis=axis_dim)
    far_high = lax.slice_in_dim(padded, 3, 3 + counted, axis=axis_dim)
    left_state = near_low + 0.5 * minmod(near_low - far_low, near_high - near_low)
    right_state = near_high - 0.5 * minmod(near_high - near_low, far_high - near_high)
    return jnp.maximum(velocity, 0.0) * left_state + jnp.minimum(velocity, 0.0) * right_state


def local(
    thickness,
    face_u,
    face_v,
    obs_cells,
    obs_weights,
    obs_values,
    obs_noise,
    cov_inverse,
    taper_mask,
):
    member_subset = thickness.shape[0]
    band_rows = thickness.shape[1]
    column_list = thickness.shape[2]
    slab_index = lax.axis_index("slab")
    stacked = jnp.concatenate([thickness, face_v[None]], 0)
    padded = padded_2(stacked, (("slab", 1),), 2)
    row_pad = padded[:member_subset]
    row_speed = padded[member_subset, 2 : band_rows + 3]
    row_fluxes = face_flux(row_pad, row_speed, 1)
    col_pad = jnp.pad(thickness, ((0, 0), (0, 0), (2, 2)))
    col_speed = jnp.pad(face_u, ((0, 0), (0, 1)))
    column_fluxes = face_flux(col_pad, col_speed, 2)
    prior_state = (
        thickness
        - (column_fluxes[:, :, 1:] - column_fluxes[:, :, :-1])
        - (row_fluxes[:, 1:, :] - row_fluxes[:, :-1, :])
    )
    state_vector = prior_state.reshape(member_subset, band_rows * column_list)
    local_cells = obs_cells - slab_index * (band_rows * column_list)
    weights = obs_weights.astype(jnp.float32)
    picked = state_vector[:, local_cells]
    obs_model = jnp.sum(picked * weights[None], -1) / jnp.sum(weights, -1)[None]
    innovation = obs_values[None, :] + obs_noise - obs_model
    white_terms = jnp.dot(innovation, cov_inverse, precision=lax.Precision.HIGHEST)
    whitened = sent_and_summed(white_terms, "slab", 1)
    model_all, white_all = in_one_piece((obs_model, whitened), "mem", 0, 1)
    obs_mean = jnp.mean(model_all, 0, keepdims=True)
    cell_state = lax.all_to_all(state_vector, "mem", split_axis=1, concat_axis=0, tiled=True)
    members = cell_state.shape[0]
    anomaly = cell_state - jnp.mean(cell_state, 0, keepdims=True)
    local_anomaly = obs_model - obs_mean
    partial_block = lax.dot_general(
        local_anomaly, white_all, (((1,), (1,)), ((), ())), precision=lax.Precision.HIGHEST
    )
    mask_column = lax.dynamic_slice_in_dim(taper_mask, slab_index, 1, 1)[:, 0].astype(jnp.float32)
    mixed_rows = sent_and_summed(
        (mask_column[:, None, None] * partial_block[None]).reshape(
            member_subset * lax.axis_size("slab"), members
        ),
        "slab",
        0,
    )
    ensemble = collect(mixed_rows, "mem", 0)
    update = lax.dot_general(
        ensemble, anomaly, (((0,), (0,)), ((), ())), precision=lax.Precision.HIGHEST
    ) / (members - 1)
    analysis_cells = cell_state + update
    returned = lax.all_to_all(analysis_cells, "mem", split_axis=0, concat_axis=1, tiled=True)
    return returned.reshape(member_subset, band_rows, column_list)


def solution(mesh):
    return jax.shard_map(
        local,
        mesh=mesh,
        in_specs=(
            P("mem", "slab", None),
            P("slab", None),
            P("slab", None),
            P("slab", None),
            P("slab", None),
            P("slab"),
            P("mem", "slab"),
            P("slab", None),
            P(),
        ),
        out_specs=P("mem", "slab", None),
        check_vma=False,
    )
```

profile of v0, /device:TPU:1, one launch (start us, length us, event | category | flops | bytes accessed | tf_op | source)
XLA Modules:
  0.0 243.9 jit_solution(1153771185223298034)
XLA Ops:
  0.0 1.1 pad_maximum_fusion.3
  1.1 1.3 collective-permute-start
  2.4 5.7 %collective-permute-start.1 = (f32[9,2,384]{2,1,0:T(2,128)S(1)}, f32[9,2,384]{2,1,0:T(2,128)S(1)}, u32[]{:S(2)}, u32[]{:S(2)}) collective-permute-start(f32[9,2,384]{2,1,0:T(2,128)S(1)} %get-tuple-element.9), channel_id=1, source_target_pairs={{0,1},{1,2},{2,3},{3,4},{4,5},{5,6},{6,7},{7,8},{8,9},{9,10},{10,1... | collective-permute-start | bytes 82952 | tf_op jit(solution)/shard_map/ppermute | solution.py:12
  8.1 0.9 pad_maximum_fusion.1
  10.0 4.7 %multiply_add_fusion = f32[8,64,385]{2,1,0:T(8,128)} fusion(f32[8,64,384]{2,1,0:T(8,128)} %param.9, f32[64,385]{1,0:T(8,128)S(1)} %get-tuple-element.12, f32[64,385]{1,0:T(8,128)S(1)} %get-tuple-element.11), kind=kLoop, calls=%fused_computation.12 | loop fusion | flops 4730880 | bytes 1772032 | tf_op jit(solution)/shard_map/add | solution.py:72
  17.1 1.6 maximum_maximum_fusion
  18.7 1.3 multiply_add_fusion.1
  20.1 1.8 fusion.5
  21.9 6.6 %copy.51 = f32[8,64,384]{0,2,1:T(8,128)} copy(f32[8,64,384]{2,1,0:T(8,128)S(1)} %fusion.5) | data formatting | bytes 1572864 | tf_op jit(solution)/shard_map/sub | solution.py:99
  28.5 5.6 %gather_fusion = f32[512,8]{1,0:T(8,128)S(1)} fusion(f32[8,24576]{0,1:T(8,128)} %bitcast.32, s32[1024]{0:T(1024)S(1)} %pad_clamp_fusion), kind=kCustom, calls=%fused_computation | custom fusion | bytes 34816 | tf_op jit(solution)/shard_map/gather | solution.py:106
  34.5 1.2 convolution_bitcast_fusion.1
  35.7 10.0 %all-to-all-start.1 = ((f32[16,8,128]{2,1,0:T(8,128)}), f32[16,8,128]{2,1,0:T(8,128)S(1)}, u32[]{:S(2)}, u32[]{:S(2)}) async-start(f32[16,8,128]{2,1,0:T(8,128)} %convolution_bitcast_fusion.1), calls=%async_computation.1 | async-start | bytes 131072 | tf_op jit(solution)/shard_map/all_to_all | solution.py:28
  45.9 8.8 %all-to-all-done.1 = f32[16,8,128]{2,1,0:T(8,128)S(1)} async-done(((f32[16,8,128]{2,1,0:T(8,128)}), f32[16,8,128]{2,1,0:T(8,128)S(1)}, u32[]{:S(2)}, u32[]{:S(2)}) %all-to-all-start.1) | async-done | bytes 65568 | tf_op jit(solution)/shard_map/all_to_all | solution.py:28
  54.8 61.2 %all_gather.3 = f32[384,256]{1,0:T(8,128)S(1)} all-gather(f32[8,256]{1,0:T(8,128)S(1)} %pad_maximum_fusion.5), channel_id=1, replica_groups=mesh['mem'=48,'slab'=16] {'mem'}, dimensions={0}, use_global_device_ids=true | all-gather | bytes 401408 | tf_op jit(solution)/shard_map/all_gather | solution.py:38
  117.1 3.5 %all-to-all-start.2 = ((f32[16,8,384]{2,1,0:T(8,128)}), f32[16,8,384]{2,1,0:T(8,128)S(1)}, u32[]{:S(2)}, u32[]{:S(2)}) async-start(f32[16,8,384]{2,1,0:T(8,128)} %broadcast_multiply_fusion), calls=%async_computation.2 | async-start | bytes 393216 | tf_op jit(solution)/shard_map/all_to_all | solution.py:28
  120.9 1.3 copy.50
  122.2 9.4 %all-to-all-done.2 = f32[16,8,384]{2,1,0:T(8,128)S(1)} async-done(((f32[16,8,384]{2,1,0:T(8,128)}), f32[16,8,384]{2,1,0:T(8,128)S(1)}, u32[]{:S(2)}, u32[]{:S(2)}) %all-to-all-start.2) | async-done | bytes 196640 | tf_op jit(solution)/shard_map/all_to_all | solution.py:28
  131.6 5.5 %all-to-all-start = ((f32[8,48,512]{2,0,1:T(8,128)}), f32[8,48,512]{2,0,1:T(8,128)S(1)}, u32[]{:S(2)}, u32[]{:S(2)}) async-start(f32[8,48,512]{2,0,1:T(8,128)} %copy.50), calls=%async_computation | async-start | bytes 1572864 | tf_op jit(solution)/shard_map/all_to_all | solution.py:113
  137.2 33.5 %all-to-all-done = f32[8,48,512]{2,0,1:T(8,128)S(1)} async-done(((f32[8,48,512]{2,0,1:T(8,128)}), f32[8,48,512]{2,0,1:T(8,128)S(1)}, u32[]{:S(2)}, u32[]{:S(2)}) %all-to-all-start) | async-done | bytes 786464 | tf_op jit(solution)/shard_map/all_to_all | solution.py:113
  171.5 4.5 %all-to-all-start.3 = ((f32[48,8,384]{2,1,0:T(8,128)}), f32[48,8,384]{2,1,0:T(8,128)S(1)}, u32[]{:S(2)}, u32[]{:S(2)}) async-start(f32[48,8,384]{2,1,0:T(8,128)} %broadcast_in_dim.8), calls=%async_computation.3 | async-start | bytes 1179648 | tf_op jit(solution)/shard_map/all_to_all | solution.py:49
  176.1 27.1 %all-to-all-done.3 = f32[48,8,384]{2,1,0:T(8,128)S(1)} async-done(((f32[48,8,384]{2,1,0:T(8,128)}), f32[48,8,384]{2,1,0:T(8,128)S(1)}, u32[]{:S(2)}, u32[]{:S(2)}) %all-to-all-start.3) | async-done | bytes 589856 | tf_op jit(solution)/shard_map/all_to_all | solution.py:49
  203.2 1.4 fusion.2
  204.7 37.7 %all_to_all.50 = f32[48,8,512]{2,1,0:T(8,128)S(1)} all-to-all(f32[48,8,512]{2,1,0:T(8,128)S(1)} %fusion.2), channel_id=1, replica_groups=mesh['mem'=48,'slab'=16] {'mem'}, dimensions={0} | all-to-all | bytes 1572864 | tf_op jit(solution)/shard_map/all_to_all | solution.py:133
  242.9 1.1 reshape.47
  (37 shorter events, 6.7 us)
Async XLA Ops:
  0.0 34.5 %copy-start = (f32[128,2048]{1,0:T(8,128)S(1)}, f32[128,2048]{1,0:T(8,128)}, u32[]{:S(2)}) copy-start(f32[128,2048]{1,0:T(8,128)} %param.16) | copy-start | bytes 3145732
  0.0 20.1 %copy-start.1 = (f32[8,64,384]{2,1,0:T(8,128)S(1)}, f32[8,64,384]{2,1,0:T(8,128)}, u32[]{:S(2)}) copy-start(f32[8,64,384]{2,1,0:T(8,128)} %param.9) | copy-start | bytes 2359300
  1.1 15.0 %collective-permute-start = (f32[9,2,384]{2,1,0:T(2,128)S(1)}, f32[9,2,384]{2,1,0:T(2,128)S(1)}, u32[]{:S(2)}, u32[]{:S(2)}) collective-permute-start(f32[9,2,384]{2,1,0:T(2,128)S(1)} %get-tuple-element.10), channel_id=1, source_target_pairs={{1,0},{2,1},{3,2},{4,3},{5,4},{6,5},{7,6},{8,7},{9,8},{10,9},{11,1... | collective-permute-start | bytes 82952 | tf_op jit(solution)/shard_map/ppermute | solution.py:15
  2.4 14.7 %collective-permute-start.1 = (f32[9,2,384]{2,1,0:T(2,128)S(1)}, f32[9,2,384]{2,1,0:T(2,128)S(1)}, u32[]{:S(2)}, u32[]{:S(2)}) collective-permute-start(f32[9,2,384]{2,1,0:T(2,128)S(1)} %get-tuple-element.9), channel_id=1, source_target_pairs={{0,1},{1,2},{2,3},{3,4},{4,5},{5,6},{6,7},{7,8},{8,9},{9,10},{10,1... | collective-permute-start | bytes 82952 | tf_op jit(solution)/shard_map/ppermute | solution.py:12
  20.1 14.4 %copy-start.3 = (f32[8,128]{1,0:T(8,128)S(1)}, f32[8,128]{1,0:T(8,128)}, u32[]{:S(2)}) copy-start(f32[8,128]{1,0:T(8,128)} %param.15) | copy-start | bytes 12292
  20.1 14.4 %copy-start.4 = (f32[128]{0:T(128)S(1)}, f32[128]{0:T(128)}, u32[]{:S(2)}) copy-start(f32[128]{0:T(128)} %param.14) | copy-start | bytes 1540
  20.1 25.6 %copy-start.2 = (s32[16,16]{1,0:T(8,128)S(1)}, s32[16,16]{1,0:T(8,128)}, u32[]{:S(2)}) copy-start(s32[16,16]{1,0:T(8,128)} %param.17) | copy-start | bytes 3076
  35.7 19.0 %all-to-all-start.1 = ((f32[16,8,128]{2,1,0:T(8,128)}), f32[16,8,128]{2,1,0:T(8,128)S(1)}, u32[]{:S(2)}, u32[]{:S(2)}) async-start(f32[16,8,128]{2,1,0:T(8,128)} %convolution_bitcast_fusion.1), calls=%async_computation.1 | async-start | bytes 131072 | tf_op jit(solution)/shard_map/all_to_all | solution.py:28
  117.1 14.5 %all-to-all-start.2 = ((f32[16,8,384]{2,1,0:T(8,128)}), f32[16,8,384]{2,1,0:T(8,128)S(1)}, u32[]{:S(2)}, u32[]{:S(2)}) async-start(f32[16,8,384]{2,1,0:T(8,128)} %broadcast_multiply_fusion), calls=%async_computation.2 | async-start | bytes 393216 | tf_op jit(solution)/shard_map/all_to_all | solution.py:28
  131.6 39.0 %all-to-all-start = ((f32[8,48,512]{2,0,1:T(8,128)}), f32[8,48,512]{2,0,1:T(8,128)S(1)}, u32[]{:S(2)}, u32[]{:S(2)}) async-start(f32[8,48,512]{2,0,1:T(8,128)} %copy.50), calls=%async_computation | async-start | bytes 1572864 | tf_op jit(solution)/shard_map/all_to_all | solution.py:113
  171.5 31.7 %all-to-all-start.3 = ((f32[48,8,384]{2,1,0:T(8,128)}), f32[48,8,384]{2,1,0:T(8,128)S(1)}, u32[]{:S(2)}, u32[]{:S(2)}) async-start(f32[48,8,384]{2,1,0:T(8,128)} %broadcast_in_dim.8), calls=%async_computation.3 | async-start | bytes 1179648 | tf_op jit(solution)/shard_map/all_to_all | solution.py:49
where the time goes:
time: 245 us; the launch traced here: 244 us
  blocking collectives  99 us (40%)
  waiting for transfers between devices  78.8 us (32%)
  starting transfers between devices  30.5 us (12%)
  local copies, waits for them, and re-layouts  16.6 us (7%)
  other arithmetic  15.9 us (6%)
  matrix products  2.98 us (1%)
    all_gather x1, blocking collectives, in_one_piece(): lax.all_gather(both, axis, axis=dim, tiled=True)  61.2 us
    all_to_all x1, blocking collectives, local(): lax.all_to_all(analysis_cells, 'mem', split_axis=0, concat_axis=1, tiled=...  37.7 us
    all_to_all x1, waiting for transfers between devices, local(): lax.all_to_all(state_vector, 'mem', split_axis=1, concat_axis=0, tiled=True)  33.5 us
    all_to_all x1, waiting for transfers between devices, copy_for_each(): lax.all_to_all(jnp.broadcast_to(x[None], (peers, *x.shape)), axis, 0, 0,...  27.1 us
    all_to_all x2, waiting for transfers between devices, sent_and_summed(): lax.all_to_all(pieces, axis, split_axis=0, concat_axis=0, tiled=True)  18.2 us
    all_to_all x2, starting transfers between devices, sent_and_summed(): lax.all_to_all(pieces, axis, split_axis=0, concat_axis=0, tiled=True)  13.5 us
    sub x1, local copies, waits for them, and re-layouts, local(): thickness - (column_fluxes[:, :, 1:] - column_fluxes[:, :, :-1])  6.65 us
    add x2, other arithmetic, face_flux(): jnp.maximum(velocity, 0.0) * left_state  6.01 us
  transfers between devices with their start and end apart: 6, of which 4 were waited for; matrix products, arithmetic and copies ran while one was open for 4% of the time, Pallas kernels for 0%

commit v1 on v0

v1 whole, which is shorter than its diff:
```python
import jax
import jax.numpy as jnp
from jax import lax
from jax.experimental import pallas as pl
from jax.experimental.pallas import tpu as pltpu
from jax.sharding import PartitionSpec as P


LANES = 128
PLANE = 4
RUN = 4
COLUMN = 4
HIGHEST = lax.Precision.HIGHEST
SMEM = pltpu.SMEM
VMEM = pltpu.VMEM


def minmod(a, b):
    return jnp.maximum(jnp.minimum(a, b), 0.0) + jnp.minimum(jnp.maximum(a, b), 0.0)


def vspec():
    return pl.BlockSpec(memory_space=VMEM)


def sspec():
    return pl.BlockSpec(memory_space=SMEM)


def edges_kernel(first_ref, last_ref, v_ref, up_ref, down_ref):
    for r in range(2):
        up_ref[r] = first_ref[:, r, :]
        down_ref[r] = last_ref[:, 6 + r, :]
    up_ref[2] = jnp.broadcast_to(v_ref[0:1, :], up_ref.shape[1:])


def forecast_kernel(
    slab_ref, cells_ref, weights_ref, h_ref, low_ref, high_ref, u_ref, v_ref, values_ref, noise_ref, cov_ref,
    f_ref, obs_ref, white_ref,
):
    members = noise_ref.shape[0]
    rows, cols = u_ref.shape
    per_row = cols // LANES
    lane = lax.broadcasted_iota(jnp.int32, (members, cols), 1)
    at_first = lane == 0
    at_last = lane == cols - 1

    blocks = {}

    def row(r):
        if r // 8 not in blocks:
            blocks[r // 8] = jnp.swapaxes(h_ref[:, r // 8 * 8 : r // 8 * 8 + 8, :], 0, 1)
        return blocks[r // 8][r % 8]

    def columns_term(h, u):
        prev = jnp.where(at_first, 0.0, pltpu.roll(h, 1, 1))
        d = h - prev
        d_next = jnp.where(at_last, -h, pltpu.roll(d, cols - 1, 1))
        half = 0.5 * minmod(d, d_next)
        left = jnp.where(at_first, 0.0, pltpu.roll(h + half, 1, 1))
        flux = jnp.maximum(u, 0.0) * left + jnp.minimum(u, 0.0) * (h - half)
        flux_next = jnp.where(at_last, 0.0, pltpu.roll(flux, cols - 1, 1))
        return flux_next - flux

    def row_flux(v, h_low, half_low, h_high, half_high):
        return jnp.maximum(v, 0.0) * (h_low + half_low) + jnp.minimum(v, 0.0) * (h_high - half_high)

    low2, low1 = low_ref[0], low_ref[1]
    h0, h1 = row(0), row(1)
    d0, d1 = h0 - low1, h1 - h0
    half_low = 0.5 * minmod(low1 - low2, d0)
    half0 = 0.5 * minmod(d0, d1)
    flux0 = row_flux(v_ref[0:1, :], low1, half_low, h0, half0)
    carry = (h0, h1, d1, half0, flux0)
    for r in range(rows):
        h, h_up, d_up, half, flux = carry
        if r + 2 < rows:
            h_up2 = row(r + 2)
        else:
            h_up2 = high_ref[r + 2 - rows]
        v = v_ref[r + 1 : r + 2, :] if r + 1 < rows else high_ref[2, 0:1, :]
        d_up2 = h_up2 - h_up
        half_up = 0.5 * minmod(d_up, d_up2)
        flux_up = row_flux(v, h, half, h_up, half_up)
        f = h - columns_term(h, u_ref[r : r + 1, :]) - (flux_up - flux)
        for t in range(per_row):
            f_ref[r * per_row + t] = f[:, t * LANES : (t + 1) * LANES]
        carry = (h_up, h_up2, d_up2, half_up, flux_up)

    base = slab_ref[0] * (rows * cols)
    count = cells_ref.shape[0]
    foot = cells_ref.shape[1]
    lane1 = lax.broadcasted_iota(jnp.int32, (members, LANES), 1)

    def observe(o, carry):
        total, norm = carry
        acc = jnp.zeros((members, LANES), jnp.float32)
        wsum = jnp.float32(0.0)
        for k in range(foot):
            c = cells_ref[o, k] - base
            w = weights_ref[o, k].astype(jnp.float32)
            tile = f_ref[c >> 7]
            acc = acc + jnp.where(lane1 == (c & (LANES - 1)), w * tile, 0.0)
            wsum = wsum + w
        here = lane1 == o
        total = jnp.where(here, jnp.sum(acc, axis=1, keepdims=True), total)
        norm = jnp.where(here, wsum, norm)
        return total, norm

    init = jnp.zeros((members, LANES), jnp.float32)
    total, norm = lax.fori_loop(0, count, observe, (init, init + 1.0), unroll=8)
    obs = total / norm
    obs_ref[...] = obs
    innovation = values_ref[...] + noise_ref[...] - obs
    white = jnp.dot(innovation, cov_ref[...], precision=HIGHEST, preferred_element_type=jnp.float32)
    for s in range(white_ref.shape[0]):
        white_ref[s] = white[:, s * LANES : (s + 1) * LANES]


def products_kernel(obs_ref, white_ref, out_ref):
    a = obs_ref[...]
    a = a - jnp.mean(a, axis=0, keepdims=True)
    w = white_ref[0]
    for s in range(1, white_ref.shape[0]):
        w = w + white_ref[s]
    out_ref[...] = lax.dot_general(
        w, a, (((1,), (1,)), ((), ())), precision=HIGHEST, preferred_element_type=jnp.float32
    )


def tapered_kernel(slab_ref, mask_ref, x_ref, out_ref):
    slabs = mask_ref.shape[0]
    members = out_ref.shape[0]
    e = jnp.zeros(out_ref.shape, jnp.float32)
    for b in range(slabs):
        e = e + mask_ref[slab_ref[0], b].astype(jnp.float32) * x_ref[b * members : (b + 1) * members, :]
    out_ref[...] = e


def mixing_kernel(x_ref, e_ref, out_ref):
    mems, tiles, members, width = x_ref.shape
    total = mems * members
    e = e_ref[...]
    depth = mems // PLANE
    for t in range(tiles):
        x = x_ref[:, t].reshape(total, width)
        x = x - jnp.mean(x, axis=0, keepdims=True)
        u = jnp.dot(e, x, precision=HIGHEST, preferred_element_type=jnp.float32) / (total - 1)
        for q in range(PLANE):
            for z in range(depth):
                at = (q * depth + z) * members
                out_ref[z * PLANE + q, t] = u[at : at + members]


def add_kernel(f_ref, y_ref, out_ref):
    rows, cols = out_ref.shape[1:]
    per_row = cols // LANES
    for r in range(0, rows, 8):
        for t in range(per_row):
            at = [(r + i) * per_row + t for i in range(8)]
            tile = jnp.stack([f_ref[i] + y_ref[i] for i in at], 0)
            out_ref[:, r : r + 8, t * LANES : (t + 1) * LANES] = jnp.swapaxes(tile, 0, 1)


def f32(*shape):
    return jax.ShapeDtypeStruct(shape, jnp.float32)


def gathered(x, axis, groups):
    return lax.all_gather(x, axis, axis=0, tiled=True, axis_index_groups=groups)


def local(
    thickness, face_u, face_v, obs_cells, obs_weights, obs_values, obs_noise, cov_inverse, taper_mask,
):
    members, rows, cols = thickness.shape
    mems = lax.axis_size("mem")
    slabs = lax.axis_size("slab")
    depth = mems // PLANE
    tiles = rows * cols // LANES
    slab = lax.axis_index("slab").astype(jnp.int32).reshape(1)
    planes = [[z * PLANE + q for q in range(PLANE)] for z in range(depth)]
    runs = [
        [(z0 + z) * PLANE + q for z in range(RUN)] for z0 in range(0, depth, RUN) for q in range(PLANE)
    ]
    strides = [
        [(z0 + z) * PLANE + q for z0 in range(0, depth, RUN)] for z in range(RUN) for q in range(PLANE)
    ]
    along_y = [[x * COLUMN + y for y in range(COLUMN)] for x in range(slabs // COLUMN)]
    along_x = [[x * COLUMN + y for x in range(slabs // COLUMN)] for y in range(COLUMN)]

    up, down = pl.pallas_call(
        edges_kernel,
        grid=(1,),
        in_specs=[
            pl.BlockSpec((members, 8, cols), lambda i: (0, 0, 0)),
            pl.BlockSpec((members, 8, cols), lambda i: (0, rows // 8 - 1, 0)),
            pl.BlockSpec((8, cols), lambda i: (0, 0)),
        ],
        out_specs=[
            pl.BlockSpec((3, members, cols), lambda i: (0, 0, 0)),
            pl.BlockSpec((2, members, cols), lambda i: (0, 0, 0)),
        ],
        out_shape=[f32(3, members, cols), f32(2, members, cols)],
        name="edges",
    )(thickness, thickness, face_v)
    low = lax.ppermute(down, "slab", [(i, i + 1) for i in range(slabs - 1)])
    high = lax.ppermute(up, "slab", [(i + 1, i) for i in range(slabs - 1)])

    forecast, obs_model, white_terms = pl.pallas_call(
        forecast_kernel,
        in_specs=[sspec(), sspec(), sspec()] + [vspec() for _ in range(8)],
        out_specs=[vspec() for _ in range(3)],
        out_shape=[f32(tiles, members, LANES), f32(members, LANES), f32(slabs, members, LANES)],
        name="forecast",
    )(
        slab, obs_cells, obs_weights, thickness, low, high, face_u, face_v,
        obs_values.reshape(1, -1), obs_noise, cov_inverse,
    )

    white_arrived = lax.all_to_all(white_terms, "slab", 0, 0, tiled=True)
    obs_all = gathered(gathered(gathered(obs_model, "mem", planes), "mem", runs), "mem", strides)
    cell_state = lax.all_to_all(
        forecast.reshape(mems, tiles // mems, members, LANES), "mem", 0, 0, tiled=True
    )
    product = pl.pallas_call(
        products_kernel,
        in_specs=[vspec(), vspec()],
        out_specs=vspec(),
        out_shape=f32(members, mems * members),
        name="products",
    )(obs_all, white_arrived)
    blocks = gathered(gathered(product, "slab", along_y), "slab", along_x)
    own_rows = pl.pallas_call(
        tapered_kernel,
        in_specs=[sspec(), sspec(), vspec()],
        out_specs=vspec(),
        out_shape=f32(members, mems * members),
        name="tapered",
    )(slab, taper_mask, blocks)
    ensemble = gathered(gathered(gathered(own_rows, "mem", runs), "mem", strides), "mem", planes)
    update = pl.pallas_call(
        mixing_kernel,
        in_specs=[vspec(), vspec()],
        out_specs=vspec(),
        out_shape=f32(mems, tiles // mems, members, LANES),
        name="mixing",
    )(cell_state, ensemble)
    returned = lax.all_to_all(update, "mem", 0, 0, tiled=True)
    analysis = pl.pallas_call(
        add_kernel,
        in_specs=[vspec(), vspec()],
        out_specs=vspec(),
        out_shape=f32(members, rows, cols),
        name="add",
    )(forecast, returned.reshape(tiles, members, LANES))
    return analysis


def solution(mesh):
    return jax.shard_map(
        local,
        mesh=mesh,
        in_specs=(
            P("mem", "slab", None),
            P("slab", None),
            P("slab", None),
            P("slab", None),
            P("slab", None),
            P("slab"),
            P("mem", "slab"),
            P("slab", None),
            P(),
        ),
        out_specs=P("mem", "slab", None),
        check_vma=False,
    )
```

time: 245 us -> 233 us (0.951)
  waiting for transfers between devices: 78.8 us -> 0.01 us
  blocking collectives: 99 us -> 175 us
  Pallas kernels: 0 us -> 27.2 us
  other arithmetic: 15.9 us -> 0 us
  local copies, waits for them, and re-layouts: 16.6 us -> 3.66 us
  starting transfers between devices: 30.5 us -> 27 us
  matrix products: 2.98 us -> 0 us
    all_to_all x4 -> x1, waiting for transfers between devices: 78.8 us -> 0.01 us  [local(): lax.all_to_all(forecast.reshape(mems, tiles // mems, members, LANES), 'me...]
    all_gather x1 -> x8, blocking collectives: 61.2 us -> 116 us  [gathered(): return lax.all_gather(x, axis, axis=0, tiled=True, axis_index_groups=groups)]
    pallas_call x0 -> x6, Pallas kernels: none -> 27.2 us  [the longest x1 15.4 us: local(): pl.pallas_call(forecast_kernel, in_specs=[sspec(), sspec(), sspec()] + [v...]
    all_to_all x1 -> x2, blocking collectives: 37.7 us -> 58.2 us  [the longest x1 38.9 us: local(): returned = lax.all_to_all(update, 'mem', 0, 0, tiled=True)]
    sub x1 -> x0, local copies, waits for them, and re-layouts: 6.65 us -> none  [local(): thickness - (column_fluxes[:, :, 1:] - column_fluxes[:, :, :-1])]
    add x2 -> x0, other arithmetic: 6.01 us -> none  [face_flux(): jnp.maximum(velocity, 0.0) * left_state]
    gather x1 -> x0, local copies, waits for them, and re-layouts: 5.6 us -> none  [local(): picked = state_vector[:, local_cells]]
    unnamed x10 -> x14, local copies, waits for them, and re-layouts: 0.04 us -> 3.66 us
  transfers between devices with their start and end apart: 6 -> 3, of which waited for: 4 -> 0; matrix products, arithmetic and copies ran while one was open for 4% -> 1% of each run, Pallas kernels for 0% -> 1%
where the time goes in v1:
time: 233 us
  blocking collectives  175 us (75%)
  Pallas kernels  27.2 us (12%)
  starting transfers between devices  27 us (12%)
  local copies, waits for them, and re-layouts  3.66 us (2%)
    all_gather x8, blocking collectives, gathered(): return lax.all_gather(x, axis, axis=0, tiled=True, axis_index_groups=groups)  116 us
    all_to_all x1, blocking collectives, local(): returned = lax.all_to_all(update, 'mem', 0, 0, tiled=True)  38.9 us
    all_to_all x1, starting transfers between devices, local(): lax.all_to_all(forecast.reshape(mems, tiles // mems, members, LANES), 'me...  20.1 us
    all_to_all x1, blocking collectives, local(): white_arrived = lax.all_to_all(white_terms, 'slab', 0, 0, tiled=True)  19.3 us
    pallas_call x1, Pallas kernels, local(): pl.pallas_call(forecast_kernel, in_specs=[sspec(), sspec(), sspec()] + [v...  15.4 us
    ppermute x1, starting transfers between devices, local(): low = lax.ppermute(down, 'slab', [(i, i + 1) for i in range(slabs - 1)])  5.66 us
  transfers between devices with their start and end apart: 3, of which 0 were waited for; matrix products, arithmetic and copies ran while one was open for 1% of the time, Pallas kernels for 1%

profile of v1, /device:TPU:1, one launch (start us, length us, event | category | flops | bytes accessed | tf_op | source)
XLA Modules:
  0.0 232.6 jit_solution(14775225741236695272)
XLA Ops:
  0.0 1.6 edges.1
  1.6 1.3 collective-permute-start.1
  2.9 5.7 %collective-permute-start = (f32[2,8,384]{2,1,0:T(8,128)}, f32[2,8,384]{2,1,0:T(8,128)S(1)}, u32[]{:S(2)}, u32[]{:S(2)}) collective-permute-start(f32[2,8,384]{2,1,0:T(8,128)} %get-tuple-element.10), channel_id=1, source_target_pairs={{0,1},{1,2},{2,3},{3,4},{4,5},{5,6},{6,7},{7,8},{8,9},{9,10},{10,1... | collective-permute-start | bytes 73736 | tf_op jit(solution)/shard_map/ppermute | solution.py:207
  8.6 0.7 copy-done.4
  9.2 0.7 copy.10.cells_ref
  10.0 0.7 copy.11.weights_ref
  10.7 0.6 copy-done.2
  11.4 15.4 %forecast.1 = (f32[192,8,128]{2,1,0:T(8,128)}, f32[8,128]{1,0:T(8,128)}, f32[16,8,128]{2,1,0:T(8,128)}) custom-call(s32[1]{0:T(128)} %bitcast.slab_ref, s32[128,4]{1,0:T(8,128)} %copy.10.cells_ref, s32[128,4]{1,0:T(8,128)} %copy.11.weights_ref, f32[8,64,384]{2,1,0:T(8,128)} %h_ref.1, f32[2,8,384]{2,1,0:T(8,128)} %copy-done.2, f32[3,8,384]{2,1,0:T(8,128)} %copy-done.1, ...), custom_call_target="tpu_custom_call" | custom-call | tf_op jit(solution)/shard_map/forecast/pallas_call | solution.py:210
  26.8 19.3 %all_to_all.15.white_ref = f32[16,8,128]{2,1,0:T(8,128)} all-to-all(f32[16,8,128]{2,1,0:T(8,128)} %get-tuple-element.14), channel_id=1, replica_groups=mesh['mem'=48,'slab'=16] {'slab'}, dimensions={0} | all-to-all | bytes 131072 | tf_op jit(solution)/shard_map/all_to_all | solution.py:221
  46.0 20.1 %all-to-all-start = ((f32[48,4,8,128]{3,2,1,0:T(8,128)}), f32[48,4,8,128]{3,2,1,0:T(8,128)S(1)}, u32[]{:S(2)}, u32[]{:S(2)}) async-start(f32[48,4,8,128]{3,2,1,0:T(8,128)} %bitcast.4), calls=%async_computation | async-start | bytes 1572864 | tf_op jit(solution)/shard_map/all_to_all | solution.py:223
  66.1 5.4 %all_gather.24 = f32[32,128]{1,0:T(8,128)S(1)} all-gather(f32[8,128]{1,0:T(8,128)S(1)} %copy-done.3), channel_id=1, replica_groups={{0,16,32,48},{64,80,96,112},{128,144,160,176},{192,208,224,240},{256,27..., dimensions={0}, use_global_device_ids=true | all-gather | bytes 20480 | tf_op jit(solution)/shard_map/all_gather | solution.py:170
  71.5 26.3 %all_gather.25 = f32[128,128]{1,0:T(8,128)S(1)} all-gather(f32[32,128]{1,0:T(8,128)S(1)} %all_gather.24), channel_id=1, replica_groups={{0,64,128,192},{16,80,144,208},{32,96,160,224},{48,112,176,240},{256,32..., dimensions={0}, use_global_device_ids=true | all-gather | bytes 81920 | tf_op jit(solution)/shard_map/all_gather | solution.py:170
  97.9 16.4 %all_gather.26.obs_ref = f32[384,128]{1,0:T(8,128)} all-gather(f32[128,128]{1,0:T(8,128)S(1)} %all_gather.25), channel_id=1, replica_groups={{0,256,512},{16,272,528},{32,288,544},{48,304,560},{64,320,576},{80,336..., dimensions={0}, use_global_device_ids=true | all-gather | bytes 262144 | tf_op jit(solution)/shard_map/all_gather | solution.py:170
  114.2 1.9 products.1
  116.2 11.0 %all_gather.27 = f32[32,384]{1,0:T(8,128)S(1)} all-gather(f32[8,384]{1,0:T(8,128)} %products.1), channel_id=1, replica_groups={{0,1,2,3},{4,5,6,7},{8,9,10,11},{12,13,14,15},{16,17,18,19},{20,21,22,2..., dimensions={0}, use_global_device_ids=true | all-gather | bytes 61440 | tf_op jit(solution)/shard_map/all_gather | solution.py:170
  127.2 10.2 %all_gather.28.x_ref = f32[128,384]{1,0:T(8,128)} all-gather(f32[32,384]{1,0:T(8,128)S(1)} %all_gather.27), channel_id=1, replica_groups={{0,4,8,12},{1,5,9,13},{2,6,10,14},{3,7,11,15},{16,20,24,28},{17,21,25,2..., dimensions={0}, use_global_device_ids=true | all-gather | bytes 245760 | tf_op jit(solution)/shard_map/all_gather | solution.py:170
  137.3 1.6 tapered.1
  138.9 10.5 %all_gather.29 = f32[32,384]{1,0:T(8,128)S(1)} all-gather(f32[8,384]{1,0:T(8,128)} %tapered.1), channel_id=1, replica_groups={{0,64,128,192},{16,80,144,208},{32,96,160,224},{48,112,176,240},{256,32..., dimensions={0}, use_global_device_ids=true | all-gather | bytes 61440 | tf_op jit(solution)/shard_map/all_gather | solution.py:170
  149.4 13.1 %all_gather.30 = f32[96,384]{1,0:T(8,128)S(1)} all-gather(f32[32,384]{1,0:T(8,128)S(1)} %all_gather.29), channel_id=1, replica_groups={{0,256,512},{16,272,528},{32,288,544},{48,304,560},{64,320,576},{80,336..., dimensions={0}, use_global_device_ids=true | all-gather | bytes 196608 | tf_op jit(solution)/shard_map/all_gather | solution.py:170
  162.5 23.5 %all_gather.31.e_ref = f32[384,384]{1,0:T(8,128)} all-gather(f32[96,384]{1,0:T(8,128)S(1)} %all_gather.30), channel_id=1, replica_groups={{0,16,32,48},{64,80,96,112},{128,144,160,176},{192,208,224,240},{256,27..., dimensions={0}, use_global_device_ids=true | all-gather | bytes 737280 | tf_op jit(solution)/shard_map/all_gather | solution.py:170
  186.1 0.9 copy-done
  187.0 4.3 %mixing.1 = f32[48,4,8,128]{3,2,1,0:T(8,128)} custom-call(f32[48,4,8,128]{3,2,1,0:T(8,128)} %copy-done, f32[384,384]{1,0:T(8,128)} %all_gather.31.e_ref), custom_call_target="tpu_custom_call" | custom-call | tf_op jit(solution)/shard_map/mixing/pallas_call | solution.py:242
  191.2 38.9 %all_to_all.16 = f32[48,4,8,128]{3,2,1,0:T(8,128)} all-to-all(f32[48,4,8,128]{3,2,1,0:T(8,128)} %mixing.1), channel_id=1, replica_groups=mesh['mem'=48,'slab'=16] {'mem'}, dimensions={0} | all-to-all | bytes 1572864 | tf_op jit(solution)/shard_map/all_to_all | solution.py:249
  230.2 2.4 %add.1 = f32[8,64,384]{2,1,0:T(8,128)} custom-call(f32[192,8,128]{2,1,0:T(8,128)} %get-tuple-element.12.f_ref, f32[192,8,128]{2,1,0:T(8,128)} %bitcast.5), custom_call_target="tpu_custom_call" | custom-call | tf_op jit(solution)/shard_map/add/pallas_call | solution.py:250
  (12 shorter events, 0.0 us)
Async XLA Ops:
  1.6 9.1 %collective-permute-start.1 = (f32[3,8,384]{2,1,0:T(8,128)}, f32[3,8,384]{2,1,0:T(8,128)S(1)}, u32[]{:S(2)}, u32[]{:S(2)}) collective-permute-start(f32[3,8,384]{2,1,0:T(8,128)} %get-tuple-element.11), channel_id=1, source_target_pairs={{1,0},{2,1},{3,2},{4,3},{5,4},{6,5},{7,6},{8,7},{9,8},{10,9},{11,1... | collective-permute-start | bytes 110600 | tf_op jit(solution)/shard_map/ppermute | solution.py:208
  2.9 7.8 %collective-permute-start = (f32[2,8,384]{2,1,0:T(8,128)}, f32[2,8,384]{2,1,0:T(8,128)S(1)}, u32[]{:S(2)}, u32[]{:S(2)}) collective-permute-start(f32[2,8,384]{2,1,0:T(8,128)} %get-tuple-element.10), channel_id=1, source_target_pairs={{0,1},{1,2},{2,3},{3,4},{4,5},{5,6},{6,7},{7,8},{8,9},{9,10},{10,1... | collective-permute-start | bytes 73736 | tf_op jit(solution)/shard_map/ppermute | solution.py:207
  8.5 0.7 copy-start.4
  9.2 0.7 copy-start.5
  10.7 0.6 copy-start.2
  10.7 0.6 copy-start.1
  46.0 20.1 %copy-start.3 = (f32[8,128]{1,0:T(8,128)S(1)}, f32[8,128]{1,0:T(8,128)}, u32[]{:S(2)}) copy-start(f32[8,128]{1,0:T(8,128)} %get-tuple-element.13) | copy-start | bytes 12292
  46.0 140.0 %all-to-all-start = ((f32[48,4,8,128]{3,2,1,0:T(8,128)}), f32[48,4,8,128]{3,2,1,0:T(8,128)S(1)}, u32[]{:S(2)}, u32[]{:S(2)}) async-start(f32[48,4,8,128]{3,2,1,0:T(8,128)} %bitcast.4), calls=%async_computation | async-start | bytes 1572864 | tf_op jit(solution)/shard_map/all_to_all | solution.py:223
  186.1 0.9 copy-start

commit v2 on v1

--- a/solution.py
+++ b/solution.py
@@ -9,7 +9,7 @@
 LANES = 128
 PLANE = 4
 RUN = 4
-COLUMN = 4
+SLAB_SWAPS = (1, 3, 4, 12)
 HIGHEST = lax.Precision.HIGHEST
 SMEM = pltpu.SMEM
 VMEM = pltpu.VMEM
@@ -17,6 +17,13 @@
 
 def minmod(a, b):
     return jnp.maximum(jnp.minimum(a, b), 0.0) + jnp.minimum(jnp.maximum(a, b), 0.0)
+
+
+def swap_order(swaps):
+    order = [0]
+    for k in swaps:
+        order = order + [v ^ k for v in order]
+    return order
 
 
 def vspec():
@@ -117,8 +124,22 @@
         white_ref[s] = white[:, s * LANES : (s + 1) * LANES]
 
 
-def products_kernel(obs_ref, white_ref, out_ref):
-    a = obs_ref[...]
+def source_z(z, t, k, depth):
+    runs = depth // RUN
+    run = z // RUN + (0, runs - 1, 1)[t]
+    run = jnp.where(run >= runs, run - runs, run)
+    return run * RUN + ((z & (RUN - 1)) ^ k)
+
+
+def products_kernel(z_ref, obs_ref, white_ref, out_ref, a_ref):
+    mems, members, width = a_ref.shape
+    depth = mems // PLANE
+    for q in range(PLANE):
+        for t in range(depth // RUN):
+            for k in range(RUN):
+                at = ((q * depth) + t * RUN + k) * members
+                a_ref[source_z(z_ref[0], t, k, depth) * PLANE + q] = obs_ref[at : at + members, :]
+    a = a_ref[...].reshape(mems * members, width)
     a = a - jnp.mean(a, axis=0, keepdims=True)
     w = white_ref[0]
     for s in range(1, white_ref.shape[0]):
@@ -128,16 +149,19 @@
     )
 
 
-def tapered_kernel(slab_ref, mask_ref, x_ref, out_ref):
-    slabs = mask_ref.shape[0]
+def tapered_kernel(slab_ref, mask_ref, own_ref, other_ref, out_ref):
     members = out_ref.shape[0]
+    slab = slab_ref[0]
+    order = swap_order(SLAB_SWAPS)
+    half = len(order) // 2
     e = jnp.zeros(out_ref.shape, jnp.float32)
-    for b in range(slabs):
-        e = e + mask_ref[slab_ref[0], b].astype(jnp.float32) * x_ref[b * members : (b + 1) * members, :]
+    for i, v in enumerate(order):
+        ref, at = (own_ref, i) if i < half else (other_ref, i - half)
+        e = e + mask_ref[slab, slab ^ v].astype(jnp.float32) * ref[at * members : (at + 1) * members, :]
     out_ref[...] = e
 
 
-def mixing_kernel(x_ref, e_ref, out_ref):
+def mixing_kernel(z_ref, x_ref, e_ref, out_ref):
     mems, tiles, members, width = x_ref.shape
     total = mems * members
     e = e_ref[...]
@@ -147,9 +171,10 @@
         x = x - jnp.mean(x, axis=0, keepdims=True)
         u = jnp.dot(e, x, precision=HIGHEST, preferred_element_type=jnp.float32) / (total - 1)
         for q in range(PLANE):
-            for z in range(depth):
-                at = (q * depth + z) * members
-                out_ref[z * PLANE + q, t] = u[at : at + members]
+            for r in range(depth // RUN):
+                for k in range(RUN):
+                    at = (q * depth + r * RUN + k) * members
+                    out_ref[source_z(z_ref[0], r, k, depth) * PLANE + q, t] = u[at : at + members]
 
 
 def add_kernel(f_ref, y_ref, out_ref):
@@ -166,8 +191,27 @@
     return jax.ShapeDtypeStruct(shape, jnp.float32)
 
 
-def gathered(x, axis, groups):
-    return lax.all_gather(x, axis, axis=0, tiled=True, axis_index_groups=groups)
+def v32(*shape):
+    return VMEM(shape, jnp.float32)
+
+
+def near(x):
+    return pltpu.with_memory_space_constraint(x, VMEM)
+
+
+def swapped(x, axis, k):
+    return lax.ppermute(x, axis, [(i, i ^ k) for i in range(lax.axis_size(axis))])
+
+
+def gathered_over_mem(x, planes):
+    mems = lax.axis_size("mem")
+    for k in (PLANE, 2 * PLANE):
+        x = jnp.concatenate([x, swapped(x, "mem", k)], 0)
+    step = RUN * PLANE
+    below = lax.ppermute(x, "mem", [(i, (i + step) % mems) for i in range(mems)])
+    above = lax.ppermute(x, "mem", [(i, (i - step) % mems) for i in range(mems)])
+    x = jnp.concatenate([x, below, above], 0)
+    return lax.all_gather(x, "mem", axis=0, tiled=True, axis_index_groups=planes)
 
 
 def local(
@@ -180,14 +224,7 @@
     tiles = rows * cols // LANES
     slab = lax.axis_index("slab").astype(jnp.int32).reshape(1)
     planes = [[z * PLANE + q for q in range(PLANE)] for z in range(depth)]
-    runs = [
-        [(z0 + z) * PLANE + q for z in range(RUN)] for z0 in range(0, depth, RUN) for q in range(PLANE)
-    ]
-    strides = [
-        [(z0 + z) * PLANE + q for z0 in range(0, depth, RUN)] for z in range(RUN) for q in range(PLANE)
-    ]
-    along_y = [[x * COLUMN + y for y in range(COLUMN)] for x in range(slabs // COLUMN)]
-    along_x = [[x * COLUMN + y for x in range(slabs // COLUMN)] for y in range(COLUMN)]
+    z = lax.shift_right_logical(lax.axis_index("mem").astype(jnp.int32), PLANE.bit_length() - 1).reshape(1)
 
     up, down = pl.pallas_call(
         edges_kernel,
@@ -201,7 +238,7 @@
             pl.BlockSpec((3, members, cols), lambda i: (0, 0, 0)),
             pl.BlockSpec((2, members, cols), lambda i: (0, 0, 0)),
         ],
-        out_shape=[f32(3, members, cols), f32(2, members, cols)],
+        out_shape=[v32(3, members, cols), v32(2, members, cols)],
         name="edges",
     )(thickness, thickness, face_v)
     low = lax.ppermute(down, "slab", [(i, i + 1) for i in range(slabs - 1)])
@@ -211,41 +248,45 @@
         forecast_kernel,
         in_specs=[sspec(), sspec(), sspec()] + [vspec() for _ in range(8)],
         out_specs=[vspec() for _ in range(3)],
-        out_shape=[f32(tiles, members, LANES), f32(members, LANES), f32(slabs, members, LANES)],
+        out_shape=[v32(tiles, members, LANES), v32(members, LANES), v32(slabs, members, LANES)],
         name="forecast",
     )(
-        slab, obs_cells, obs_weights, thickness, low, high, face_u, face_v,
+        slab, obs_cells, obs_weights, thickness, near(low), near(high), face_u, face_v,
         obs_values.reshape(1, -1), obs_noise, cov_inverse,
     )
 
     white_arrived = lax.all_to_all(white_terms, "slab", 0, 0, tiled=True)
-    obs_all = gathered(gathered(gathered(obs_model, "mem", planes), "mem", runs), "mem", strides)
+    obs_all = gathered_over_mem(obs_model, planes)
     cell_state = lax.all_to_all(
         forecast.reshape(mems, tiles // mems, members, LANES), "mem", 0, 0, tiled=True
     )
     product = pl.pallas_call(
         products_kernel,
-        in_specs=[vspec(), vspec()],
+        in_specs=[sspec(), vspec(), vspec()],
         out_specs=vspec(),
-        out_shape=f32(members, mems * members),
+        out_shape=v32(members, mems * members),
+        scratch_shapes=[VMEM((mems, members, LANES), jnp.float32)],
         name="products",
-    )(obs_all, white_arrived)
-    blocks = gathered(gathered(product, "slab", along_y), "slab", along_x)
+    )(z, near(obs_all), near(white_arrived))
+    blocks = product
+    for k in SLAB_SWAPS[:-1]:
+        blocks = jnp.concatenate([blocks, swapped(blocks, "slab", k)], 0)
+    other_blocks = swapped(blocks, "slab", SLAB_SWAPS[-1])
     own_rows = pl.pallas_call(
         tapered_kernel,
-        in_specs=[sspec(), sspec(), vspec()],
+        in_specs=[sspec(), sspec(), vspec(), vspec()],
         out_specs=vspec(),
-        out_shape=f32(members, mems * members),
+        out_shape=v32(members, mems * members),
         name="tapered",
-    )(slab, taper_mask, blocks)
-    ensemble = gathered(gathered(gathered(own_rows, "mem", runs), "mem", strides), "mem", planes)
+    )(slab, taper_mask, near(blocks), near(other_blocks))
+    ensemble = gathered_over_mem(own_rows, planes)
     update = pl.pallas_call(
         mixing_kernel,
-        in_specs=[vspec(), vspec()],
+        in_specs=[sspec(), vspec(), vspec()],
         out_specs=vspec(),
-        out_shape=f32(mems, tiles // mems, members, LANES),
+        out_shape=v32(mems, tiles // mems, members, LANES),
         name="mixing",
-    )(cell_state, ensemble)
+    )(z, near(cell_state), near(ensemble))
     returned = lax.all_to_all(update, "mem", 0, 0, tiled=True)
     analysis = pl.pallas_call(
         add_kernel,
@@ -253,7 +294,7 @@
         out_specs=vspec(),
         out_shape=f32(members, rows, cols),
         name="add",
-    )(forecast, returned.reshape(tiles, members, LANES))
+    )(near(forecast), near(returned.reshape(tiles, members, LANES)))
     return analysis
 
 

time: 233 us -> 231 us (level)
  blocking collectives: 175 us -> 88.3 us
  waiting for transfers between devices: 0.01 us -> 47 us
  starting transfers between devices: 27 us -> 71 us
  Pallas kernels: 27.2 us -> 21.5 us
    all_gather x8 -> x2, blocking collectives: 116 us -> 25.4 us  [gathered_over_mem(): lax.all_gather(x, 'mem', axis=0, tiled=True, axis_index_groups=planes)]
    ppermute x0 -> x12, waiting for transfers between devices: none -> 47 us  [the longest x8 39.1 us: swapped(): lax.ppermute(x, axis, [(i, i ^ k) for i in range(lax.axis_size(axis))])]
    ppermute x0 -> x12, starting transfers between devices: none -> 44.3 us  [the longest x8 24.8 us: swapped(): lax.ppermute(x, axis, [(i, i ^ k) for i in range(lax.axis_size(axis))])]
    all_to_all x1, blocking collectives: 38.9 us -> 43.9 us  [local(): returned = lax.all_to_all(update, 'mem', 0, 0, tiled=True)]
    pallas_call x3, Pallas kernels: 7.76 us -> 3.29 us  [the longest x1 2.06 us: local(): pl.pallas_call(mixing_kernel, in_specs=[sspec(), vspec(), vspec()], out_s...]
  transfers between devices with their start and end apart: 3 -> 15, of which waited for: 0 -> 10; matrix products, arithmetic and copies ran while one was open for 1% -> 1% of each run, Pallas kernels for 1% -> 1%
where the time goes in v2:
time: 231 us; the launch traced here: 230 us
  blocking collectives  88.3 us (38%)
  starting transfers between devices  71 us (31%)
  waiting for transfers between devices  47 us (20%)
  Pallas kernels  21.5 us (9%)
    all_to_all x1, blocking collectives, local(): returned = lax.all_to_all(update, 'mem', 0, 0, tiled=True)  43.9 us
    ppermute x8, waiting for transfers between devices, swapped(): lax.ppermute(x, axis, [(i, i ^ k) for i in range(lax.axis_size(axis))])  39.1 us
    all_gather x2, blocking collectives, gathered_over_mem(): lax.all_gather(x, 'mem', axis=0, tiled=True, axis_index_groups=planes)  25.4 us
    ppermute x8, starting transfers between devices, swapped(): lax.ppermute(x, axis, [(i, i ^ k) for i in range(lax.axis_size(axis))])  24.8 us
    all_to_all x1, starting transfers between devices, local(): lax.all_to_all(forecast.reshape(mems, tiles // mems, members, LANES), 'me...  19.8 us
    all_to_all x1, blocking collectives, local(): white_arrived = lax.all_to_all(white_terms, 'slab', 0, 0, tiled=True)  19 us
    ppermute x2, starting transfers between devices, gathered_over_mem(): lax.ppermute(x, 'mem', [(i, (i + step) % mems) for i in range(mems)])  15.5 us
    pallas_call x1, Pallas kernels, local(): pl.pallas_call(forecast_kernel, in_specs=[sspec(), sspec(), sspec()] + [v...  15.1 us
  transfers between devices with their start and end apart: 15, of which 10 were waited for; matrix products, arithmetic and copies ran while one was open for 1% of the time, Pallas kernels for 1%

profile of v2, /device:TPU:1, one launch (start us, length us, event | category | flops | bytes accessed | tf_op | source)
XLA Modules:
  0.0 230.3 jit_solution(15196550195573234794)
XLA Ops:
  2.3 5.7 %collective-permute-start = (f32[2,8,384]{2,1,0:T(8,128)S(1)}, f32[2,8,384]{2,1,0:T(8,128)S(1)}, u32[]{:S(2)}, u32[]{:S(2)}) collective-permute-start(f32[2,8,384]{2,1,0:T(8,128)S(1)} %get-tuple-element.10), channel_id=1, source_target_pairs={{0,1},{1,2},{2,3},{3,4},{4,5},{5,6},{6,7},{7,8},{8,9},{9,10},{10,1... | collective-permute-start | bytes 73736 | tf_op jit(solution)/shard_map/ppermute | solution.py:244
  10.1 15.1 %forecast.1 = (f32[192,8,128]{2,1,0:T(8,128)}, f32[8,128]{1,0:T(8,128)S(1)}, f32[16,8,128]{2,1,0:T(8,128)S(1)}) custom-call(s32[1]{0:T(128)} %bitcast.slab_ref, s32[128,4]{1,0:T(8,128)} %copy.10.cells_ref, s32[128,4]{1,0:T(8,128)} %copy.11.weights_ref, f32[8,64,384]{2,1,0:T(8,128)} %h_ref.1, f32[2,8,384]{2,1,0:T(8,128)S(1)} %collective-permute-done.low_ref, ...), custom_call_target="tpu_custom_call" | custom-call | tf_op jit(solution)/shard_map/forecast/pallas_call | solution.py:247
  25.2 19.0 %all_to_all.15.white_ref = f32[16,8,128]{2,1,0:T(8,128)S(1)} all-to-all(f32[16,8,128]{2,1,0:T(8,128)S(1)} %get-tuple-element.14), channel_id=1, replica_groups=mesh['mem'=48,'slab'=16] {'slab'}, dimensions={0} | all-to-all | bytes 131072 | tf_op jit(solution)/shard_map/all_to_all | solution.py:258
  44.1 19.8 %all-to-all-start = ((f32[48,4,8,128]{3,2,1,0:T(8,128)}), f32[48,4,8,128]{3,2,1,0:T(8,128)S(1)}, u32[]{:S(2)}, u32[]{:S(2)}) async-start(f32[48,4,8,128]{3,2,1,0:T(8,128)} %bitcast.3), calls=%async_computation | async-start | bytes 1572864 | tf_op jit(solution)/shard_map/all_to_all | solution.py:260
  63.9 3.3 %collective-permute-start.2 = (f32[8,128]{1,0:T(8,128)S(1)}, f32[8,128]{1,0:T(8,128)S(1)}, u32[]{:S(2)}, u32[]{:S(2)}) collective-permute-start(f32[8,128]{1,0:T(8,128)S(1)} %get-tuple-element.13), channel_id=1, source_target_pairs={{0,64},{16,80},{32,96},{48,112},{64,0},{80,16},{96,32},{112,48},{1... | collective-permute-start | bytes 12296 | tf_op jit(solution)/shard_map/ppermute | solution.py:203
  67.2 20.9 %collective-permute-done.2 = f32[8,128]{1,0:T(8,128)S(1)} collective-permute-done((f32[8,128]{1,0:T(8,128)S(1)}, f32[8,128]{1,0:T(8,128)S(1)}, u32[]{:S(2)}, u32[]{:S(2)}) %collective-permute-start.2) | collective-permute-done | bytes 4128 | tf_op jit(solution)/shard_map/ppermute | solution.py:203
  88.1 4.7 %collective-permute-start.3 = (f32[16,128]{1,0:T(8,128)S(1)}, f32[16,128]{1,0:T(8,128)S(1)}, u32[]{:S(2)}, u32[]{:S(2)}) collective-permute-start(f32[16,128]{1,0:T(8,128)S(1)} %pad_maximum_fusion.5), channel_id=1, source_target_pairs={{0,128},{16,144},{32,160},{48,176},{64,192},{80,208},{96,224},{112... | collective-permute-start | bytes 24584 | tf_op jit(solution)/shard_map/ppermute | solution.py:203
  94.3 8.3 %collective-permute-start.4 = (f32[32,128]{1,0:T(8,128)S(1)}, f32[32,128]{1,0:T(8,128)S(1)}, u32[]{:S(2)}, u32[]{:S(2)}) collective-permute-start(f32[32,128]{1,0:T(8,128)S(1)} %get-tuple-element.15), channel_id=1, source_target_pairs={{0,256},{16,272},{32,288},{48,304},{64,320},{80,336},{96,352},{112... | collective-permute-start | bytes 49160 | tf_op jit(solution)/shard_map/ppermute | solution.py:211
  102.6 2.1 collective-permute-start.5
  104.7 6.2 %collective-permute-done.5 = f32[32,128]{1,0:T(8,128)S(1)} collective-permute-done((f32[32,128]{1,0:T(8,128)S(1)}, f32[32,128]{1,0:T(8,128)S(1)}, u32[]{:S(2)}, u32[]{:S(2)}) %collective-permute-start.5) | collective-permute-done | bytes 16416 | tf_op jit(solution)/shard_map/ppermute | solution.py:212
  111.0 9.2 %all_gather.6.obs_ref = f32[384,128]{1,0:T(8,128)S(1)} all-gather(f32[96,128]{1,0:T(8,128)S(1)} %constant_dynamic-update-slice_fusion.3), channel_id=1, replica_groups={{0,16,32,48},{64,80,96,112},{128,144,160,176},{192,208,224,240},{256,27..., dimensions={0}, use_global_device_ids=true | all-gather | bytes 245760 | tf_op jit(solution)/shard_map/all_gather | solution.py:214
  120.6 2.3 %collective-permute-start.6 = (f32[8,384]{1,0:T(8,128)S(1)}, f32[8,384]{1,0:T(8,128)S(1)}, u32[]{:S(2)}, u32[]{:S(2)}) collective-permute-start(f32[8,384]{1,0:T(8,128)S(1)} %products.1), channel_id=1, source_target_pairs={{0,1},{1,0},{2,3},{3,2},{4,5},{5,4},{6,7},{7,6},{8,9},{9,8},{10,11... | collective-permute-start | bytes 36872 | tf_op jit(solution)/shard_map/ppermute | solution.py:203
  122.9 3.0 %collective-permute-done.6 = f32[8,384]{1,0:T(8,128)S(1)} collective-permute-done((f32[8,384]{1,0:T(8,128)S(1)}, f32[8,384]{1,0:T(8,128)S(1)}, u32[]{:S(2)}, u32[]{:S(2)}) %collective-permute-start.6) | collective-permute-done | bytes 12320 | tf_op jit(solution)/shard_map/ppermute | solution.py:203
  125.9 2.5 %collective-permute-start.7 = (f32[16,384]{1,0:T(8,128)S(1)}, f32[16,384]{1,0:T(8,128)S(1)}, u32[]{:S(2)}, u32[]{:S(2)}) collective-permute-start(f32[16,384]{1,0:T(8,128)S(1)} %pad_maximum_fusion.3), channel_id=1, source_target_pairs={{0,3},{1,2},{2,1},{3,0},{4,7},{5,6},{6,5},{7,4},{8,11},{9,10},{10,... | collective-permute-start | bytes 73736 | tf_op jit(solution)/shard_map/ppermute | solution.py:203
  128.4 4.3 %collective-permute-done.7 = f32[16,384]{1,0:T(8,128)S(1)} collective-permute-done((f32[16,384]{1,0:T(8,128)S(1)}, f32[16,384]{1,0:T(8,128)S(1)}, u32[]{:S(2)}, u32[]{:S(2)}) %collective-permute-start.7) | collective-permute-done | bytes 24608 | tf_op jit(solution)/shard_map/ppermute | solution.py:203
  134.8 2.8 %collective-permute-done.8 = f32[32,384]{1,0:T(8,128)S(1)} collective-permute-done((f32[32,384]{1,0:T(8,128)S(1)}, f32[32,384]{1,0:T(8,128)S(1)}, u32[]{:S(2)}, u32[]{:S(2)}) %collective-permute-start.8) | collective-permute-done | bytes 49184 | tf_op jit(solution)/shard_map/ppermute | solution.py:203
  137.6 2.6 %collective-permute-start.9 = (f32[64,384]{1,0:T(8,128)S(1)}, f32[64,384]{1,0:T(8,128)S(1)}, u32[]{:S(2)}, u32[]{:S(2)}) collective-permute-start(f32[64,384]{1,0:T(8,128)S(1)} %pad_maximum_fusion.own_ref), channel_id=1, source_target_pairs={{0,12},{1,13},{2,14},{3,15},{4,8},{5,9},{6,10},{7,11},{8,4},{9,5},... | collective-permute-start | bytes 294920 | tf_op jit(solution)/shard_map/ppermute | solution.py:203
  140.2 3.9 %collective-permute-done.9.other_ref = f32[64,384]{1,0:T(8,128)S(1)} collective-permute-done((f32[64,384]{1,0:T(8,128)S(1)}, f32[64,384]{1,0:T(8,128)S(1)}, u32[]{:S(2)}, u32[]{:S(2)}) %collective-permute-start.9) | collective-permute-done | bytes 98336 | tf_op jit(solution)/shard_map/ppermute | solution.py:203
  145.0 2.8 %collective-permute-start.10 = (f32[8,384]{1,0:T(8,128)S(1)}, f32[8,384]{1,0:T(8,128)S(1)}, u32[]{:S(2)}, u32[]{:S(2)}) collective-permute-start(f32[8,384]{1,0:T(8,128)S(1)} %tapered.1), channel_id=1, source_target_pairs={{0,64},{16,80},{32,96},{48,112},{64,0},{80,16},{96,32},{112,48},{1... | collective-permute-start | bytes 36872 | tf_op jit(solution)/shard_map/ppermute | solution.py:203
  149.4 4.5 %collective-permute-start.11 = (f32[16,384]{1,0:T(8,128)S(1)}, f32[16,384]{1,0:T(8,128)S(1)}, u32[]{:S(2)}, u32[]{:S(2)}) collective-permute-start(f32[16,384]{1,0:T(8,128)S(1)} %pad_maximum_fusion.4), channel_id=1, source_target_pairs={{0,128},{16,144},{32,160},{48,176},{64,192},{80,208},{96,224},{112... | collective-permute-start | bytes 73736 | tf_op jit(solution)/shard_map/ppermute | solution.py:203
  157.0 7.3 %collective-permute-start.12 = (f32[32,384]{1,0:T(8,128)S(1)}, f32[32,384]{1,0:T(8,128)S(1)}, u32[]{:S(2)}, u32[]{:S(2)}) collective-permute-start(f32[32,384]{1,0:T(8,128)S(1)} %pad_maximum_fusion.2), channel_id=1, source_target_pairs={{0,256},{16,272},{32,288},{48,304},{64,320},{80,336},{96,352},{112... | collective-permute-start | bytes 147464 | tf_op jit(solution)/shard_map/ppermute | solution.py:211
  166.0 16.2 %all_gather.7.e_ref = f32[384,384]{1,0:T(8,128)S(1)} all-gather(f32[96,384]{1,0:T(8,128)S(1)} %constant_dynamic-update-slice_fusion.8), channel_id=1, replica_groups={{0,16,32,48},{64,80,96,112},{128,144,160,176},{192,208,224,240},{256,27..., dimensions={0}, use_global_device_ids=true | all-gather | bytes 737280 | tf_op jit(solution)/shard_map/all_gather | solution.py:214
  184.2 43.9 %all_to_all.16 = f32[48,4,8,128]{3,2,1,0:T(8,128)S(1)} all-to-all(f32[48,4,8,128]{3,2,1,0:T(8,128)S(1)} %mixing.1), channel_id=1, replica_groups=mesh['mem'=48,'slab'=16] {'mem'}, dimensions={0} | all-to-all | bytes 1572864 | tf_op jit(solution)/shard_map/all_to_all | solution.py:290
  228.2 2.2 add.1
  (38 shorter events, 17.6 us)
Async XLA Ops:
  1.0 9.1 %collective-permute-start.1 = (f32[3,8,384]{2,1,0:T(8,128)S(1)}, f32[3,8,384]{2,1,0:T(8,128)S(1)}, u32[]{:S(2)}, u32[]{:S(2)}) collective-permute-start(f32[3,8,384]{2,1,0:T(8,128)S(1)} %get-tuple-element.11), channel_id=1, source_target_pairs={{1,0},{2,1},{3,2},{4,3},{5,4},{6,5},{7,6},{8,7},{9,8},{10,9},{11,1... | collective-permute-start | bytes 110600 | tf_op jit(solution)/shard_map/ppermute | solution.py:245
  2.3 7.8 %collective-permute-start = (f32[2,8,384]{2,1,0:T(8,128)S(1)}, f32[2,8,384]{2,1,0:T(8,128)S(1)}, u32[]{:S(2)}, u32[]{:S(2)}) collective-permute-start(f32[2,8,384]{2,1,0:T(8,128)S(1)} %get-tuple-element.10), channel_id=1, source_target_pairs={{0,1},{1,2},{2,3},{3,4},{4,5},{5,6},{6,7},{7,8},{8,9},{9,10},{10,1... | collective-permute-start | bytes 73736 | tf_op jit(solution)/shard_map/ppermute | solution.py:244
  7.9 0.7 copy-start
  8.6 0.7 copy-start.1
  44.1 138.0 %all-to-all-start = ((f32[48,4,8,128]{3,2,1,0:T(8,128)}), f32[48,4,8,128]{3,2,1,0:T(8,128)S(1)}, u32[]{:S(2)}, u32[]{:S(2)}) async-start(f32[48,4,8,128]{3,2,1,0:T(8,128)} %bitcast.3), calls=%async_computation | async-start | bytes 1572864 | tf_op jit(solution)/shard_map/all_to_all | solution.py:260
  63.9 24.2 %collective-permute-start.2 = (f32[8,128]{1,0:T(8,128)S(1)}, f32[8,128]{1,0:T(8,128)S(1)}, u32[]{:S(2)}, u32[]{:S(2)}) collective-permute-start(f32[8,128]{1,0:T(8,128)S(1)} %get-tuple-element.13), channel_id=1, source_target_pairs={{0,64},{16,80},{32,96},{48,112},{64,0},{80,16},{96,32},{112,48},{1... | collective-permute-start | bytes 12296 | tf_op jit(solution)/shard_map/ppermute | solution.py:203
  88.1 6.2 %collective-permute-start.3 = (f32[16,128]{1,0:T(8,128)S(1)}, f32[16,128]{1,0:T(8,128)S(1)}, u32[]{:S(2)}, u32[]{:S(2)}) collective-permute-start(f32[16,128]{1,0:T(8,128)S(1)} %pad_maximum_fusion.5), channel_id=1, source_target_pairs={{0,128},{16,144},{32,160},{48,176},{64,192},{80,208},{96,224},{112... | collective-permute-start | bytes 24584 | tf_op jit(solution)/shard_map/ppermute | solution.py:203
  94.3 10.4 %collective-permute-start.4 = (f32[32,128]{1,0:T(8,128)S(1)}, f32[32,128]{1,0:T(8,128)S(1)}, u32[]{:S(2)}, u32[]{:S(2)}) collective-permute-start(f32[32,128]{1,0:T(8,128)S(1)} %get-tuple-element.15), channel_id=1, source_target_pairs={{0,256},{16,272},{32,288},{48,304},{64,320},{80,336},{96,352},{112... | collective-permute-start | bytes 49160 | tf_op jit(solution)/shard_map/ppermute | solution.py:211
  102.6 8.4 %collective-permute-start.5 = (f32[32,128]{1,0:T(8,128)S(1)}, f32[32,128]{1,0:T(8,128)S(1)}, u32[]{:S(2)}, u32[]{:S(2)}) collective-permute-start(f32[32,128]{1,0:T(8,128)S(1)} %get-tuple-element.15), channel_id=1, source_target_pairs={{0,512},{16,528},{32,544},{48,560},{64,576},{80,592},{96,608},{112... | collective-permute-start | bytes 49160 | tf_op jit(solution)/shard_map/ppermute | solution.py:212
  120.6 5.3 %collective-permute-start.6 = (f32[8,384]{1,0:T(8,128)S(1)}, f32[8,384]{1,0:T(8,128)S(1)}, u32[]{:S(2)}, u32[]{:S(2)}) collective-permute-start(f32[8,384]{1,0:T(8,128)S(1)} %products.1), channel_id=1, source_target_pairs={{0,1},{1,0},{2,3},{3,2},{4,5},{5,4},{6,7},{7,6},{8,9},{9,8},{10,11... | collective-permute-start | bytes 36872 | tf_op jit(solution)/shard_map/ppermute | solution.py:203
  125.9 6.8 %collective-permute-start.7 = (f32[16,384]{1,0:T(8,128)S(1)}, f32[16,384]{1,0:T(8,128)S(1)}, u32[]{:S(2)}, u32[]{:S(2)}) collective-permute-start(f32[16,384]{1,0:T(8,128)S(1)} %pad_maximum_fusion.3), channel_id=1, source_target_pairs={{0,3},{1,2},{2,1},{3,0},{4,7},{5,6},{6,5},{7,4},{8,11},{9,10},{10,... | collective-permute-start | bytes 73736 | tf_op jit(solution)/shard_map/ppermute | solution.py:203
  132.7 4.8 %collective-permute-start.8 = (f32[32,384]{1,0:T(8,128)S(1)}, f32[32,384]{1,0:T(8,128)S(1)}, u32[]{:S(2)}, u32[]{:S(2)}) collective-permute-start(f32[32,384]{1,0:T(8,128)S(1)} %pad_maximum_fusion.1), channel_id=1, source_target_pairs={{0,4},{1,5},{2,6},{3,7},{4,0},{5,1},{6,2},{7,3},{8,12},{9,13},{10,... | collective-permute-start | bytes 147464 | tf_op jit(solution)/shard_map/ppermute | solution.py:203
  137.6 6.6 %collective-permute-start.9 = (f32[64,384]{1,0:T(8,128)S(1)}, f32[64,384]{1,0:T(8,128)S(1)}, u32[]{:S(2)}, u32[]{:S(2)}) collective-permute-start(f32[64,384]{1,0:T(8,128)S(1)} %pad_maximum_fusion.own_ref), channel_id=1, source_target_pairs={{0,12},{1,13},{2,14},{3,15},{4,8},{5,9},{6,10},{7,11},{8,4},{9,5},... | collective-permute-start | bytes 294920 | tf_op jit(solution)/shard_map/ppermute | solution.py:203
  145.0 4.4 %collective-permute-start.10 = (f32[8,384]{1,0:T(8,128)S(1)}, f32[8,384]{1,0:T(8,128)S(1)}, u32[]{:S(2)}, u32[]{:S(2)}) collective-permute-start(f32[8,384]{1,0:T(8,128)S(1)} %tapered.1), channel_id=1, source_target_pairs={{0,64},{16,80},{32,96},{48,112},{64,0},{80,16},{96,32},{112,48},{1... | collective-permute-start | bytes 36872 | tf_op jit(solution)/shard_map/ppermute | solution.py:203
  149.4 5.7 %collective-permute-start.11 = (f32[16,384]{1,0:T(8,128)S(1)}, f32[16,384]{1,0:T(8,128)S(1)}, u32[]{:S(2)}, u32[]{:S(2)}) collective-permute-start(f32[16,384]{1,0:T(8,128)S(1)} %pad_maximum_fusion.4), channel_id=1, source_target_pairs={{0,128},{16,144},{32,160},{48,176},{64,192},{80,208},{96,224},{112... | collective-permute-start | bytes 73736 | tf_op jit(solution)/shard_map/ppermute | solution.py:203
  155.1 10.9 %collective-permute-start.13 = (f32[32,384]{1,0:T(8,128)S(1)}, f32[32,384]{1,0:T(8,128)S(1)}, u32[]{:S(2)}, u32[]{:S(2)}) collective-permute-start(f32[32,384]{1,0:T(8,128)S(1)} %pad_maximum_fusion.2), channel_id=1, source_target_pairs={{0,512},{16,528},{32,544},{48,560},{64,576},{80,592},{96,608},{112... | collective-permute-start | bytes 147464 | tf_op jit(solution)/shard_map/ppermute | solution.py:212
  157.0 8.9 %collective-permute-start.12 = (f32[32,384]{1,0:T(8,128)S(1)}, f32[32,384]{1,0:T(8,128)S(1)}, u32[]{:S(2)}, u32[]{:S(2)}) collective-permute-start(f32[32,384]{1,0:T(8,128)S(1)} %pad_maximum_fusion.2), channel_id=1, source_target_pairs={{0,256},{16,272},{32,288},{48,304},{64,320},{80,336},{96,352},{112... | collective-permute-start | bytes 147464 | tf_op jit(solution)/shard_map/ppermute | solution.py:211

commit v3 on v1

v3 whole, which is shorter than its diff:
```python
import jax
import jax.numpy as jnp
from jax import lax
from jax.experimental import pallas as pl
from jax.experimental.pallas import tpu as pltpu
from jax.sharding import PartitionSpec as P


LANES = 128
PLANE = 4
SLAB_SWAPS = (1, 3, 4, 12)
HIGHEST = lax.Precision.HIGHEST
SMEM = pltpu.SMEM
VMEM = pltpu.VMEM


def minmod(a, b):
    return jnp.maximum(jnp.minimum(a, b), 0.0) + jnp.minimum(jnp.maximum(a, b), 0.0)


def swap_order(swaps):
    order = [0]
    for k in swaps:
        order = order + [v ^ k for v in order]
    return order


def vspec():
    return pl.BlockSpec(memory_space=VMEM)


def sspec():
    return pl.BlockSpec(memory_space=SMEM)


def edges_kernel(first_ref, last_ref, v_ref, up_ref, down_ref):
    for r in range(2):
        up_ref[r] = first_ref[:, r, :]
        down_ref[r] = last_ref[:, 6 + r, :]
    up_ref[2] = jnp.broadcast_to(v_ref[0:1, :], up_ref.shape[1:])


def forecast_kernel(
    slab_ref, tile_ref, shift_ref, h_ref, low_ref, high_ref, u_ref, v_ref, weights_ref, values_ref, noise_ref, cov_ref,
    f_ref, near_ref, far_ref, white_ref,
):
    members = noise_ref.shape[0]
    rows, cols = u_ref.shape
    per_row = cols // LANES
    mems = f_ref.shape[0]
    tiles = f_ref.shape[1] - 1
    lane = lax.broadcasted_iota(jnp.int32, (members, cols), 1)
    at_first = lane == 0
    at_last = lane == cols - 1

    blocks = {}

    def row(r):
        if r // 8 not in blocks:
            blocks[r // 8] = jnp.swapaxes(h_ref[:, r // 8 * 8 : r // 8 * 8 + 8, :], 0, 1)
        return blocks[r // 8][r % 8]

    def columns_term(h, u):
        prev = jnp.where(at_first, 0.0, pltpu.roll(h, 1, 1))
        d = h - prev
        d_next = jnp.where(at_last, -h, pltpu.roll(d, cols - 1, 1))
        half = 0.5 * minmod(d, d_next)
        left = jnp.where(at_first, 0.0, pltpu.roll(h + half, 1, 1))
        flux = jnp.maximum(u, 0.0) * left + jnp.minimum(u, 0.0) * (h - half)
        flux_next = jnp.where(at_last, 0.0, pltpu.roll(flux, cols - 1, 1))
        return flux_next - flux

    def row_flux(v, h_low, half_low, h_high, half_high):
        return jnp.maximum(v, 0.0) * (h_low + half_low) + jnp.minimum(v, 0.0) * (h_high - half_high)

    low2, low1 = low_ref[0], low_ref[1]
    h0, h1 = row(0), row(1)
    d0, d1 = h0 - low1, h1 - h0
    half_low = 0.5 * minmod(low1 - low2, d0)
    half0 = 0.5 * minmod(d0, d1)
    flux0 = row_flux(v_ref[0:1, :], low1, half_low, h0, half0)
    carry = (h0, h1, d1, half0, flux0)
    for r in range(rows):
        h, h_up, d_up, half, flux = carry
        if r + 2 < rows:
            h_up2 = row(r + 2)
        else:
            h_up2 = high_ref[r + 2 - rows]
        v = v_ref[r + 1 : r + 2, :] if r + 1 < rows else high_ref[2, 0:1, :]
        d_up2 = h_up2 - h_up
        half_up = 0.5 * minmod(d_up, d_up2)
        flux_up = row_flux(v, h, half, h_up, half_up)
        f = h - columns_term(h, u_ref[r : r + 1, :]) - (flux_up - flux)
        for t in range(per_row):
            at = r * per_row + t
            f_ref[at // tiles, at % tiles] = f[:, t * LANES : (t + 1) * LANES]
        carry = (h_up, h_up2, d_up2, half_up, flux_up)

    foot, count = tile_ref.shape
    lane1 = lax.broadcasted_iota(jnp.int32, (members, LANES), 1)

    def observe(o, picked):
        here = lane1 == o
        out = []
        for k in range(foot):
            at = tile_ref[k, o]
            tile = f_ref[at // tiles, at % tiles]
            out.append(jnp.where(here, pltpu.roll(tile, shift_ref[k, o], 1), picked[k]))
        return tuple(out)

    zero = jnp.zeros((members, LANES), jnp.float32)
    picked = lax.fori_loop(0, count, observe, (zero,) * foot, unroll=4)
    weights = weights_ref[...].astype(jnp.float32)
    obs = picked[0] * weights[0:1]
    for k in range(1, foot):
        obs = obs + picked[k] * weights[k : k + 1]
    obs = obs / jnp.sum(weights, axis=0, keepdims=True)
    for p in range(mems):
        f_ref[p, tiles] = obs
    innovation = values_ref[...] + noise_ref[...] - obs
    white = jnp.dot(innovation, cov_ref[...], precision=HIGHEST, preferred_element_type=jnp.float32)
    order = swap_order(SLAB_SWAPS)
    blocks = white_ref
    for s in range(len(order)):
        blocks[s] = white[:, s * LANES : (s + 1) * LANES]
    half = len(order) // 2
    for i, v in enumerate(order):
        ref, at = (near_ref, i) if i < half else (far_ref, i - half)
        ref[at] = blocks[slab_ref[0] ^ v]


def products_kernel(slab_ref, mask_ref, x_ref, white_ref, swap_ref, out_ref):
    mems, tiles, members, width = x_ref.shape
    a = x_ref[:, tiles - 1].reshape(mems * members, width)
    a = a - jnp.mean(a, axis=0, keepdims=True)
    w = white_ref[...] + swap_ref[...]
    p = lax.dot_general(w, a, (((1,), (1,)), ((), ())), precision=HIGHEST, preferred_element_type=jnp.float32)
    for s in range(out_ref.shape[0]):
        out_ref[s] = mask_ref[s, slab_ref[0]].astype(jnp.float32) * p


def summed_kernel(x_ref, out_ref):
    e = x_ref[0]
    for s in range(1, x_ref.shape[0]):
        e = e + x_ref[s]
    for z in range(out_ref.shape[0]):
        out_ref[z] = e


def mixing_kernel(x_ref, e_ref, out_ref):
    mems, tiles, members, width = out_ref.shape
    total = mems * members
    e = e_ref[...]
    depth = mems // PLANE
    for t in range(tiles):
        x = x_ref[:, t].reshape(total, width)
        x = x - jnp.mean(x, axis=0, keepdims=True)
        u = jnp.dot(e, x, precision=HIGHEST, preferred_element_type=jnp.float32) / (total - 1)
        for q in range(PLANE):
            for z in range(depth):
                at = (q * depth + z) * members
                out_ref[z * PLANE + q, t] = u[at : at + members]


def add_kernel(f_ref, y_ref, out_ref):
    rows, cols = out_ref.shape[1:]
    per_row = cols // LANES
    for r in range(0, rows, 8):
        for t in range(per_row):
            at = [(r + i) * per_row + t for i in range(8)]
            tile = jnp.stack([f_ref[i // y_ref.shape[1], i % y_ref.shape[1]] + y_ref[i // y_ref.shape[1], i % y_ref.shape[1]] for i in at], 0)
            out_ref[:, r : r + 8, t * LANES : (t + 1) * LANES] = jnp.swapaxes(tile, 0, 1)


def f32(*shape):
    return jax.ShapeDtypeStruct(shape, jnp.float32)


def v32(*shape):
    return VMEM(shape, jnp.float32)


def near(x):
    return pltpu.with_memory_space_constraint(x, VMEM)


def swapped(x, axis, k):
    return lax.ppermute(x, axis, [(i, i ^ k) for i in range(lax.axis_size(axis))])


def local(
    thickness, face_u, face_v, obs_cells, obs_weights, obs_values, obs_noise, cov_inverse, taper_mask,
):
    members, rows, cols = thickness.shape
    mems = lax.axis_size("mem")
    slabs = lax.axis_size("slab")
    depth = mems // PLANE
    tiles = rows * cols // LANES // mems
    slab = lax.axis_index("slab").astype(jnp.int32).reshape(1)
    planes = [[z * PLANE + q for q in range(PLANE)] for z in range(depth)]
    columns = [[z * PLANE + q for z in range(depth)] for q in range(PLANE)]
    cells = obs_cells.T - slab * (rows * cols)
    cell_tile = lax.shift_right_logical(cells, LANES.bit_length() - 1)
    cell_shift = (lax.broadcasted_iota(jnp.int32, cells.shape, 1) - cells) & (LANES - 1)

    up, down = pl.pallas_call(
        edges_kernel,
        grid=(1,),
        in_specs=[
            pl.BlockSpec((members, 8, cols), lambda i: (0, 0, 0)),
            pl.BlockSpec((members, 8, cols), lambda i: (0, rows // 8 - 1, 0)),
            pl.BlockSpec((8, cols), lambda i: (0, 0)),
        ],
        out_specs=[
            pl.BlockSpec((3, members, cols), lambda i: (0, 0, 0)),
            pl.BlockSpec((2, members, cols), lambda i: (0, 0, 0)),
        ],
        out_shape=[v32(3, members, cols), v32(2, members, cols)],
        name="edges",
    )(thickness, thickness, face_v)
    low = lax.ppermute(down, "slab", [(i, i + 1) for i in range(slabs - 1)])
    high = lax.ppermute(up, "slab", [(i + 1, i) for i in range(slabs - 1)])

    forecast, white, white_far = pl.pallas_call(
        forecast_kernel,
        in_specs=[sspec(), sspec(), sspec()] + [vspec() for _ in range(9)],
        out_specs=[vspec() for _ in range(3)],
        out_shape=[
            v32(mems, tiles + 1, members, LANES),
            v32(slabs // 2, members, LANES),
            v32(slabs // 2, members, LANES),
        ],
        scratch_shapes=[v32(slabs, members, LANES)],
        name="forecast",
    )(
        slab, cell_tile, cell_shift, thickness, near(low), near(high), face_u, face_v, obs_weights.T,
        obs_values.reshape(1, -1), obs_noise, cov_inverse,
    )

    cell_state = lax.all_to_all(forecast, "mem", 0, 0, tiled=True)
    arrived = swapped(white_far, "slab", SLAB_SWAPS[-1])
    for k in SLAB_SWAPS[-2::-1]:
        half = white.shape[0] // 2
        white, white_far = white[:half] + arrived[:half], white[half:] + arrived[half:]
        arrived = swapped(white_far, "slab", k)
    parts = pl.pallas_call(
        products_kernel,
        in_specs=[sspec(), sspec(), vspec(), vspec(), vspec()],
        out_specs=vspec(),
        out_shape=v32(slabs, members, mems * members),
        name="products",
    )(slab, taper_mask, near(cell_state), near(white[0]), near(arrived[0]))
    parts = lax.all_to_all(parts, "slab", 0, 0, tiled=True)
    copies = pl.pallas_call(
        summed_kernel,
        in_specs=[vspec()],
        out_specs=vspec(),
        out_shape=v32(depth, members, mems * members),
        name="summed",
    )(near(parts))
    over_z = lax.all_to_all(copies, "mem", 0, 0, tiled=True, axis_index_groups=columns)
    ensemble = lax.all_gather(
        over_z.reshape(depth * members, mems * members), "mem", axis=0, tiled=True, axis_index_groups=planes
    )
    update = pl.pallas_call(
        mixing_kernel,
        in_specs=[vspec(), vspec()],
        out_specs=vspec(),
        out_shape=v32(mems, tiles, members, LANES),
        name="mixing",
    )(near(cell_state), near(ensemble))
    returned = lax.all_to_all(update, "mem", 0, 0, tiled=True)
    return pl.pallas_call(
        add_kernel,
        in_specs=[vspec(), vspec()],
        out_specs=vspec(),
        out_shape=f32(members, rows, cols),
        name="add",
    )(near(forecast), near(returned))


def solution(mesh):
    return jax.shard_map(
        local,
        mesh=mesh,
        in_specs=(
            P("mem", "slab", None),
            P("slab", None),
            P("slab", None),
            P("slab", None),
            P("slab", None),
            P("slab"),
            P("mem", "slab"),
            P("slab", None),
            P(),
        ),
        out_specs=P("mem", "slab", None),
        check_vma=False,
    )
```

time: 233 us -> 174 us (0.75)
  blocking collectives: 175 us -> 80.6 us
  waiting for transfers between devices: 0.01 us -> 26.5 us
  starting transfers between devices: 27 us -> 41.1 us
  Pallas kernels: 27.2 us -> 23.4 us
  local copies, waits for them, and re-layouts: 3.66 us -> 0.68 us
    all_gather x8 -> x1, blocking collectives: 116 us -> 9.24 us  [local(): lax.all_gather(over_z.reshape(depth * members, mems * members), 'mem', ax...]
    ppermute x0 -> x4, starting transfers between devices: none -> 17.5 us  [swapped(): lax.ppermute(x, axis, [(i, i ^ k) for i in range(lax.axis_size(axis))])]
    all_to_all x1, waiting for transfers between devices: 0.01 us -> 14.7 us  [local(): cell_state = lax.all_to_all(forecast, 'mem', 0, 0, tiled=True)]
    all_to_all x1 -> x2, blocking collectives: 19.3 us -> 33.8 us  [the longest x1 19.5 us: local(): parts = lax.all_to_all(parts, 'slab', 0, 0, tiled=True)]
    ppermute x0 -> x4, waiting for transfers between devices: none -> 7.23 us  [swapped(): lax.ppermute(x, axis, [(i, i ^ k) for i in range(lax.axis_size(axis))])]
    ppermute x1, waiting for transfers between devices: 0.01 us -> 4.58 us  [local(): high = lax.ppermute(up, 'slab', [(i + 1, i) for i in range(slabs - 1)])]
    unnamed x14 -> x2, local copies, waits for them, and re-layouts: 3.66 us -> 0.68 us
    all_to_all x1, starting transfers between devices: 20.1 us -> 17.3 us  [local(): cell_state = lax.all_to_all(forecast, 'mem', 0, 0, tiled=True)]
  transfers between devices with their start and end apart: 3 -> 7, of which waited for: 0 -> 6; matrix products, arithmetic and copies ran while one was open for 1% -> 0% of each run, Pallas kernels for 1% -> 0%
where the time goes in v3:
time: 174 us; the launch traced here: 173 us
  blocking collectives  80.6 us (46%)
  starting transfers between devices  41.1 us (24%)
  waiting for transfers between devices  26.5 us (15%)
  Pallas kernels  23.4 us (13%)
    all_to_all x1, blocking collectives, local(): returned = lax.all_to_all(update, 'mem', 0, 0, tiled=True)  37.6 us
    all_to_all x1, blocking collectives, local(): parts = lax.all_to_all(parts, 'slab', 0, 0, tiled=True)  19.5 us
    ppermute x4, starting transfers between devices, swapped(): lax.ppermute(x, axis, [(i, i ^ k) for i in range(lax.axis_size(axis))])  17.5 us
    all_to_all x1, starting transfers between devices, local(): cell_state = lax.all_to_all(forecast, 'mem', 0, 0, tiled=True)  17.3 us
    pallas_call x1, Pallas kernels, local(): pl.pallas_call(forecast_kernel, in_specs=[sspec(), sspec(), sspec()] + [v...  16.9 us
    all_to_all x1, waiting for transfers between devices, local(): cell_state = lax.all_to_all(forecast, 'mem', 0, 0, tiled=True)  14.7 us
    all_to_all x1, blocking collectives, local(): lax.all_to_all(copies, 'mem', 0, 0, tiled=True, axis_index_groups=columns)  14.3 us
    all_gather x1, blocking collectives, local(): lax.all_gather(over_z.reshape(depth * members, mems * members), 'mem', ax...  9.24 us
  transfers between devices with their start and end apart: 7, of which 6 were waited for; matrix products, arithmetic and copies ran while one was open for 0% of the time, Pallas kernels for 0%

profile of v3, /device:TPU:1, one launch (start us, length us, event | category | flops | bytes accessed | tf_op | source)
XLA Modules:
  0.0 173.0 jit_solution(13874807754798763586)
XLA Ops:
  0.0 1.0 edges.1
  1.0 5.0 %collective-permute-start = (f32[2,8,384]{2,1,0:T(8,128)S(1)}, f32[2,8,384]{2,1,0:T(8,128)S(1)}, u32[]{:S(2)}, u32[]{:S(2)}) collective-permute-start(f32[2,8,384]{2,1,0:T(8,128)S(1)} %get-tuple-element.10), channel_id=1, source_target_pairs={{0,1},{1,2},{2,3},{3,4},{4,5},{5,6},{6,7},{7,8},{8,9},{9,10},{10,1... | collective-permute-start | bytes 73736 | tf_op jit(solution)/shard_map/ppermute | solution.py:221
  6.0 1.3 collective-permute-start.1
  7.3 0.7 copy-done
  8.0 0.6 fusion.1
  8.6 4.6 %collective-permute-done.1.high_ref = f32[3,8,384]{2,1,0:T(8,128)S(1)} collective-permute-done((f32[3,8,384]{2,1,0:T(8,128)S(1)}, f32[3,8,384]{2,1,0:T(8,128)S(1)}, u32[]{:S(2)}, u32[]{:S(2)}) %collective-permute-start.1) | collective-permute-done | bytes 36896 | tf_op jit(solution)/shard_map/ppermute | solution.py:222
  13.2 16.9 %forecast.1 = (f32[48,5,8,128]{3,2,1,0:T(8,128)}, f32[8,8,128]{2,1,0:T(8,128)S(1)}, f32[8,8,128]{2,1,0:T(8,128)S(1)}) custom-call(s32[1]{0:T(128)} %bitcast.slab_ref, s32[4,128]{1,0:T(4,128)} %get-tuple-element.22.tile_ref, s32[4,128]{1,0:T(4,128)} %get-tuple-element.21.shift_ref, f32[8,64,384]{2,1,0:T(8,128)} %h_ref.1, ...), custom_call_target="tpu_custom_call" | custom-call | tf_op jit(solution)/shard_map/forecast/pallas_call | solution.py:224
  30.1 17.3 %all-to-all-start = ((f32[48,5,8,128]{3,2,1,0:T(8,128)}), f32[48,5,8,128]{3,2,1,0:T(8,128)S(1)}, u32[]{:S(2)}, u32[]{:S(2)}) async-start(f32[48,5,8,128]{3,2,1,0:T(8,128)} %get-tuple-element.12.f_ref), calls=%async_computation | async-start | bytes 1966080 | tf_op jit(solution)/shard_map/all_to_all | solution.py:240
  47.4 4.4 %collective-permute-start.2 = (f32[8,8,128]{2,1,0:T(8,128)S(1)}, f32[8,8,128]{2,1,0:T(8,128)S(1)}, u32[]{:S(2)}, u32[]{:S(2)}) collective-permute-start(f32[8,8,128]{2,1,0:T(8,128)S(1)} %get-tuple-element.14), channel_id=1, source_target_pairs={{0,12},{1,13},{2,14},{3,15},{4,8},{5,9},{6,10},{7,11},{8,4},{9,5},... | collective-permute-start | bytes 98312 | tf_op jit(solution)/shard_map/ppermute | solution.py:188
  51.8 1.8 %collective-permute-done.2 = f32[8,8,128]{2,1,0:T(8,128)S(1)} collective-permute-done((f32[8,8,128]{2,1,0:T(8,128)S(1)}, f32[8,8,128]{2,1,0:T(8,128)S(1)}, u32[]{:S(2)}, u32[]{:S(2)}) %collective-permute-start.2) | collective-permute-done | bytes 32800 | tf_op jit(solution)/shard_map/ppermute | solution.py:188
  53.6 1.9 %collective-permute-start.3 = (f32[4,8,128]{2,1,0:T(8,128)S(1)}, f32[4,8,128]{2,1,0:T(8,128)S(1)}, u32[]{:S(2)}, u32[]{:S(2)}) collective-permute-start(f32[4,8,128]{2,1,0:T(8,128)S(1)} %get-tuple-element.16), channel_id=1, source_target_pairs={{0,4},{1,5},{2,6},{3,7},{4,0},{5,1},{6,2},{7,3},{8,12},{9,13},{10,... | collective-permute-start | bytes 49160 | tf_op jit(solution)/shard_map/ppermute | solution.py:188
  55.5 2.8 %collective-permute-done.3 = f32[4,8,128]{2,1,0:T(8,128)S(1)} collective-permute-done((f32[4,8,128]{2,1,0:T(8,128)S(1)}, f32[4,8,128]{2,1,0:T(8,128)S(1)}, u32[]{:S(2)}, u32[]{:S(2)}) %collective-permute-start.3) | collective-permute-done | bytes 16416 | tf_op jit(solution)/shard_map/ppermute | solution.py:188
  58.3 6.1 %collective-permute-start.4 = (f32[2,8,128]{2,1,0:T(8,128)S(1)}, f32[2,8,128]{2,1,0:T(8,128)S(1)}, u32[]{:S(2)}, u32[]{:S(2)}) collective-permute-start(f32[2,8,128]{2,1,0:T(8,128)S(1)} %get-tuple-element.18), channel_id=1, source_target_pairs={{0,3},{1,2},{2,1},{3,0},{4,7},{5,6},{6,5},{7,4},{8,11},{9,10},{10,... | collective-permute-start | bytes 24584 | tf_op jit(solution)/shard_map/ppermute | solution.py:188
  64.5 1.3 collective-permute-done.4
  65.8 5.1 %collective-permute-start.5 = (f32[1,8,128]{2,1,0:T(8,128)S(1)}, f32[1,8,128]{2,1,0:T(8,128)S(1)}, u32[]{:S(2)}, u32[]{:S(2)}) collective-permute-start(f32[1,8,128]{2,1,0:T(8,128)S(1)} %get-tuple-element.19), channel_id=1, source_target_pairs={{0,1},{1,0},{2,3},{3,2},{4,5},{5,4},{6,7},{7,6},{8,9},{9,8},{10,11... | collective-permute-start | bytes 12296 | tf_op jit(solution)/shard_map/ppermute | solution.py:188
  70.9 1.3 collective-permute-done.5
  72.2 14.7 %all-to-all-done.x_ref = f32[48,5,8,128]{3,2,1,0:T(8,128)S(1)} async-done(((f32[48,5,8,128]{3,2,1,0:T(8,128)}), f32[48,5,8,128]{3,2,1,0:T(8,128)S(1)}, u32[]{:S(2)}, u32[]{:S(2)}) %all-to-all-start) | async-done | bytes 983072 | tf_op jit(solution)/shard_map/all_to_all | solution.py:240
  86.9 1.2 products.1
  88.1 19.5 %all_to_all.20.x_ref = f32[16,8,384]{2,1,0:T(8,128)S(1)} all-to-all(f32[16,8,384]{2,1,0:T(8,128)S(1)} %products.1), channel_id=1, replica_groups=mesh['mem'=48,'slab'=16] {'slab'}, dimensions={0} | all-to-all | bytes 393216 | tf_op jit(solution)/shard_map/all_to_all | solution.py:253
  107.6 14.3 %all_to_all.21 = f32[12,8,384]{2,1,0:T(8,128)S(1)} all-to-all(f32[12,8,384]{2,1,0:T(8,128)S(1)} %summed.1), channel_id=1, replica_groups={{0,64,128,192,256,320,384,448,512,576,640,704},{16,80,144,208,272,336,4..., dimensions={0} | all-to-all | bytes 294912 | tf_op jit(solution)/shard_map/all_to_all | solution.py:261
  121.9 9.2 %all_gather.3.e_ref = f32[384,384]{1,0:T(8,128)S(1)} all-gather(f32[96,384]{1,0:T(8,128)S(1)} %bitcast.14), channel_id=1, replica_groups={{0,16,32,48},{64,80,96,112},{128,144,160,176},{192,208,224,240},{256,27..., dimensions={0}, use_global_device_ids=true | all-gather | bytes 737280 | tf_op jit(solution)/shard_map/all_gather | solution.py:262
  131.1 2.1 %mixing.1 = f32[48,4,8,128]{3,2,1,0:T(8,128)S(1)} custom-call(f32[48,5,8,128]{3,2,1,0:T(8,128)S(1)} %all-to-all-done.x_ref, f32[384,384]{1,0:T(8,128)S(1)} %all_gather.3.e_ref), custom_call_target="tpu_custom_call" | custom-call | tf_op jit(solution)/shard_map/mixing/pallas_call | solution.py:265
  133.2 37.6 %all_to_all.22.y_ref = f32[48,4,8,128]{3,2,1,0:T(8,128)S(1)} all-to-all(f32[48,4,8,128]{3,2,1,0:T(8,128)S(1)} %mixing.1), channel_id=1, replica_groups=mesh['mem'=48,'slab'=16] {'mem'}, dimensions={0} | all-to-all | bytes 1572864 | tf_op jit(solution)/shard_map/all_to_all | solution.py:272
  170.7 2.3 %add.33 = f32[8,64,384]{2,1,0:T(8,128)} custom-call(f32[48,5,8,128]{3,2,1,0:T(8,128)} %get-tuple-element.12.f_ref, f32[48,4,8,128]{3,2,1,0:T(8,128)S(1)} %all_to_all.22.y_ref), custom_call_target="tpu_custom_call" | custom-call | tf_op jit(solution)/shard_map/add/pallas_call | solution.py:273
  (6 shorter events, 0.0 us)
Async XLA Ops:
  1.0 7.6 %collective-permute-start = (f32[2,8,384]{2,1,0:T(8,128)S(1)}, f32[2,8,384]{2,1,0:T(8,128)S(1)}, u32[]{:S(2)}, u32[]{:S(2)}) collective-permute-start(f32[2,8,384]{2,1,0:T(8,128)S(1)} %get-tuple-element.10), channel_id=1, source_target_pairs={{0,1},{1,2},{2,3},{3,4},{4,5},{5,6},{6,7},{7,8},{8,9},{9,10},{10,1... | collective-permute-start | bytes 73736 | tf_op jit(solution)/shard_map/ppermute | solution.py:221
  6.0 7.2 %collective-permute-start.1 = (f32[3,8,384]{2,1,0:T(8,128)S(1)}, f32[3,8,384]{2,1,0:T(8,128)S(1)}, u32[]{:S(2)}, u32[]{:S(2)}) collective-permute-start(f32[3,8,384]{2,1,0:T(8,128)S(1)} %get-tuple-element.11), channel_id=1, source_target_pairs={{1,0},{2,1},{3,2},{4,3},{5,4},{6,5},{7,6},{8,7},{9,8},{10,9},{11,1... | collective-permute-start | bytes 110600 | tf_op jit(solution)/shard_map/ppermute | solution.py:222
  7.3 0.7 copy-start
  30.1 56.8 %all-to-all-start = ((f32[48,5,8,128]{3,2,1,0:T(8,128)}), f32[48,5,8,128]{3,2,1,0:T(8,128)S(1)}, u32[]{:S(2)}, u32[]{:S(2)}) async-start(f32[48,5,8,128]{3,2,1,0:T(8,128)} %get-tuple-element.12.f_ref), calls=%async_computation | async-start | bytes 1966080 | tf_op jit(solution)/shard_map/all_to_all | solution.py:240
  47.4 6.2 %collective-permute-start.2 = (f32[8,8,128]{2,1,0:T(8,128)S(1)}, f32[8,8,128]{2,1,0:T(8,128)S(1)}, u32[]{:S(2)}, u32[]{:S(2)}) collective-permute-start(f32[8,8,128]{2,1,0:T(8,128)S(1)} %get-tuple-element.14), channel_id=1, source_target_pairs={{0,12},{1,13},{2,14},{3,15},{4,8},{5,9},{6,10},{7,11},{8,4},{9,5},... | collective-permute-start | bytes 98312 | tf_op jit(solution)/shard_map/ppermute | solution.py:188
  53.6 4.8 %collective-permute-start.3 = (f32[4,8,128]{2,1,0:T(8,128)S(1)}, f32[4,8,128]{2,1,0:T(8,128)S(1)}, u32[]{:S(2)}, u32[]{:S(2)}) collective-permute-start(f32[4,8,128]{2,1,0:T(8,128)S(1)} %get-tuple-element.16), channel_id=1, source_target_pairs={{0,4},{1,5},{2,6},{3,7},{4,0},{5,1},{6,2},{7,3},{8,12},{9,13},{10,... | collective-permute-start | bytes 49160 | tf_op jit(solution)/shard_map/ppermute | solution.py:188
  58.3 7.5 %collective-permute-start.4 = (f32[2,8,128]{2,1,0:T(8,128)S(1)}, f32[2,8,128]{2,1,0:T(8,128)S(1)}, u32[]{:S(2)}, u32[]{:S(2)}) collective-permute-start(f32[2,8,128]{2,1,0:T(8,128)S(1)} %get-tuple-element.18), channel_id=1, source_target_pairs={{0,3},{1,2},{2,1},{3,0},{4,7},{5,6},{6,5},{7,4},{8,11},{9,10},{10,... | collective-permute-start | bytes 24584 | tf_op jit(solution)/shard_map/ppermute | solution.py:188
  65.8 6.3 %collective-permute-start.5 = (f32[1,8,128]{2,1,0:T(8,128)S(1)}, f32[1,8,128]{2,1,0:T(8,128)S(1)}, u32[]{:S(2)}, u32[]{:S(2)}) collective-permute-start(f32[1,8,128]{2,1,0:T(8,128)S(1)} %get-tuple-element.19), channel_id=1, source_target_pairs={{0,1},{1,0},{2,3},{3,2},{4,5},{5,4},{6,7},{7,6},{8,9},{9,8},{10,11... | collective-permute-start | bytes 12296 | tf_op jit(solution)/shard_map/ppermute | solution.py:188

commit v4 on v3

--- a/solution.py
+++ b/solution.py
@@ -10,6 +10,7 @@
 PLANE = 4
 SLAB_SWAPS = (1, 3, 4, 12)
 HIGHEST = lax.Precision.HIGHEST
+ROOM = pltpu.CompilerParams(vmem_limit_bytes=12 << 20)
 SMEM = pltpu.SMEM
 VMEM = pltpu.VMEM
 
@@ -41,14 +42,17 @@
 
 
 def forecast_kernel(
-    slab_ref, tile_ref, shift_ref, h_ref, low_ref, high_ref, u_ref, v_ref, weights_ref, values_ref, noise_ref, cov_ref,
-    f_ref, near_ref, far_ref, white_ref,
+    slab_ref, spot0_ref, spot1_ref, spot2_ref, spot3_ref, h_ref, low_ref, high_ref, u_ref, v_ref, weights_ref,
+    values_ref, noise_ref, cov_hbm,
+    f_ref, first_ref, second_ref, near_ref, far_ref, white_ref, cov_ref, cov_sem,
 ):
+    cov_copy = pltpu.make_async_copy(cov_hbm, cov_ref, cov_sem)
+    cov_copy.start()
     members = noise_ref.shape[0]
     rows, cols = u_ref.shape
     per_row = cols // LANES
-    mems = f_ref.shape[0]
-    tiles = f_ref.shape[1] - 1
+    mems, held = second_ref.shape[:2]
+    tiles = 2 * held
     lane = lax.broadcasted_iota(jnp.int32, (members, cols), 1)
     at_first = lane == 0
     at_last = lane == cols - 1
@@ -93,31 +97,38 @@
         f = h - columns_term(h, u_ref[r : r + 1, :]) - (flux_up - flux)
         for t in range(per_row):
             at = r * per_row + t
-            f_ref[at // tiles, at % tiles] = f[:, t * LANES : (t + 1) * LANES]
+            tile = f[:, t * LANES : (t + 1) * LANES]
+            f_ref[at] = tile
+            if at % tiles < held:
+                first_ref[at // tiles, at % tiles] = tile
+            else:
+                second_ref[at // tiles, at % tiles - held] = tile
         carry = (h_up, h_up2, d_up2, half_up, flux_up)
 
-    foot, count = tile_ref.shape
+    spots = (spot0_ref, spot1_ref, spot2_ref, spot3_ref)
+    foot, count = weights_ref.shape
     lane1 = lax.broadcasted_iota(jnp.int32, (members, LANES), 1)
 
     def observe(o, picked):
         here = lane1 == o
         out = []
         for k in range(foot):
-            at = tile_ref[k, o]
-            tile = f_ref[at // tiles, at % tiles]
-            out.append(jnp.where(here, pltpu.roll(tile, shift_ref[k, o], 1), picked[k]))
+            spot = spots[k][o]
+            tile = f_ref[lax.shift_right_logical(spot, LANES.bit_length() - 1)]
+            out.append(jnp.where(here, pltpu.roll(tile, spot & (LANES - 1), 1), picked[k]))
         return tuple(out)
 
     zero = jnp.zeros((members, LANES), jnp.float32)
-    picked = lax.fori_loop(0, count, observe, (zero,) * foot, unroll=4)
+    picked = lax.fori_loop(0, count, observe, (zero,) * foot, unroll=8)
     weights = weights_ref[...].astype(jnp.float32)
     obs = picked[0] * weights[0:1]
     for k in range(1, foot):
         obs = obs + picked[k] * weights[k : k + 1]
     obs = obs / jnp.sum(weights, axis=0, keepdims=True)
     for p in range(mems):
-        f_ref[p, tiles] = obs
+        first_ref[p, held] = obs
     innovation = values_ref[...] + noise_ref[...] - obs
+    cov_copy.wait()
     white = jnp.dot(innovation, cov_ref[...], precision=HIGHEST, preferred_element_type=jnp.float32)
     order = swap_order(SLAB_SWAPS)
     blocks = white_ref
@@ -143,17 +154,18 @@
     e = x_ref[0]
     for s in range(1, x_ref.shape[0]):
         e = e + x_ref[s]
-    for z in range(out_ref.shape[0]):
-        out_ref[z] = e
-
-
-def mixing_kernel(x_ref, e_ref, out_ref):
+    out_ref[...] = e
+
+
+def mixing_kernel(first_ref, second_ref, e_ref, out_ref):
     mems, tiles, members, width = out_ref.shape
     total = mems * members
+    held = second_ref.shape[1]
     e = e_ref[...]
     depth = mems // PLANE
     for t in range(tiles):
-        x = x_ref[:, t].reshape(total, width)
+        x = first_ref[:, t] if t < held else second_ref[:, t - held]
+        x = x.reshape(total, width)
         x = x - jnp.mean(x, axis=0, keepdims=True)
         u = jnp.dot(e, x, precision=HIGHEST, preferred_element_type=jnp.float32) / (total - 1)
         for q in range(PLANE):
@@ -165,10 +177,11 @@
 def add_kernel(f_ref, y_ref, out_ref):
     rows, cols = out_ref.shape[1:]
     per_row = cols // LANES
+    start = pl.program_id(0) * (rows * per_row)
     for r in range(0, rows, 8):
         for t in range(per_row):
-            at = [(r + i) * per_row + t for i in range(8)]
-            tile = jnp.stack([f_ref[i // y_ref.shape[1], i % y_ref.shape[1]] + y_ref[i // y_ref.shape[1], i % y_ref.shape[1]] for i in at], 0)
+            at = [start + (r + i) * per_row + t for i in range(8)]
+            tile = jnp.stack([f_ref[i] + y_ref[i] for i in at], 0)
             out_ref[:, r : r + 8, t * LANES : (t + 1) * LANES] = jnp.swapaxes(tile, 0, 1)
 
 
@@ -178,6 +191,10 @@
 
 def v32(*shape):
     return VMEM(shape, jnp.float32)
+
+
+def away(x):
+    return pltpu.with_memory_space_constraint(x, pltpu.HBM)
 
 
 def near(x):
@@ -200,8 +217,8 @@
     planes = [[z * PLANE + q for q in range(PLANE)] for z in range(depth)]
     columns = [[z * PLANE + q for z in range(depth)] for q in range(PLANE)]
     cells = obs_cells.T - slab * (rows * cols)
-    cell_tile = lax.shift_right_logical(cells, LANES.bit_length() - 1)
     cell_shift = (lax.broadcasted_iota(jnp.int32, cells.shape, 1) - cells) & (LANES - 1)
+    spots = (cells & -LANES) | cell_shift
 
     up, down = pl.pallas_call(
         edges_kernel,
@@ -216,28 +233,32 @@
             pl.BlockSpec((2, members, cols), lambda i: (0, 0, 0)),
         ],
         out_shape=[v32(3, members, cols), v32(2, members, cols)],
+        compiler_params=ROOM,
         name="edges",
-    )(thickness, thickness, face_v)
+    )(away(thickness), away(thickness), away(face_v))
     low = lax.ppermute(down, "slab", [(i, i + 1) for i in range(slabs - 1)])
     high = lax.ppermute(up, "slab", [(i + 1, i) for i in range(slabs - 1)])
 
-    forecast, white, white_far = pl.pallas_call(
+    forecast, first, second, white, white_far = pl.pallas_call(
         forecast_kernel,
-        in_specs=[sspec(), sspec(), sspec()] + [vspec() for _ in range(9)],
-        out_specs=[vspec() for _ in range(3)],
+        in_specs=[sspec() for _ in range(5)] + [vspec() for _ in range(8)] + [pl.BlockSpec(memory_space=pltpu.HBM)],
+        out_specs=[vspec() for _ in range(5)],
         out_shape=[
-            v32(mems, tiles + 1, members, LANES),
+            v32(mems * tiles, members, LANES),
+            v32(mems, tiles // 2 + 1, members, LANES),
+            v32(mems, tiles // 2, members, LANES),
             v32(slabs // 2, members, LANES),
             v32(slabs // 2, members, LANES),
         ],
-        scratch_shapes=[v32(slabs, members, LANES)],
+        scratch_shapes=[v32(slabs, members, LANES), v32(*cov_inverse.shape), pltpu.SemaphoreType.DMA],
+        compiler_params=ROOM,
         name="forecast",
     )(
-        slab, cell_tile, cell_shift, thickness, near(low), near(high), face_u, face_v, obs_weights.T,
-        obs_values.reshape(1, -1), obs_noise, cov_inverse,
+        slab, spots[0], spots[1], spots[2], spots[3], near(thickness), near(low), near(high), near(face_u),
+        near(face_v), near(obs_weights.T), near(obs_values.reshape(1, -1)), near(obs_noise), away(cov_inverse),
     )
 
-    cell_state = lax.all_to_all(forecast, "mem", 0, 0, tiled=True)
+    first = lax.all_to_all(first, "mem", 0, 0, tiled=True)
     arrived = swapped(white_far, "slab", SLAB_SWAPS[-1])
     for k in SLAB_SWAPS[-2::-1]:
         half = white.shape[0] // 2
@@ -248,35 +269,40 @@
         in_specs=[sspec(), sspec(), vspec(), vspec(), vspec()],
         out_specs=vspec(),
         out_shape=v32(slabs, members, mems * members),
+        compiler_params=ROOM,
         name="products",
-    )(slab, taper_mask, near(cell_state), near(white[0]), near(arrived[0]))
+    )(slab, taper_mask, near(first), near(white[0]), near(arrived[0]))
     parts = lax.all_to_all(parts, "slab", 0, 0, tiled=True)
-    copies = pl.pallas_call(
+    second = lax.all_to_all(second, "mem", 0, 0, tiled=True)
+    own_rows = pl.pallas_call(
         summed_kernel,
         in_specs=[vspec()],
         out_specs=vspec(),
-        out_shape=v32(depth, members, mems * members),
+        out_shape=v32(members, mems * members),
+        compiler_params=ROOM,
         name="summed",
     )(near(parts))
-    over_z = lax.all_to_all(copies, "mem", 0, 0, tiled=True, axis_index_groups=columns)
-    ensemble = lax.all_gather(
-        over_z.reshape(depth * members, mems * members), "mem", axis=0, tiled=True, axis_index_groups=planes
-    )
+    ensemble = lax.all_gather(own_rows, "mem", axis=0, tiled=True, axis_index_groups=columns)
+    ensemble = lax.all_gather(ensemble, "mem", axis=0, tiled=True, axis_index_groups=planes)
     update = pl.pallas_call(
         mixing_kernel,
-        in_specs=[vspec(), vspec()],
+        in_specs=[vspec(), vspec(), vspec()],
         out_specs=vspec(),
         out_shape=v32(mems, tiles, members, LANES),
+        compiler_params=ROOM,
         name="mixing",
-    )(near(cell_state), near(ensemble))
+    )(near(first), near(second), near(ensemble))
     returned = lax.all_to_all(update, "mem", 0, 0, tiled=True)
+    steps = 4
     return pl.pallas_call(
         add_kernel,
+        grid=(steps,),
         in_specs=[vspec(), vspec()],
-        out_specs=vspec(),
+        out_specs=pl.BlockSpec((members, rows // steps, cols), lambda i: (0, i, 0)),
         out_shape=f32(members, rows, cols),
+        compiler_params=ROOM,
         name="add",
-    )(near(forecast), near(returned))
+    )(near(forecast), near(returned.reshape(mems * tiles, members, LANES)))
 
 
 def solution(mesh):

time: 174 us -> 186 us (1.069)
  blocking collectives: 80.6 us -> 99.8 us
  waiting for transfers between devices: 26.5 us -> 14.7 us
  starting transfers between devices: 41.1 us -> 51.5 us
  Pallas kernels: 23.4 us -> 17.9 us
    all_gather x1 -> x2, blocking collectives: 9.24 us -> 40.7 us  [the longest x1 28.6 us: local(): lax.all_gather(own_rows, 'mem', axis=0, tiled=True, axis_index_groups=col...]
    all_to_all x1 -> x0, blocking collectives: 14.3 us -> none  [local(): lax.all_to_all(copies, 'mem', 0, 0, tiled=True, axis_index_groups=columns)]
    all_to_all x1 -> x2, waiting for transfers between devices: 14.7 us -> 2.28 us  [the longest x1 2.28 us: local(): first = lax.all_to_all(first, 'mem', 0, 0, tiled=True)]
    all_to_all x1 -> x2, starting transfers between devices: 17.3 us -> 27.5 us  [the longest x1 17.3 us: local(): first = lax.all_to_all(first, 'mem', 0, 0, tiled=True)]
    pallas_call x3, Pallas kernels: 21.2 us -> 15.7 us  [the longest x1 12.2 us: local(): pl.pallas_call(forecast_kernel, in_specs=[sspec() for _ in range(5)] + [v...]
    all_to_all x1, blocking collectives: 37.6 us -> 40 us  [local(): returned = lax.all_to_all(update, 'mem', 0, 0, tiled=True)]
  transfers between devices with their start and end apart: 7 -> 8, of which waited for: 6 -> 6; matrix products, arithmetic and copies ran while one was open for 0% -> 0% of each run, Pallas kernels for 0% -> 0%
where the time goes in v4:
time: 186 us; the launch traced here: 185 us
  blocking collectives  99.8 us (54%)
  starting transfers between devices  51.5 us (28%)
  Pallas kernels  17.9 us (10%)
  waiting for transfers between devices  14.7 us (8%)
    all_to_all x1, blocking collectives, local(): returned = lax.all_to_all(update, 'mem', 0, 0, tiled=True)  40 us
    all_gather x1, blocking collectives, local(): lax.all_gather(own_rows, 'mem', axis=0, tiled=True, axis_index_groups=col...  28.6 us
    all_to_all x1, blocking collectives, local(): parts = lax.all_to_all(parts, 'slab', 0, 0, tiled=True)  19 us
    ppermute x4, starting transfers between devices, swapped(): lax.ppermute(x, axis, [(i, i ^ k) for i in range(lax.axis_size(axis))])  17.6 us
    all_to_all x1, starting transfers between devices, local(): first = lax.all_to_all(first, 'mem', 0, 0, tiled=True)  17.3 us
    pallas_call x1, Pallas kernels, local(): pl.pallas_call(forecast_kernel, in_specs=[sspec() for _ in range(5)] + [v...  12.2 us
    all_gather x1, blocking collectives, local(): lax.all_gather(ensemble, 'mem', axis=0, tiled=True, axis_index_groups=pla...  12.1 us
    all_to_all x1, starting transfers between devices, local(): second = lax.all_to_all(second, 'mem', 0, 0, tiled=True)  10.2 us
  transfers between devices with their start and end apart: 8, of which 6 were waited for; matrix products, arithmetic and copies ran while one was open for 0% of the time, Pallas kernels for 0%

profile of v4, /device:TPU:1, one launch (start us, length us, event | category | flops | bytes accessed | tf_op | source)
XLA Modules:
  0.0 185.3 jit_solution(6883384320676847056)
XLA Ops:
  0.0 1.0 edges.1
  1.1 5.0 %collective-permute-start = (f32[2,8,384]{2,1,0:T(8,128)S(1)}, f32[2,8,384]{2,1,0:T(8,128)S(1)}, u32[]{:S(2)}, u32[]{:S(2)}) collective-permute-start(f32[2,8,384]{2,1,0:T(8,128)S(1)} %get-tuple-element.12), channel_id=1, source_target_pairs={{0,1},{1,2},{2,3},{3,4},{4,5},{5,6},{6,7},{7,8},{8,9},{9,10},{10,1... | collective-permute-start | bytes 73736 | tf_op jit(solution)/shard_map/ppermute | solution.py:239
  6.1 1.3 collective-permute-start.1
  7.4 0.7 copy-done.7
  8.1 5.2 %collective-permute-done.1.high_ref = f32[3,8,384]{2,1,0:T(8,128)S(1)} collective-permute-done((f32[3,8,384]{2,1,0:T(8,128)S(1)}, f32[3,8,384]{2,1,0:T(8,128)S(1)}, u32[]{:S(2)}, u32[]{:S(2)}) %collective-permute-start.1) | collective-permute-done | bytes 36896 | tf_op jit(solution)/shard_map/ppermute | solution.py:240
  14.0 12.2 %forecast.1 = (f32[192,8,128]{2,1,0:T(8,128)S(1)}, f32[48,3,8,128]{3,2,1,0:T(8,128)}, f32[48,2,8,128]{3,2,1,0:T(8,128)}, f32[8,8,128]{2,1,0:T(8,128)S(1)}, f32[8,8,128]{2,1,0:T(8,128)S(1)}) custom-call(s32[1]{0:T(128)} %bitcast.slab_ref, s32[128]{0:T(128)S(1)} %get-tuple-element.28.spot0_ref, s32[128]{0:T(128)S(1)} %get-tuple-element.27.spot1_ref, ...), custom_call_target="tpu_custom_call" | custom-call | tf_op jit(solution)/shard_map/forecast/pallas_call | solution.py:242
  26.1 17.3 %all-to-all-start = ((f32[48,3,8,128]{3,2,1,0:T(8,128)}), f32[48,3,8,128]{3,2,1,0:T(8,128)S(1)}, u32[]{:S(2)}, u32[]{:S(2)}) async-start(f32[48,3,8,128]{3,2,1,0:T(8,128)} %get-tuple-element.15), calls=%async_computation | async-start | bytes 1179648 | tf_op jit(solution)/shard_map/all_to_all | solution.py:261
  43.5 4.4 %collective-permute-start.2 = (f32[8,8,128]{2,1,0:T(8,128)S(1)}, f32[8,8,128]{2,1,0:T(8,128)S(1)}, u32[]{:S(2)}, u32[]{:S(2)}) collective-permute-start(f32[8,8,128]{2,1,0:T(8,128)S(1)} %get-tuple-element.18), channel_id=1, source_target_pairs={{0,12},{1,13},{2,14},{3,15},{4,8},{5,9},{6,10},{7,11},{8,4},{9,5},... | collective-permute-start | bytes 98312 | tf_op jit(solution)/shard_map/ppermute | solution.py:205
  47.9 1.8 collective-permute-done.2
  49.6 1.9 %collective-permute-start.3 = (f32[4,8,128]{2,1,0:T(8,128)S(1)}, f32[4,8,128]{2,1,0:T(8,128)S(1)}, u32[]{:S(2)}, u32[]{:S(2)}) collective-permute-start(f32[4,8,128]{2,1,0:T(8,128)S(1)} %get-tuple-element.20), channel_id=1, source_target_pairs={{0,4},{1,5},{2,6},{3,7},{4,0},{5,1},{6,2},{7,3},{8,12},{9,13},{10,... | collective-permute-start | bytes 49160 | tf_op jit(solution)/shard_map/ppermute | solution.py:205
  51.6 2.8 %collective-permute-done.3 = f32[4,8,128]{2,1,0:T(8,128)S(1)} collective-permute-done((f32[4,8,128]{2,1,0:T(8,128)S(1)}, f32[4,8,128]{2,1,0:T(8,128)S(1)}, u32[]{:S(2)}, u32[]{:S(2)}) %collective-permute-start.3) | collective-permute-done | bytes 16416 | tf_op jit(solution)/shard_map/ppermute | solution.py:205
  54.4 6.1 %collective-permute-start.4 = (f32[2,8,128]{2,1,0:T(8,128)S(1)}, f32[2,8,128]{2,1,0:T(8,128)S(1)}, u32[]{:S(2)}, u32[]{:S(2)}) collective-permute-start(f32[2,8,128]{2,1,0:T(8,128)S(1)} %get-tuple-element.22), channel_id=1, source_target_pairs={{0,3},{1,2},{2,1},{3,0},{4,7},{5,6},{6,5},{7,4},{8,11},{9,10},{10,... | collective-permute-start | bytes 24584 | tf_op jit(solution)/shard_map/ppermute | solution.py:205
  60.5 1.3 collective-permute-done.4
  61.9 5.2 %collective-permute-start.5 = (f32[1,8,128]{2,1,0:T(8,128)S(1)}, f32[1,8,128]{2,1,0:T(8,128)S(1)}, u32[]{:S(2)}, u32[]{:S(2)}) collective-permute-start(f32[1,8,128]{2,1,0:T(8,128)S(1)} %get-tuple-element.23), channel_id=1, source_target_pairs={{0,1},{1,0},{2,3},{3,2},{4,5},{5,4},{6,7},{7,6},{8,9},{9,8},{10,11... | collective-permute-start | bytes 12296 | tf_op jit(solution)/shard_map/ppermute | solution.py:205
  67.1 1.3 collective-permute-done.5
  68.4 2.3 %all-to-all-done.x_ref.first_ref = f32[48,3,8,128]{3,2,1,0:T(8,128)S(1)} async-done(((f32[48,3,8,128]{3,2,1,0:T(8,128)}), f32[48,3,8,128]{3,2,1,0:T(8,128)S(1)}, u32[]{:S(2)}, u32[]{:S(2)}) %all-to-all-start) | async-done | bytes 589856 | tf_op jit(solution)/shard_map/all_to_all | solution.py:261
  70.6 1.1 products.1
  71.7 19.0 %all_to_all.20.x_ref = f32[16,8,384]{2,1,0:T(8,128)S(1)} all-to-all(f32[16,8,384]{2,1,0:T(8,128)S(1)} %products.1), channel_id=1, replica_groups=mesh['mem'=48,'slab'=16] {'slab'}, dimensions={0} | all-to-all | bytes 393216 | tf_op jit(solution)/shard_map/all_to_all | solution.py:275
  90.8 10.2 %all-to-all-start.1 = ((f32[48,2,8,128]{3,2,1,0:T(8,128)}), f32[48,2,8,128]{3,2,1,0:T(8,128)S(1)}, u32[]{:S(2)}, u32[]{:S(2)}) async-start(f32[48,2,8,128]{3,2,1,0:T(8,128)} %get-tuple-element.16), calls=%async_computation.1 | async-start | bytes 786432 | tf_op jit(solution)/shard_map/all_to_all | solution.py:276
  101.0 28.6 %all_gather.6 = f32[96,384]{1,0:T(8,128)S(1)} all-gather(f32[8,384]{1,0:T(8,128)S(1)} %summed.1), channel_id=1, replica_groups={{0,64,128,192,256,320,384,448,512,576,640,704},{16,80,144,208,272,336,4..., dimensions={0}, use_global_device_ids=true | all-gather | bytes 159744 | tf_op jit(solution)/shard_map/all_gather | solution.py:285
  129.6 12.1 %all_gather.7.e_ref = f32[384,384]{1,0:T(8,128)S(1)} all-gather(f32[96,384]{1,0:T(8,128)S(1)} %all_gather.6), channel_id=1, replica_groups={{0,16,32,48},{64,80,96,112},{128,144,160,176},{192,208,224,240},{256,27..., dimensions={0}, use_global_device_ids=true | all-gather | bytes 737280 | tf_op jit(solution)/shard_map/all_gather | solution.py:286
  141.7 2.1 %mixing.1 = f32[48,4,8,128]{3,2,1,0:T(8,128)S(1)} custom-call(f32[48,3,8,128]{3,2,1,0:T(8,128)S(1)} %all-to-all-done.x_ref.first_ref, f32[48,2,8,128]{3,2,1,0:T(8,128)S(1)} %all-to-all-done.1.second_ref, f32[384,384]{1,0:T(8,128)S(1)} %all_gather.7.e_ref), custom_call_target="tpu_custom_call" | custom-call | tf_op jit(solution)/shard_map/mixing/pallas_call | solution.py:287
  143.8 40.0 %all_to_all.21 = f32[48,4,8,128]{3,2,1,0:T(8,128)S(1)} all-to-all(f32[48,4,8,128]{3,2,1,0:T(8,128)S(1)} %mixing.1), channel_id=1, replica_groups=mesh['mem'=48,'slab'=16] {'mem'}, dimensions={0} | all-to-all | bytes 1572864 | tf_op jit(solution)/shard_map/all_to_all | solution.py:295
  183.8 1.5 add.33
  (23 shorter events, 0.7 us)
Async XLA Ops:
  0.0 13.3 %copy-start = (f32[8,64,384]{2,1,0:T(8,128)S(1)}, f32[8,64,384]{2,1,0:T(8,128)}, u32[]{:S(2)}) copy-start(f32[8,64,384]{2,1,0:T(8,128)} %h_ref.1) | copy-start | bytes 2359300
  0.0 13.3 %copy-start.1 = (f32[64,384]{1,0:T(8,128)S(1)}, f32[64,384]{1,0:T(8,128)}, u32[]{:S(2)}) copy-start(f32[64,384]{1,0:T(8,128)} %v_ref.3) | copy-start | bytes 294916
  0.0 13.3 %copy-start.2 = (f32[64,384]{1,0:T(8,128)S(1)}, f32[64,384]{1,0:T(8,128)}, u32[]{:S(2)}) copy-start(f32[64,384]{1,0:T(8,128)} %u_ref.1) | copy-start | bytes 294916
  1.1 7.0 %collective-permute-start = (f32[2,8,384]{2,1,0:T(8,128)S(1)}, f32[2,8,384]{2,1,0:T(8,128)S(1)}, u32[]{:S(2)}, u32[]{:S(2)}) collective-permute-start(f32[2,8,384]{2,1,0:T(8,128)S(1)} %get-tuple-element.12), channel_id=1, source_target_pairs={{0,1},{1,2},{2,3},{3,4},{4,5},{5,6},{6,7},{7,8},{8,9},{9,10},{10,1... | collective-permute-start | bytes 73736 | tf_op jit(solution)/shard_map/ppermute | solution.py:239
  6.1 7.2 %collective-permute-start.1 = (f32[3,8,384]{2,1,0:T(8,128)S(1)}, f32[3,8,384]{2,1,0:T(8,128)S(1)}, u32[]{:S(2)}, u32[]{:S(2)}) collective-permute-start(f32[3,8,384]{2,1,0:T(8,128)S(1)} %get-tuple-element.13), channel_id=1, source_target_pairs={{1,0},{2,1},{3,2},{4,3},{5,4},{6,5},{7,6},{8,7},{9,8},{10,9},{11,1... | collective-permute-start | bytes 110600 | tf_op jit(solution)/shard_map/ppermute | solution.py:240
  7.4 0.7 copy-start.7
  13.3 0.7 copy-start.4
  13.3 0.7 copy-start.5
  13.3 0.7 copy-start.6
  26.1 44.5 %all-to-all-start = ((f32[48,3,8,128]{3,2,1,0:T(8,128)}), f32[48,3,8,128]{3,2,1,0:T(8,128)S(1)}, u32[]{:S(2)}, u32[]{:S(2)}) async-start(f32[48,3,8,128]{3,2,1,0:T(8,128)} %get-tuple-element.15), calls=%async_computation | async-start | bytes 1179648 | tf_op jit(solution)/shard_map/all_to_all | solution.py:261
  43.5 6.2 %collective-permute-start.2 = (f32[8,8,128]{2,1,0:T(8,128)S(1)}, f32[8,8,128]{2,1,0:T(8,128)S(1)}, u32[]{:S(2)}, u32[]{:S(2)}) collective-permute-start(f32[8,8,128]{2,1,0:T(8,128)S(1)} %get-tuple-element.18), channel_id=1, source_target_pairs={{0,12},{1,13},{2,14},{3,15},{4,8},{5,9},{6,10},{7,11},{8,4},{9,5},... | collective-permute-start | bytes 98312 | tf_op jit(solution)/shard_map/ppermute | solution.py:205
  49.6 4.8 %collective-permute-start.3 = (f32[4,8,128]{2,1,0:T(8,128)S(1)}, f32[4,8,128]{2,1,0:T(8,128)S(1)}, u32[]{:S(2)}, u32[]{:S(2)}) collective-permute-start(f32[4,8,128]{2,1,0:T(8,128)S(1)} %get-tuple-element.20), channel_id=1, source_target_pairs={{0,4},{1,5},{2,6},{3,7},{4,0},{5,1},{6,2},{7,3},{8,12},{9,13},{10,... | collective-permute-start | bytes 49160 | tf_op jit(solution)/shard_map/ppermute | solution.py:205
  54.4 7.5 %collective-permute-start.4 = (f32[2,8,128]{2,1,0:T(8,128)S(1)}, f32[2,8,128]{2,1,0:T(8,128)S(1)}, u32[]{:S(2)}, u32[]{:S(2)}) collective-permute-start(f32[2,8,128]{2,1,0:T(8,128)S(1)} %get-tuple-element.22), channel_id=1, source_target_pairs={{0,3},{1,2},{2,1},{3,0},{4,7},{5,6},{6,5},{7,4},{8,11},{9,10},{10,... | collective-permute-start | bytes 24584 | tf_op jit(solution)/shard_map/ppermute | solution.py:205
  61.9 8.8 %copy-start.3 = (s32[16,16]{1,0:T(8,128)S(1)}, s32[16,16]{1,0:T(8,128)}, u32[]{:S(2)}) copy-start(s32[16,16]{1,0:T(8,128)} %mask_ref.1) | copy-start | bytes 3076
  61.9 6.5 %collective-permute-start.5 = (f32[1,8,128]{2,1,0:T(8,128)S(1)}, f32[1,8,128]{2,1,0:T(8,128)S(1)}, u32[]{:S(2)}, u32[]{:S(2)}) collective-permute-start(f32[1,8,128]{2,1,0:T(8,128)S(1)} %get-tuple-element.23), channel_id=1, source_target_pairs={{0,1},{1,0},{2,3},{3,2},{4,5},{5,4},{6,7},{7,6},{8,9},{9,8},{10,11... | collective-permute-start | bytes 12296 | tf_op jit(solution)/shard_map/ppermute | solution.py:205
  90.8 50.9 %all-to-all-start.1 = ((f32[48,2,8,128]{3,2,1,0:T(8,128)}), f32[48,2,8,128]{3,2,1,0:T(8,128)S(1)}, u32[]{:S(2)}, u32[]{:S(2)}) async-start(f32[48,2,8,128]{3,2,1,0:T(8,128)} %get-tuple-element.16), calls=%async_computation.1 | async-start | bytes 786432 | tf_op jit(solution)/shard_map/all_to_all | solution.py:276

commit v5 on v4

--- a/solution.py
+++ b/solution.py
@@ -8,7 +8,8 @@
 
 LANES = 128
 PLANE = 4
-SLAB_SWAPS = (1, 3, 4, 12)
+RUN = 4
+COLUMN = 4
 HIGHEST = lax.Precision.HIGHEST
 ROOM = pltpu.CompilerParams(vmem_limit_bytes=12 << 20)
 SMEM = pltpu.SMEM
@@ -17,13 +18,6 @@
 
 def minmod(a, b):
     return jnp.maximum(jnp.minimum(a, b), 0.0) + jnp.minimum(jnp.maximum(a, b), 0.0)
-
-
-def swap_order(swaps):
-    order = [0]
-    for k in swaps:
-        order = order + [v ^ k for v in order]
-    return order
 
 
 def vspec():
@@ -44,16 +38,15 @@
 def forecast_kernel(
     slab_ref, spot0_ref, spot1_ref, spot2_ref, spot3_ref, h_ref, low_ref, high_ref, u_ref, v_ref, weights_ref,
     values_ref, noise_ref, cov_hbm,
-    f_ref, first_ref, second_ref, near_ref, far_ref, white_ref, cov_ref, cov_sem,
+    f_ref, obs_ref, white0_ref, white1_ref, white2_ref, white3_ref, stack_ref, cov_ref, cov_sem,
 ):
     cov_copy = pltpu.make_async_copy(cov_hbm, cov_ref, cov_sem)
     cov_copy.start()
     members = noise_ref.shape[0]
     rows, cols = u_ref.shape
     per_row = cols // LANES
-    mems, held = second_ref.shape[:2]
-    tiles = 2 * held
-    lane = lax.broadcasted_iota(jnp.int32, (members, cols), 1)
+    batch = 8
+    lane = lax.broadcasted_iota(jnp.int32, (members * batch, cols), 1)
     at_first = lane == 0
     at_last = lane == cols - 1
 
@@ -94,15 +87,15 @@
         d_up2 = h_up2 - h_up
         half_up = 0.5 * minmod(d_up, d_up2)
         flux_up = row_flux(v, h, half, h_up, half_up)
-        f = h - columns_term(h, u_ref[r : r + 1, :]) - (flux_up - flux)
+        if r % batch == 0:
+            inside = range(r, r + batch)
+            term = columns_term(
+                jnp.concatenate([row(i) for i in inside], 0),
+                jnp.concatenate([jnp.broadcast_to(u_ref[i : i + 1, :], (members, cols)) for i in inside], 0),
+            )
+        f = h - term[r % batch * members : (r % batch + 1) * members] - (flux_up - flux)
         for t in range(per_row):
-            at = r * per_row + t
-            tile = f[:, t * LANES : (t + 1) * LANES]
-            f_ref[at] = tile
-            if at % tiles < held:
-                first_ref[at // tiles, at % tiles] = tile
-            else:
-                second_ref[at // tiles, at % tiles - held] = tile
+            f_ref[r * per_row + t] = f[:, t * LANES : (t + 1) * LANES]
         carry = (h_up, h_up2, d_up2, half_up, flux_up)
 
     spots = (spot0_ref, spot1_ref, spot2_ref, spot3_ref)
@@ -125,26 +118,36 @@
     for k in range(1, foot):
         obs = obs + picked[k] * weights[k : k + 1]
     obs = obs / jnp.sum(weights, axis=0, keepdims=True)
-    for p in range(mems):
-        first_ref[p, held] = obs
+    for p in range(obs_ref.shape[0]):
+        obs_ref[p] = obs
     innovation = values_ref[...] + noise_ref[...] - obs
     cov_copy.wait()
     white = jnp.dot(innovation, cov_ref[...], precision=HIGHEST, preferred_element_type=jnp.float32)
-    order = swap_order(SLAB_SWAPS)
-    blocks = white_ref
-    for s in range(len(order)):
-        blocks[s] = white[:, s * LANES : (s + 1) * LANES]
-    half = len(order) // 2
-    for i, v in enumerate(order):
-        ref, at = (near_ref, i) if i < half else (far_ref, i - half)
-        ref[at] = blocks[slab_ref[0] ^ v]
-
-
-def products_kernel(slab_ref, mask_ref, x_ref, white_ref, swap_ref, out_ref):
-    mems, tiles, members, width = x_ref.shape
-    a = x_ref[:, tiles - 1].reshape(mems * members, width)
+    groups = (white0_ref, white1_ref, white2_ref, white3_ref)
+    for s in range(len(groups) * COLUMN):
+        stack_ref[s] = white[:, s * LANES : (s + 1) * LANES]
+    for k, ref in enumerate(groups):
+        for i in range(COLUMN):
+            ref[i] = stack_ref[slab_ref[0] ^ (k * COLUMN + i)]
+
+
+def halved_kernel(x0_ref, x1_ref, x2_ref, x3_ref, out0_ref, out1_ref, out2_ref, out3_ref):
+    for i, ref in enumerate((out0_ref, out1_ref, out2_ref, out3_ref)):
+        ref[...] = x0_ref[i] + x1_ref[i] + x2_ref[i] + x3_ref[i]
+
+
+def source_z(z, t, k, depth):
+    runs = depth // RUN
+    run = lax.shift_right_logical(z, RUN.bit_length() - 1) + (0, runs - 1, 1)[t]
+    run = jnp.where(run >= runs, run - runs, run)
+    return run * RUN + ((z & (RUN - 1)) ^ k)
+
+
+def products_kernel(slab_ref, mask_ref, obs_ref, w0_ref, w1_ref, w2_ref, w3_ref, out_ref):
+    mems, members, width = obs_ref.shape
+    a = obs_ref[...].reshape(mems * members, width)
     a = a - jnp.mean(a, axis=0, keepdims=True)
-    w = white_ref[...] + swap_ref[...]
+    w = w0_ref[...] + w1_ref[...] + w2_ref[...] + w3_ref[...]
     p = lax.dot_general(w, a, (((1,), (1,)), ((), ())), precision=HIGHEST, preferred_element_type=jnp.float32)
     for s in range(out_ref.shape[0]):
         out_ref[s] = mask_ref[s, slab_ref[0]].astype(jnp.float32) * p
@@ -157,21 +160,20 @@
     out_ref[...] = e
 
 
-def mixing_kernel(first_ref, second_ref, e_ref, out_ref):
-    mems, tiles, members, width = out_ref.shape
+def mixing_kernel(z_ref, x_ref, e_ref, out_ref):
+    mems, tiles, members, width = x_ref.shape
     total = mems * members
-    held = second_ref.shape[1]
+    depth = mems // PLANE
     e = e_ref[...]
-    depth = mems // PLANE
     for t in range(tiles):
-        x = first_ref[:, t] if t < held else second_ref[:, t - held]
-        x = x.reshape(total, width)
+        x = x_ref[:, t].reshape(total, width)
         x = x - jnp.mean(x, axis=0, keepdims=True)
         u = jnp.dot(e, x, precision=HIGHEST, preferred_element_type=jnp.float32) / (total - 1)
         for q in range(PLANE):
-            for z in range(depth):
-                at = (q * depth + z) * members
-                out_ref[z * PLANE + q, t] = u[at : at + members]
+            for r in range(depth // RUN):
+                for k in range(RUN):
+                    at = (q * depth + r * RUN + k) * members
+                    out_ref[source_z(z_ref[0], r, k, depth) * PLANE + q, t] = u[at : at + members]
 
 
 def add_kernel(f_ref, y_ref, out_ref):
@@ -203,6 +205,11 @@
 
 def swapped(x, axis, k):
     return lax.ppermute(x, axis, [(i, i ^ k) for i in range(lax.axis_size(axis))])
+
+
+def shifted(x, axis, k):
+    count = lax.axis_size(axis)
+    return lax.ppermute(x, axis, [(i, (i + k) % count) for i in range(count)])
 
 
 def local(
@@ -215,7 +222,7 @@
     tiles = rows * cols // LANES // mems
     slab = lax.axis_index("slab").astype(jnp.int32).reshape(1)
     planes = [[z * PLANE + q for q in range(PLANE)] for z in range(depth)]
-    columns = [[z * PLANE + q for z in range(depth)] for q in range(PLANE)]
+    z = lax.shift_right_logical(lax.axis_index("mem").astype(jnp.int32), PLANE.bit_length() - 1).reshape(1)
     cells = obs_cells.T - slab * (rows * cols)
     cell_shift = (lax.broadcasted_iota(jnp.int32, cells.shape, 1) - cells) & (LANES - 1)
     spots = (cells & -LANES) | cell_shift
@@ -239,17 +246,12 @@
     low = lax.ppermute(down, "slab", [(i, i + 1) for i in range(slabs - 1)])
     high = lax.ppermute(up, "slab", [(i + 1, i) for i in range(slabs - 1)])
 
-    forecast, first, second, white, white_far = pl.pallas_call(
+    forecast, obs_copies, *white = pl.pallas_call(
         forecast_kernel,
         in_specs=[sspec() for _ in range(5)] + [vspec() for _ in range(8)] + [pl.BlockSpec(memory_space=pltpu.HBM)],
-        out_specs=[vspec() for _ in range(5)],
-        out_shape=[
-            v32(mems * tiles, members, LANES),
-            v32(mems, tiles // 2 + 1, members, LANES),
-            v32(mems, tiles // 2, members, LANES),
-            v32(slabs // 2, members, LANES),
-            v32(slabs // 2, members, LANES),
-        ],
+        out_specs=[vspec() for _ in range(6)],
+        out_shape=[v32(mems * tiles, members, LANES), v32(mems, members, LANES)]
+        + [v32(COLUMN, members, LANES) for _ in range(4)],
         scratch_shapes=[v32(slabs, members, LANES), v32(*cov_inverse.shape), pltpu.SemaphoreType.DMA],
         compiler_params=ROOM,
         name="forecast",
@@ -258,22 +260,27 @@
         near(face_v), near(obs_weights.T), near(obs_values.reshape(1, -1)), near(obs_noise), away(cov_inverse),
     )
 
-    first = lax.all_to_all(first, "mem", 0, 0, tiled=True)
-    arrived = swapped(white_far, "slab", SLAB_SWAPS[-1])
-    for k in SLAB_SWAPS[-2::-1]:
-        half = white.shape[0] // 2
-        white, white_far = white[:half] + arrived[:half], white[half:] + arrived[half:]
-        arrived = swapped(white_far, "slab", k)
+    obs_all = lax.all_to_all(obs_copies, "mem", 0, 0, tiled=True)
+    arrived = [swapped(white[k], "slab", k * COLUMN) for k in (1, 3, 2)]
+    white = pl.pallas_call(
+        halved_kernel,
+        in_specs=[vspec() for _ in range(4)],
+        out_specs=[vspec() for _ in range(4)],
+        out_shape=[v32(members, LANES) for _ in range(4)],
+        compiler_params=ROOM,
+        name="halved",
+    )(near(white[0]), *[near(x) for x in arrived])
+    arrived = [swapped(white[k], "slab", k) for k in (1, 3, 2)]
     parts = pl.pallas_call(
         products_kernel,
-        in_specs=[sspec(), sspec(), vspec(), vspec(), vspec()],
+        in_specs=[sspec(), sspec()] + [vspec() for _ in range(5)],
         out_specs=vspec(),
         out_shape=v32(slabs, members, mems * members),
         compiler_params=ROOM,
         name="products",
-    )(slab, taper_mask, near(first), near(white[0]), near(arrived[0]))
+    )(slab, taper_mask, near(obs_all), near(white[0]), *[near(x) for x in arrived])
     parts = lax.all_to_all(parts, "slab", 0, 0, tiled=True)
-    second = lax.all_to_all(second, "mem", 0, 0, tiled=True)
+    cell_state = lax.all_to_all(forecast.reshape(mems, tiles, members, LANES), "mem", 0, 0, tiled=True)
     own_rows = pl.pallas_call(
         summed_kernel,
         in_specs=[vspec()],
@@ -282,16 +289,18 @@
         compiler_params=ROOM,
         name="summed",
     )(near(parts))
-    ensemble = lax.all_gather(own_rows, "mem", axis=0, tiled=True, axis_index_groups=columns)
+    run = jnp.concatenate([own_rows] + [swapped(own_rows, "mem", k * PLANE) for k in range(1, RUN)], 0)
+    below, above = shifted(run, "mem", RUN * PLANE), shifted(run, "mem", -RUN * PLANE)
+    ensemble = jnp.concatenate([run, below, above], 0)
     ensemble = lax.all_gather(ensemble, "mem", axis=0, tiled=True, axis_index_groups=planes)
     update = pl.pallas_call(
         mixing_kernel,
-        in_specs=[vspec(), vspec(), vspec()],
+        in_specs=[sspec(), vspec(), vspec()],
         out_specs=vspec(),
         out_shape=v32(mems, tiles, members, LANES),
         compiler_params=ROOM,
         name="mixing",
-    )(near(first), near(second), near(ensemble))
+    )(z, near(cell_state), near(ensemble))
     returned = lax.all_to_all(update, "mem", 0, 0, tiled=True)
     steps = 4
     return pl.pallas_call(

time: 186 us -> 196 us (1.054)
  blocking collectives: 99.8 us -> 65.4 us
  starting transfers between devices: 51.5 us -> 80.2 us
  waiting for transfers between devices: 14.7 us -> 35.9 us
  Pallas kernels: 17.9 us -> 12.2 us
    all_gather x1 -> x0, blocking collectives: 28.6 us -> none  [local(): lax.all_gather(own_rows, 'mem', axis=0, tiled=True, axis_index_groups=col...]
    ppermute x4 -> x9, waiting for transfers between devices: 7.22 us -> 24.9 us  [swapped(): lax.ppermute(x, axis, [(i, i ^ k) for i in range(lax.axis_size(axis))])]
    ppermute x4 -> x9, starting transfers between devices: 17.6 us -> 31.5 us  [swapped(): lax.ppermute(x, axis, [(i, i ^ k) for i in range(lax.axis_size(axis))])]
    ppermute x0 -> x2, starting transfers between devices: none -> 10 us  [shifted(): return lax.ppermute(x, axis, [(i, (i + k) % count) for i in range(count)])]
    pallas_call x1, Pallas kernels: 12.2 us -> 5.35 us  [local(): pl.pallas_call(forecast_kernel, in_specs=[sspec() for _ in range(5)] + [v...]
    ppermute x0 -> x2, waiting for transfers between devices: none -> 5.79 us  [shifted(): return lax.ppermute(x, axis, [(i, (i + k) % count) for i in range(count)])]
    all_to_all x2, starting transfers between devices: 27.5 us -> 32.3 us  [the longest x1 17.3 us: local(): obs_all = lax.all_to_all(obs_copies, 'mem', 0, 0, tiled=True)]
    all_to_all x1, blocking collectives: 19 us -> 15.7 us  [local(): parts = lax.all_to_all(parts, 'slab', 0, 0, tiled=True)]
  transfers between devices with their start and end apart: 8 -> 15, of which waited for: 6 -> 6; matrix products, arithmetic and copies ran while one was open for 0% -> 0% of each run, Pallas kernels for 0% -> 0%
where the time goes in v5:
time: 196 us; the launch traced here: 195 us
  starting transfers between devices  80.2 us (41%)
  blocking collectives  65.4 us (33%)
  waiting for transfers between devices  35.9 us (18%)
  Pallas kernels  12.2 us (6%)
    all_to_all x1, blocking collectives, local(): returned = lax.all_to_all(update, 'mem', 0, 0, tiled=True)  39.9 us
    ppermute x9, starting transfers between devices, swapped(): lax.ppermute(x, axis, [(i, i ^ k) for i in range(lax.axis_size(axis))])  31.5 us
    ppermute x9, waiting for transfers between devices, swapped(): lax.ppermute(x, axis, [(i, i ^ k) for i in range(lax.axis_size(axis))])  24.9 us
    all_to_all x1, starting transfers between devices, local(): obs_all = lax.all_to_all(obs_copies, 'mem', 0, 0, tiled=True)  17.3 us
    all_to_all x1, blocking collectives, local(): parts = lax.all_to_all(parts, 'slab', 0, 0, tiled=True)  15.7 us
    all_to_all x1, starting transfers between devices, local(): lax.all_to_all(forecast.reshape(mems, tiles, members, LANES), 'mem', 0, 0...  15 us
    ppermute x2, starting transfers between devices, shifted(): return lax.ppermute(x, axis, [(i, (i + k) % count) for i in range(count)])  10 us
    all_gather x1, blocking collectives, local(): lax.all_gather(ensemble, 'mem', axis=0, tiled=True, axis_index_groups=pla...  9.82 us
  transfers between devices with their start and end apart: 15, of which 6 were waited for; matrix products, arithmetic and copies ran while one was open for 0% of the time, Pallas kernels for 0%

profile of v5, /device:TPU:1, one launch (start us, length us, event | category | flops | bytes accessed | tf_op | source)
XLA Modules:
  0.0 195.3 jit_solution(160987203166012731)
XLA Ops:
  1.1 5.0 %collective-permute-start = (f32[2,8,384]{2,1,0:T(8,128)S(1)}, f32[2,8,384]{2,1,0:T(8,128)S(1)}, u32[]{:S(2)}, u32[]{:S(2)}) collective-permute-start(f32[2,8,384]{2,1,0:T(8,128)S(1)} %get-tuple-element.17), channel_id=1, source_target_pairs={{0,1},{1,2},{2,3},{3,4},{4,5},{5,6},{6,7},{7,8},{8,9},{9,10},{10,1... | collective-permute-start | bytes 73736 | tf_op jit(solution)/shard_map/ppermute | solution.py:246
  8.1 5.2 %collective-permute-done.1.high_ref = f32[3,8,384]{2,1,0:T(8,128)S(1)} collective-permute-done((f32[3,8,384]{2,1,0:T(8,128)S(1)}, f32[3,8,384]{2,1,0:T(8,128)S(1)}, u32[]{:S(2)}, u32[]{:S(2)}) %collective-permute-start.1) | collective-permute-done | bytes 36896 | tf_op jit(solution)/shard_map/ppermute | solution.py:247
  14.0 5.3 %forecast.1 = (f32[192,8,128]{2,1,0:T(8,128)}, f32[48,8,128]{2,1,0:T(8,128)}, f32[4,8,128]{2,1,0:T(8,128)S(1)}, f32[4,8,128]{2,1,0:T(8,128)S(1)}, f32[4,8,128]{2,1,0:T(8,128)S(1)}, /*index=5*/f32[4,8,128]{2,1,0:T(8,128)S(1)}) custom-call(s32[1]{0:T(128)} %bitcast.slab_ref, s32[128]{0:T(128)S(1)} %get-tuple-element.32.spot0_ref, ...), custom_call_target="tpu_custom_call" | custom-call | tf_op jit(solution)/shard_map/forecast/pallas_call | solution.py:249
  19.3 17.3 %all-to-all-start.1 = ((f32[48,8,128]{2,1,0:T(8,128)}), f32[48,8,128]{2,1,0:T(8,128)S(1)}, u32[]{:S(2)}, u32[]{:S(2)}) async-start(f32[48,8,128]{2,1,0:T(8,128)} %get-tuple-element.20), calls=%async_computation.1 | async-start | bytes 393216 | tf_op jit(solution)/shard_map/all_to_all | solution.py:263
  36.6 3.1 %collective-permute-start.2 = (f32[4,8,128]{2,1,0:T(8,128)S(1)}, f32[4,8,128]{2,1,0:T(8,128)S(1)}, u32[]{:S(2)}, u32[]{:S(2)}) collective-permute-start(f32[4,8,128]{2,1,0:T(8,128)S(1)} %get-tuple-element.22), channel_id=1, source_target_pairs={{0,4},{1,5},{2,6},{3,7},{4,0},{5,1},{6,2},{7,3},{8,12},{9,13},{10,... | collective-permute-start | bytes 49160 | tf_op jit(solution)/shard_map/ppermute | solution.py:207
  39.8 3.7 %collective-permute-start.3 = (f32[4,8,128]{2,1,0:T(8,128)S(1)}, f32[4,8,128]{2,1,0:T(8,128)S(1)}, u32[]{:S(2)}, u32[]{:S(2)}) collective-permute-start(f32[4,8,128]{2,1,0:T(8,128)S(1)} %get-tuple-element.23), channel_id=1, source_target_pairs={{0,12},{1,13},{2,14},{3,15},{4,8},{5,9},{6,10},{7,11},{8,4},{9,5},... | collective-permute-start | bytes 49160 | tf_op jit(solution)/shard_map/ppermute | solution.py:207
  43.5 2.6 %collective-permute-start.4 = (f32[4,8,128]{2,1,0:T(8,128)S(1)}, f32[4,8,128]{2,1,0:T(8,128)S(1)}, u32[]{:S(2)}, u32[]{:S(2)}) collective-permute-start(f32[4,8,128]{2,1,0:T(8,128)S(1)} %get-tuple-element.24), channel_id=1, source_target_pairs={{0,8},{1,9},{2,10},{3,11},{4,12},{5,13},{6,14},{7,15},{8,0},{9,1},... | collective-permute-start | bytes 49160 | tf_op jit(solution)/shard_map/ppermute | solution.py:207
  46.1 3.7 %collective-permute-done.4.x3_ref = f32[4,8,128]{2,1,0:T(8,128)S(1)} collective-permute-done((f32[4,8,128]{2,1,0:T(8,128)S(1)}, f32[4,8,128]{2,1,0:T(8,128)S(1)}, u32[]{:S(2)}, u32[]{:S(2)}) %collective-permute-start.4) | collective-permute-done | bytes 16416 | tf_op jit(solution)/shard_map/ppermute | solution.py:207
  49.8 5.8 %collective-permute-start.5 = (f32[8,128]{1,0:T(8,128)S(1)}, f32[8,128]{1,0:T(8,128)S(1)}, u32[]{:S(2)}, u32[]{:S(2)}) collective-permute-start(f32[8,128]{1,0:T(8,128)S(1)} %get-tuple-element.26), channel_id=1, source_target_pairs={{0,1},{1,0},{2,3},{3,2},{4,5},{5,4},{6,7},{7,6},{8,9},{9,8},{10,11... | collective-permute-start | bytes 12296 | tf_op jit(solution)/shard_map/ppermute | solution.py:207
  57.6 5.1 %collective-permute-start.7 = (f32[8,128]{1,0:T(8,128)S(1)}, f32[8,128]{1,0:T(8,128)S(1)}, u32[]{:S(2)}, u32[]{:S(2)}) collective-permute-start(f32[8,128]{1,0:T(8,128)S(1)} %get-tuple-element.28), channel_id=1, source_target_pairs={{0,2},{1,3},{2,0},{3,1},{4,6},{5,7},{6,4},{7,5},{8,10},{9,11},{10,... | collective-permute-start | bytes 12296 | tf_op jit(solution)/shard_map/ppermute | solution.py:207
  62.7 3.1 %collective-permute-done.7.w3_ref = f32[8,128]{1,0:T(8,128)S(1)} collective-permute-done((f32[8,128]{1,0:T(8,128)S(1)}, f32[8,128]{1,0:T(8,128)S(1)}, u32[]{:S(2)}, u32[]{:S(2)}) %collective-permute-start.7) | collective-permute-done | bytes 4128 | tf_op jit(solution)/shard_map/ppermute | solution.py:207
  66.9 15.7 %all_to_all.20.x_ref = f32[16,8,384]{2,1,0:T(8,128)S(1)} all-to-all(f32[16,8,384]{2,1,0:T(8,128)S(1)} %products.1), channel_id=1, replica_groups=mesh['mem'=48,'slab'=16] {'slab'}, dimensions={0} | all-to-all | bytes 393216 | tf_op jit(solution)/shard_map/all_to_all | solution.py:282
  82.7 15.0 %all-to-all-start = ((f32[48,4,8,128]{3,2,1,0:T(8,128)}), f32[48,4,8,128]{3,2,1,0:T(8,128)S(1)}, u32[]{:S(2)}, u32[]{:S(2)}) async-start(f32[48,4,8,128]{3,2,1,0:T(8,128)} %bitcast.10), calls=%async_computation | async-start | bytes 1572864 | tf_op jit(solution)/shard_map/all_to_all | solution.py:283
  97.7 5.1 %collective-permute-start.10 = (f32[8,384]{1,0:T(8,128)S(1)}, f32[8,384]{1,0:T(8,128)S(1)}, u32[]{:S(2)}, u32[]{:S(2)}) collective-permute-start(f32[8,384]{1,0:T(8,128)S(1)} %summed.1), channel_id=1, source_target_pairs={{0,192},{16,208},{32,224},{48,240},{64,128},{80,144},{96,160},{112... | collective-permute-start | bytes 36872 | tf_op jit(solution)/shard_map/ppermute | solution.py:207
  104.7 2.3 %collective-permute-start.8 = (f32[8,384]{1,0:T(8,128)S(1)}, f32[8,384]{1,0:T(8,128)S(1)}, u32[]{:S(2)}, u32[]{:S(2)}) collective-permute-start(f32[8,384]{1,0:T(8,128)S(1)} %summed.1), channel_id=1, source_target_pairs={{0,64},{16,80},{32,96},{48,112},{64,0},{80,16},{96,32},{112,48},{1... | collective-permute-start | bytes 36872 | tf_op jit(solution)/shard_map/ppermute | solution.py:207
  107.0 15.2 %collective-permute-done.10 = f32[8,384]{1,0:T(8,128)S(1)} collective-permute-done((f32[8,384]{1,0:T(8,128)S(1)}, f32[8,384]{1,0:T(8,128)S(1)}, u32[]{:S(2)}, u32[]{:S(2)}) %collective-permute-start.10) | collective-permute-done | bytes 12320 | tf_op jit(solution)/shard_map/ppermute | solution.py:207
  122.2 2.9 %collective-permute-done.9 = f32[8,384]{1,0:T(8,128)S(1)} collective-permute-done((f32[8,384]{1,0:T(8,128)S(1)}, f32[8,384]{1,0:T(8,128)S(1)}, u32[]{:S(2)}, u32[]{:S(2)}) %collective-permute-start.9) | collective-permute-done | bytes 12320 | tf_op jit(solution)/shard_map/ppermute | solution.py:207
  125.1 7.0 %collective-permute-start.12 = (f32[32,384]{1,0:T(8,128)S(1)}, f32[32,384]{1,0:T(8,128)S(1)}, u32[]{:S(2)}, u32[]{:S(2)}) collective-permute-start(f32[32,384]{1,0:T(8,128)S(1)} %pad_maximum_fusion), channel_id=1, source_target_pairs={{0,512},{16,528},{32,544},{48,560},{64,576},{80,592},{96,608},{112... | collective-permute-start | bytes 147464 | tf_op jit(solution)/shard_map/ppermute | solution.py:212
  132.1 3.0 %collective-permute-start.11 = (f32[32,384]{1,0:T(8,128)S(1)}, f32[32,384]{1,0:T(8,128)S(1)}, u32[]{:S(2)}, u32[]{:S(2)}) collective-permute-start(f32[32,384]{1,0:T(8,128)S(1)} %pad_maximum_fusion), channel_id=1, source_target_pairs={{0,256},{16,272},{32,288},{48,304},{64,320},{80,336},{96,352},{112... | collective-permute-start | bytes 147464 | tf_op jit(solution)/shard_map/ppermute | solution.py:212
  135.1 5.8 %collective-permute-done.11 = f32[32,384]{1,0:T(8,128)S(1)} collective-permute-done((f32[32,384]{1,0:T(8,128)S(1)}, f32[32,384]{1,0:T(8,128)S(1)}, u32[]{:S(2)}, u32[]{:S(2)}) %collective-permute-start.11) | collective-permute-done | bytes 49184 | tf_op jit(solution)/shard_map/ppermute | solution.py:212
  140.9 9.8 %all_gather.3.e_ref = f32[384,384]{1,0:T(8,128)S(1)} all-gather(f32[96,384]{1,0:T(8,128)S(1)} %constant_dynamic-update-slice_fusion), channel_id=1, replica_groups={{0,16,32,48},{64,80,96,112},{128,144,160,176},{192,208,224,240},{256,27..., dimensions={0}, use_global_device_ids=true | all-gather | bytes 737280 | tf_op jit(solution)/shard_map/all_gather | solution.py:295
  150.8 2.1 %mixing.1 = f32[48,4,8,128]{3,2,1,0:T(8,128)S(1)} custom-call(s32[1]{0:T(128)} %bitcast.9.z_ref, f32[48,4,8,128]{3,2,1,0:T(8,128)S(1)} %all-to-all-done.x_ref, f32[384,384]{1,0:T(8,128)S(1)} %all_gather.3.e_ref), custom_call_target="tpu_custom_call" | custom-call | tf_op jit(solution)/shard_map/mixing/pallas_call | solution.py:296
  152.8 39.9 %all_to_all.21 = f32[48,4,8,128]{3,2,1,0:T(8,128)S(1)} all-to-all(f32[48,4,8,128]{3,2,1,0:T(8,128)S(1)} %mixing.1), channel_id=1, replica_groups=mesh['mem'=48,'slab'=16] {'mem'}, dimensions={0} | all-to-all | bytes 1572864 | tf_op jit(solution)/shard_map/all_to_all | solution.py:304
  192.7 2.7 %add.1 = f32[8,64,384]{2,1,0:T(8,128)} custom-call(f32[192,8,128]{2,1,0:T(8,128)} %get-tuple-element.19.f_ref, f32[192,8,128]{2,1,0:T(8,128)S(1)} %bitcast.24), custom_call_target="tpu_custom_call" | custom-call | tf_op jit(solution)/shard_map/add/pallas_call | solution.py:306
  (41 shorter events, 8.8 us)
Async XLA Ops:
  0.0 13.3 %copy-start = (f32[8,64,384]{2,1,0:T(8,128)S(1)}, f32[8,64,384]{2,1,0:T(8,128)}, u32[]{:S(2)}) copy-start(f32[8,64,384]{2,1,0:T(8,128)} %h_ref.1) | copy-start | bytes 2359300
  0.0 13.3 %copy-start.1 = (f32[64,384]{1,0:T(8,128)S(1)}, f32[64,384]{1,0:T(8,128)}, u32[]{:S(2)}) copy-start(f32[64,384]{1,0:T(8,128)} %v_ref.3) | copy-start | bytes 294916
  0.0 13.3 %copy-start.2 = (f32[64,384]{1,0:T(8,128)S(1)}, f32[64,384]{1,0:T(8,128)}, u32[]{:S(2)}) copy-start(f32[64,384]{1,0:T(8,128)} %u_ref.1) | copy-start | bytes 294916
  1.1 7.0 %collective-permute-start = (f32[2,8,384]{2,1,0:T(8,128)S(1)}, f32[2,8,384]{2,1,0:T(8,128)S(1)}, u32[]{:S(2)}, u32[]{:S(2)}) collective-permute-start(f32[2,8,384]{2,1,0:T(8,128)S(1)} %get-tuple-element.17), channel_id=1, source_target_pairs={{0,1},{1,2},{2,3},{3,4},{4,5},{5,6},{6,7},{7,8},{8,9},{9,10},{10,1... | collective-permute-start | bytes 73736 | tf_op jit(solution)/shard_map/ppermute | solution.py:246
  6.1 7.2 %collective-permute-start.1 = (f32[3,8,384]{2,1,0:T(8,128)S(1)}, f32[3,8,384]{2,1,0:T(8,128)S(1)}, u32[]{:S(2)}, u32[]{:S(2)}) collective-permute-start(f32[3,8,384]{2,1,0:T(8,128)S(1)} %get-tuple-element.18), channel_id=1, source_target_pairs={{1,0},{2,1},{3,2},{4,3},{5,4},{6,5},{7,6},{8,7},{9,8},{10,9},{11,1... | collective-permute-start | bytes 110600 | tf_op jit(solution)/shard_map/ppermute | solution.py:247
  7.4 0.7 copy-start.7
  13.3 0.7 copy-start.4
  13.3 0.7 copy-start.5
  13.3 0.7 copy-start.6
  19.3 46.5 %all-to-all-start.1 = ((f32[48,8,128]{2,1,0:T(8,128)}), f32[48,8,128]{2,1,0:T(8,128)S(1)}, u32[]{:S(2)}, u32[]{:S(2)}) async-start(f32[48,8,128]{2,1,0:T(8,128)} %get-tuple-element.20), calls=%async_computation.1 | async-start | bytes 393216 | tf_op jit(solution)/shard_map/all_to_all | solution.py:263
  36.6 9.4 %collective-permute-start.2 = (f32[4,8,128]{2,1,0:T(8,128)S(1)}, f32[4,8,128]{2,1,0:T(8,128)S(1)}, u32[]{:S(2)}, u32[]{:S(2)}) collective-permute-start(f32[4,8,128]{2,1,0:T(8,128)S(1)} %get-tuple-element.22), channel_id=1, source_target_pairs={{0,4},{1,5},{2,6},{3,7},{4,0},{5,1},{6,2},{7,3},{8,12},{9,13},{10,... | collective-permute-start | bytes 49160 | tf_op jit(solution)/shard_map/ppermute | solution.py:207
  39.8 6.3 %collective-permute-start.3 = (f32[4,8,128]{2,1,0:T(8,128)S(1)}, f32[4,8,128]{2,1,0:T(8,128)S(1)}, u32[]{:S(2)}, u32[]{:S(2)}) collective-permute-start(f32[4,8,128]{2,1,0:T(8,128)S(1)} %get-tuple-element.23), channel_id=1, source_target_pairs={{0,12},{1,13},{2,14},{3,15},{4,8},{5,9},{6,10},{7,11},{8,4},{9,5},... | collective-permute-start | bytes 49160 | tf_op jit(solution)/shard_map/ppermute | solution.py:207
  43.5 6.3 %collective-permute-start.4 = (f32[4,8,128]{2,1,0:T(8,128)S(1)}, f32[4,8,128]{2,1,0:T(8,128)S(1)}, u32[]{:S(2)}, u32[]{:S(2)}) collective-permute-start(f32[4,8,128]{2,1,0:T(8,128)S(1)} %get-tuple-element.24), channel_id=1, source_target_pairs={{0,8},{1,9},{2,10},{3,11},{4,12},{5,13},{6,14},{7,15},{8,0},{9,1},... | collective-permute-start | bytes 49160 | tf_op jit(solution)/shard_map/ppermute | solution.py:207
  49.8 16.1 %copy-start.3 = (s32[16,16]{1,0:T(8,128)S(1)}, s32[16,16]{1,0:T(8,128)}, u32[]{:S(2)}) copy-start(s32[16,16]{1,0:T(8,128)} %mask_ref.1) | copy-start | bytes 3076
  49.8 12.9 %collective-permute-start.5 = (f32[8,128]{1,0:T(8,128)S(1)}, f32[8,128]{1,0:T(8,128)S(1)}, u32[]{:S(2)}, u32[]{:S(2)}) collective-permute-start(f32[8,128]{1,0:T(8,128)S(1)} %get-tuple-element.26), channel_id=1, source_target_pairs={{0,1},{1,0},{2,3},{3,2},{4,5},{5,4},{6,7},{7,6},{8,9},{9,8},{10,11... | collective-permute-start | bytes 12296 | tf_op jit(solution)/shard_map/ppermute | solution.py:207
  55.6 7.1 %collective-permute-start.6 = (f32[8,128]{1,0:T(8,128)S(1)}, f32[8,128]{1,0:T(8,128)S(1)}, u32[]{:S(2)}, u32[]{:S(2)}) collective-permute-start(f32[8,128]{1,0:T(8,128)S(1)} %get-tuple-element.27), channel_id=1, source_target_pairs={{0,3},{1,2},{2,1},{3,0},{4,7},{5,6},{6,5},{7,4},{8,11},{9,10},{10,... | collective-permute-start | bytes 12296 | tf_op jit(solution)/shard_map/ppermute | solution.py:207
  57.6 8.3 %collective-permute-start.7 = (f32[8,128]{1,0:T(8,128)S(1)}, f32[8,128]{1,0:T(8,128)S(1)}, u32[]{:S(2)}, u32[]{:S(2)}) collective-permute-start(f32[8,128]{1,0:T(8,128)S(1)} %get-tuple-element.28), channel_id=1, source_target_pairs={{0,2},{1,3},{2,0},{3,1},{4,6},{5,7},{6,4},{7,5},{8,10},{9,11},{10,... | collective-permute-start | bytes 12296 | tf_op jit(solution)/shard_map/ppermute | solution.py:207
  82.7 68.1 %all-to-all-start = ((f32[48,4,8,128]{3,2,1,0:T(8,128)}), f32[48,4,8,128]{3,2,1,0:T(8,128)S(1)}, u32[]{:S(2)}, u32[]{:S(2)}) async-start(f32[48,4,8,128]{3,2,1,0:T(8,128)} %bitcast.10), calls=%async_computation | async-start | bytes 1572864 | tf_op jit(solution)/shard_map/all_to_all | solution.py:283
  97.7 24.5 %collective-permute-start.10 = (f32[8,384]{1,0:T(8,128)S(1)}, f32[8,384]{1,0:T(8,128)S(1)}, u32[]{:S(2)}, u32[]{:S(2)}) collective-permute-start(f32[8,384]{1,0:T(8,128)S(1)} %summed.1), channel_id=1, source_target_pairs={{0,192},{16,208},{32,224},{48,240},{64,128},{80,144},{96,160},{112... | collective-permute-start | bytes 36872 | tf_op jit(solution)/shard_map/ppermute | solution.py:207
  102.7 22.3 %collective-permute-start.9 = (f32[8,384]{1,0:T(8,128)S(1)}, f32[8,384]{1,0:T(8,128)S(1)}, u32[]{:S(2)}, u32[]{:S(2)}) collective-permute-start(f32[8,384]{1,0:T(8,128)S(1)} %summed.1), channel_id=1, source_target_pairs={{0,128},{16,144},{32,160},{48,176},{64,192},{80,208},{96,224},{112... | collective-permute-start | bytes 36872 | tf_op jit(solution)/shard_map/ppermute | solution.py:207
  104.7 20.4 %collective-permute-start.8 = (f32[8,384]{1,0:T(8,128)S(1)}, f32[8,384]{1,0:T(8,128)S(1)}, u32[]{:S(2)}, u32[]{:S(2)}) collective-permute-start(f32[8,384]{1,0:T(8,128)S(1)} %summed.1), channel_id=1, source_target_pairs={{0,64},{16,80},{32,96},{48,112},{64,0},{80,16},{96,32},{112,48},{1... | collective-permute-start | bytes 36872 | tf_op jit(solution)/shard_map/ppermute | solution.py:207
  125.1 15.8 %collective-permute-start.12 = (f32[32,384]{1,0:T(8,128)S(1)}, f32[32,384]{1,0:T(8,128)S(1)}, u32[]{:S(2)}, u32[]{:S(2)}) collective-permute-start(f32[32,384]{1,0:T(8,128)S(1)} %pad_maximum_fusion), channel_id=1, source_target_pairs={{0,512},{16,528},{32,544},{48,560},{64,576},{80,592},{96,608},{112... | collective-permute-start | bytes 147464 | tf_op jit(solution)/shard_map/ppermute | solution.py:212
  132.1 8.8 %collective-permute-start.11 = (f32[32,384]{1,0:T(8,128)S(1)}, f32[32,384]{1,0:T(8,128)S(1)}, u32[]{:S(2)}, u32[]{:S(2)}) collective-permute-start(f32[32,384]{1,0:T(8,128)S(1)} %pad_maximum_fusion), channel_id=1, source_target_pairs={{0,256},{16,272},{32,288},{48,304},{64,320},{80,336},{96,352},{112... | collective-permute-start | bytes 147464 | tf_op jit(solution)/shard_map/ppermute | solution.py:212

commit v6 on v4

--- a/solution.py
+++ b/solution.py
@@ -44,16 +44,16 @@
 def forecast_kernel(
     slab_ref, spot0_ref, spot1_ref, spot2_ref, spot3_ref, h_ref, low_ref, high_ref, u_ref, v_ref, weights_ref,
     values_ref, noise_ref, cov_hbm,
-    f_ref, first_ref, second_ref, near_ref, far_ref, white_ref, cov_ref, cov_sem,
+    f_ref, pieces_ref, near_ref, far_ref, stack_ref, cov_ref, cov_sem,
 ):
     cov_copy = pltpu.make_async_copy(cov_hbm, cov_ref, cov_sem)
     cov_copy.start()
     members = noise_ref.shape[0]
     rows, cols = u_ref.shape
     per_row = cols // LANES
-    mems, held = second_ref.shape[:2]
-    tiles = 2 * held
-    lane = lax.broadcasted_iota(jnp.int32, (members, cols), 1)
+    mems, tiles = pieces_ref.shape[0], pieces_ref.shape[1] - 1
+    batch = 8
+    lane = lax.broadcasted_iota(jnp.int32, (members * batch, cols), 1)
     at_first = lane == 0
     at_last = lane == cols - 1
 
@@ -94,15 +94,18 @@
         d_up2 = h_up2 - h_up
         half_up = 0.5 * minmod(d_up, d_up2)
         flux_up = row_flux(v, h, half, h_up, half_up)
-        f = h - columns_term(h, u_ref[r : r + 1, :]) - (flux_up - flux)
+        if r % batch == 0:
+            inside = range(r, r + batch)
+            term = columns_term(
+                jnp.concatenate([row(i) for i in inside], 0),
+                jnp.concatenate([jnp.broadcast_to(u_ref[i : i + 1, :], (members, cols)) for i in inside], 0),
+            )
+        f = h - term[r % batch * members : (r % batch + 1) * members] - (flux_up - flux)
         for t in range(per_row):
             at = r * per_row + t
             tile = f[:, t * LANES : (t + 1) * LANES]
             f_ref[at] = tile
-            if at % tiles < held:
-                first_ref[at // tiles, at % tiles] = tile
-            else:
-                second_ref[at // tiles, at % tiles - held] = tile
+            pieces_ref[at // tiles, at % tiles] = tile
         carry = (h_up, h_up2, d_up2, half_up, flux_up)
 
     spots = (spot0_ref, spot1_ref, spot2_ref, spot3_ref)
@@ -126,18 +129,17 @@
         obs = obs + picked[k] * weights[k : k + 1]
     obs = obs / jnp.sum(weights, axis=0, keepdims=True)
     for p in range(mems):
-        first_ref[p, held] = obs
+        pieces_ref[p, tiles] = obs
     innovation = values_ref[...] + noise_ref[...] - obs
     cov_copy.wait()
     white = jnp.dot(innovation, cov_ref[...], precision=HIGHEST, preferred_element_type=jnp.float32)
     order = swap_order(SLAB_SWAPS)
-    blocks = white_ref
     for s in range(len(order)):
-        blocks[s] = white[:, s * LANES : (s + 1) * LANES]
+        stack_ref[s] = white[:, s * LANES : (s + 1) * LANES]
     half = len(order) // 2
     for i, v in enumerate(order):
         ref, at = (near_ref, i) if i < half else (far_ref, i - half)
-        ref[at] = blocks[slab_ref[0] ^ v]
+        ref[at] = stack_ref[slab_ref[0] ^ v]
 
 
 def products_kernel(slab_ref, mask_ref, x_ref, white_ref, swap_ref, out_ref):
@@ -154,18 +156,17 @@
     e = x_ref[0]
     for s in range(1, x_ref.shape[0]):
         e = e + x_ref[s]
-    out_ref[...] = e
-
-
-def mixing_kernel(first_ref, second_ref, e_ref, out_ref):
+    for z in range(out_ref.shape[0]):
+        out_ref[z] = e
+
+
+def mixing_kernel(x_ref, e_ref, out_ref):
     mems, tiles, members, width = out_ref.shape
     total = mems * members
-    held = second_ref.shape[1]
     e = e_ref[...]
     depth = mems // PLANE
     for t in range(tiles):
-        x = first_ref[:, t] if t < held else second_ref[:, t - held]
-        x = x.reshape(total, width)
+        x = x_ref[:, t].reshape(total, width)
         x = x - jnp.mean(x, axis=0, keepdims=True)
         u = jnp.dot(e, x, precision=HIGHEST, preferred_element_type=jnp.float32) / (total - 1)
         for q in range(PLANE):
@@ -239,17 +240,12 @@
     low = lax.ppermute(down, "slab", [(i, i + 1) for i in range(slabs - 1)])
     high = lax.ppermute(up, "slab", [(i + 1, i) for i in range(slabs - 1)])
 
-    forecast, first, second, white, white_far = pl.pallas_call(
+    forecast, pieces, white, white_far = pl.pallas_call(
         forecast_kernel,
         in_specs=[sspec() for _ in range(5)] + [vspec() for _ in range(8)] + [pl.BlockSpec(memory_space=pltpu.HBM)],
-        out_specs=[vspec() for _ in range(5)],
-        out_shape=[
-            v32(mems * tiles, members, LANES),
-            v32(mems, tiles // 2 + 1, members, LANES),
-            v32(mems, tiles // 2, members, LANES),
-            v32(slabs // 2, members, LANES),
-            v32(slabs // 2, members, LANES),
-        ],
+        out_specs=[vspec() for _ in range(4)],
+        out_shape=[v32(mems * tiles, members, LANES), v32(mems, tiles + 1, members, LANES)]
+        + [v32(slabs // 2, members, LANES) for _ in range(2)],
         scratch_shapes=[v32(slabs, members, LANES), v32(*cov_inverse.shape), pltpu.SemaphoreType.DMA],
         compiler_params=ROOM,
         name="forecast",
@@ -258,7 +254,7 @@
         near(face_v), near(obs_weights.T), near(obs_values.reshape(1, -1)), near(obs_noise), away(cov_inverse),
     )
 
-    first = lax.all_to_all(first, "mem", 0, 0, tiled=True)
+    cell_state = lax.all_to_all(pieces, "mem", 0, 0, tiled=True)
     arrived = swapped(white_far, "slab", SLAB_SWAPS[-1])
     for k in SLAB_SWAPS[-2::-1]:
         half = white.shape[0] // 2
@@ -271,27 +267,28 @@
         out_shape=v32(slabs, members, mems * members),
         compiler_params=ROOM,
         name="products",
-    )(slab, taper_mask, near(first), near(white[0]), near(arrived[0]))
+    )(slab, taper_mask, near(cell_state), near(white[0]), near(arrived[0]))
     parts = lax.all_to_all(parts, "slab", 0, 0, tiled=True)
-    second = lax.all_to_all(second, "mem", 0, 0, tiled=True)
-    own_rows = pl.pallas_call(
+    copies = pl.pallas_call(
         summed_kernel,
         in_specs=[vspec()],
         out_specs=vspec(),
-        out_shape=v32(members, mems * members),
+        out_shape=v32(depth, members, mems * members),
         compiler_params=ROOM,
         name="summed",
     )(near(parts))
-    ensemble = lax.all_gather(own_rows, "mem", axis=0, tiled=True, axis_index_groups=columns)
-    ensemble = lax.all_gather(ensemble, "mem", axis=0, tiled=True, axis_index_groups=planes)
+    over_z = lax.all_to_all(copies, "mem", 0, 0, tiled=True, axis_index_groups=columns)
+    ensemble = lax.all_gather(
+        over_z.reshape(depth * members, mems * members), "mem", axis=0, tiled=True, axis_index_groups=planes
+    )
     update = pl.pallas_call(
         mixing_kernel,
-        in_specs=[vspec(), vspec(), vspec()],
+        in_specs=[vspec(), vspec()],
         out_specs=vspec(),
         out_shape=v32(mems, tiles, members, LANES),
         compiler_params=ROOM,
         name="mixing",
-    )(near(first), near(second), near(ensemble))
+    )(near(cell_state), near(ensemble))
     returned = lax.all_to_all(update, "mem", 0, 0, tiled=True)
     steps = 4
     return pl.pallas_call(

time: 186 us -> 162 us (0.87)
  blocking collectives: 99.8 us -> 80.6 us
  waiting for transfers between devices: 14.7 us -> 27 us
  starting transfers between devices: 51.5 us -> 41.3 us
  Pallas kernels: 17.9 us -> 11.1 us
    all_gather x2 -> x1, blocking collectives: 40.7 us -> 9.24 us  [local(): lax.all_gather(over_z.reshape(depth * members, mems * members), 'mem', ax...]
    all_to_all x0 -> x1, blocking collectives: none -> 14.3 us  [local(): lax.all_to_all(copies, 'mem', 0, 0, tiled=True, axis_index_groups=columns)]
    all_to_all x2 -> x1, waiting for transfers between devices: 2.28 us -> 14.6 us  [local(): cell_state = lax.all_to_all(pieces, 'mem', 0, 0, tiled=True)]
    all_to_all x2 -> x1, starting transfers between devices: 27.5 us -> 17.3 us  [local(): cell_state = lax.all_to_all(pieces, 'mem', 0, 0, tiled=True)]
    pallas_call x1, Pallas kernels: 12.2 us -> 5.4 us  [local(): pl.pallas_call(forecast_kernel, in_specs=[sspec() for _ in range(5)] + [v...]
    all_to_all x1, blocking collectives: 40 us -> 37.6 us  [local(): returned = lax.all_to_all(update, 'mem', 0, 0, tiled=True)]
  transfers between devices with their start and end apart: 8 -> 7, of which waited for: 6 -> 6; matrix products, arithmetic and copies ran while one was open for 0% -> 0% of each run, Pallas kernels for 0% -> 0%
where the time goes in v6:
time: 162 us; the launch traced here: 161 us
  blocking collectives  80.6 us (50%)
  starting transfers between devices  41.3 us (25%)
  waiting for transfers between devices  27 us (17%)
  Pallas kernels  11.1 us (7%)
    all_to_all x1, blocking collectives, local(): returned = lax.all_to_all(update, 'mem', 0, 0, tiled=True)  37.6 us
    all_to_all x1, blocking collectives, local(): parts = lax.all_to_all(parts, 'slab', 0, 0, tiled=True)  19.5 us
    ppermute x4, starting transfers between devices, swapped(): lax.ppermute(x, axis, [(i, i ^ k) for i in range(lax.axis_size(axis))])  17.6 us
    all_to_all x1, starting transfers between devices, local(): cell_state = lax.all_to_all(pieces, 'mem', 0, 0, tiled=True)  17.3 us
    all_to_all x1, waiting for transfers between devices, local(): cell_state = lax.all_to_all(pieces, 'mem', 0, 0, tiled=True)  14.6 us
    all_to_all x1, blocking collectives, local(): lax.all_to_all(copies, 'mem', 0, 0, tiled=True, axis_index_groups=columns)  14.3 us
    all_gather x1, blocking collectives, local(): lax.all_gather(over_z.reshape(depth * members, mems * members), 'mem', ax...  9.24 us
    ppermute x4, waiting for transfers between devices, swapped(): lax.ppermute(x, axis, [(i, i ^ k) for i in range(lax.axis_size(axis))])  7.23 us
  transfers between devices with their start and end apart: 7, of which 6 were waited for; matrix products, arithmetic and copies ran while one was open for 0% of the time, Pallas kernels for 0%

profile of v6, /device:TPU:1, one launch (start us, length us, event | category | flops | bytes accessed | tf_op | source)
XLA Modules:
  0.0 161.4 jit_solution(4605775385918792638)
XLA Ops:
  0.0 1.0 edges.1
  1.1 5.0 %collective-permute-start = (f32[2,8,384]{2,1,0:T(8,128)S(1)}, f32[2,8,384]{2,1,0:T(8,128)S(1)}, u32[]{:S(2)}, u32[]{:S(2)}) collective-permute-start(f32[2,8,384]{2,1,0:T(8,128)S(1)} %get-tuple-element.11), channel_id=1, source_target_pairs={{0,1},{1,2},{2,3},{3,4},{4,5},{5,6},{6,7},{7,8},{8,9},{9,10},{10,1... | collective-permute-start | bytes 73736 | tf_op jit(solution)/shard_map/ppermute | solution.py:240
  6.1 1.3 collective-permute-start.1
  7.4 0.7 copy-done.7
  8.1 5.2 %collective-permute-done.1.high_ref = f32[3,8,384]{2,1,0:T(8,128)S(1)} collective-permute-done((f32[3,8,384]{2,1,0:T(8,128)S(1)}, f32[3,8,384]{2,1,0:T(8,128)S(1)}, u32[]{:S(2)}, u32[]{:S(2)}) %collective-permute-start.1) | collective-permute-done | bytes 36896 | tf_op jit(solution)/shard_map/ppermute | solution.py:241
  13.3 0.7 copy-done.4
  14.0 5.4 %forecast.1 = (f32[192,8,128]{2,1,0:T(8,128)S(1)}, f32[48,5,8,128]{3,2,1,0:T(8,128)}, f32[8,8,128]{2,1,0:T(8,128)S(1)}, f32[8,8,128]{2,1,0:T(8,128)S(1)}) custom-call(s32[1]{0:T(128)} %bitcast.slab_ref, s32[128]{0:T(128)S(1)} %get-tuple-element.26.spot0_ref, s32[128]{0:T(128)S(1)} %get-tuple-element.25.spot1_ref, s32[128]{0:T(128)S(1)} %get-tuple-element.24.spot2_ref, ...), custom_call_target="tpu_custom_call" | custom-call | tf_op jit(solution)/shard_map/forecast/pallas_call | solution.py:243
  19.4 17.3 %all-to-all-start = ((f32[48,5,8,128]{3,2,1,0:T(8,128)}), f32[48,5,8,128]{3,2,1,0:T(8,128)S(1)}, u32[]{:S(2)}, u32[]{:S(2)}) async-start(f32[48,5,8,128]{3,2,1,0:T(8,128)} %get-tuple-element.14), calls=%async_computation | async-start | bytes 1966080 | tf_op jit(solution)/shard_map/all_to_all | solution.py:257
  36.7 4.4 %collective-permute-start.2 = (f32[8,8,128]{2,1,0:T(8,128)S(1)}, f32[8,8,128]{2,1,0:T(8,128)S(1)}, u32[]{:S(2)}, u32[]{:S(2)}) collective-permute-start(f32[8,8,128]{2,1,0:T(8,128)S(1)} %get-tuple-element.16), channel_id=1, source_target_pairs={{0,12},{1,13},{2,14},{3,15},{4,8},{5,9},{6,10},{7,11},{8,4},{9,5},... | collective-permute-start | bytes 98312 | tf_op jit(solution)/shard_map/ppermute | solution.py:206
  41.1 1.8 %collective-permute-done.2 = f32[8,8,128]{2,1,0:T(8,128)S(1)} collective-permute-done((f32[8,8,128]{2,1,0:T(8,128)S(1)}, f32[8,8,128]{2,1,0:T(8,128)S(1)}, u32[]{:S(2)}, u32[]{:S(2)}) %collective-permute-start.2) | collective-permute-done | bytes 32800 | tf_op jit(solution)/shard_map/ppermute | solution.py:206
  42.9 1.9 %collective-permute-start.3 = (f32[4,8,128]{2,1,0:T(8,128)S(1)}, f32[4,8,128]{2,1,0:T(8,128)S(1)}, u32[]{:S(2)}, u32[]{:S(2)}) collective-permute-start(f32[4,8,128]{2,1,0:T(8,128)S(1)} %get-tuple-element.18), channel_id=1, source_target_pairs={{0,4},{1,5},{2,6},{3,7},{4,0},{5,1},{6,2},{7,3},{8,12},{9,13},{10,... | collective-permute-start | bytes 49160 | tf_op jit(solution)/shard_map/ppermute | solution.py:206
  44.8 2.8 %collective-permute-done.3 = f32[4,8,128]{2,1,0:T(8,128)S(1)} collective-permute-done((f32[4,8,128]{2,1,0:T(8,128)S(1)}, f32[4,8,128]{2,1,0:T(8,128)S(1)}, u32[]{:S(2)}, u32[]{:S(2)}) %collective-permute-start.3) | collective-permute-done | bytes 16416 | tf_op jit(solution)/shard_map/ppermute | solution.py:206
  47.6 6.1 %collective-permute-start.4 = (f32[2,8,128]{2,1,0:T(8,128)S(1)}, f32[2,8,128]{2,1,0:T(8,128)S(1)}, u32[]{:S(2)}, u32[]{:S(2)}) collective-permute-start(f32[2,8,128]{2,1,0:T(8,128)S(1)} %get-tuple-element.20), channel_id=1, source_target_pairs={{0,3},{1,2},{2,1},{3,0},{4,7},{5,6},{6,5},{7,4},{8,11},{9,10},{10,... | collective-permute-start | bytes 24584 | tf_op jit(solution)/shard_map/ppermute | solution.py:206
  53.8 1.3 collective-permute-done.4
  55.1 5.2 %collective-permute-start.5 = (f32[1,8,128]{2,1,0:T(8,128)S(1)}, f32[1,8,128]{2,1,0:T(8,128)S(1)}, u32[]{:S(2)}, u32[]{:S(2)}) collective-permute-start(f32[1,8,128]{2,1,0:T(8,128)S(1)} %get-tuple-element.21), channel_id=1, source_target_pairs={{0,1},{1,0},{2,3},{3,2},{4,5},{5,4},{6,7},{7,6},{8,9},{9,8},{10,11... | collective-permute-start | bytes 12296 | tf_op jit(solution)/shard_map/ppermute | solution.py:206
  60.3 1.3 collective-permute-done.5
  61.6 14.6 %all-to-all-done.x_ref = f32[48,5,8,128]{3,2,1,0:T(8,128)S(1)} async-done(((f32[48,5,8,128]{3,2,1,0:T(8,128)}), f32[48,5,8,128]{3,2,1,0:T(8,128)S(1)}, u32[]{:S(2)}, u32[]{:S(2)}) %all-to-all-start) | async-done | bytes 983072 | tf_op jit(solution)/shard_map/all_to_all | solution.py:257
  76.2 1.1 products.1
  77.2 19.5 %all_to_all.20.x_ref = f32[16,8,384]{2,1,0:T(8,128)S(1)} all-to-all(f32[16,8,384]{2,1,0:T(8,128)S(1)} %products.1), channel_id=1, replica_groups=mesh['mem'=48,'slab'=16] {'slab'}, dimensions={0} | all-to-all | bytes 393216 | tf_op jit(solution)/shard_map/all_to_all | solution.py:271
  96.8 14.3 %all_to_all.21 = f32[12,8,384]{2,1,0:T(8,128)S(1)} all-to-all(f32[12,8,384]{2,1,0:T(8,128)S(1)} %summed.1), channel_id=1, replica_groups={{0,64,128,192,256,320,384,448,512,576,640,704},{16,80,144,208,272,336,4..., dimensions={0} | all-to-all | bytes 294912 | tf_op jit(solution)/shard_map/all_to_all | solution.py:280
  111.0 9.2 %all_gather.3.e_ref = f32[384,384]{1,0:T(8,128)S(1)} all-gather(f32[96,384]{1,0:T(8,128)S(1)} %bitcast.30), channel_id=1, replica_groups={{0,16,32,48},{64,80,96,112},{128,144,160,176},{192,208,224,240},{256,27..., dimensions={0}, use_global_device_ids=true | all-gather | bytes 737280 | tf_op jit(solution)/shard_map/all_gather | solution.py:281
  120.3 2.1 %mixing.1 = f32[48,4,8,128]{3,2,1,0:T(8,128)S(1)} custom-call(f32[48,5,8,128]{3,2,1,0:T(8,128)S(1)} %all-to-all-done.x_ref, f32[384,384]{1,0:T(8,128)S(1)} %all_gather.3.e_ref), custom_call_target="tpu_custom_call" | custom-call | tf_op jit(solution)/shard_map/mixing/pallas_call | solution.py:284
  122.4 37.6 %all_to_all.22 = f32[48,4,8,128]{3,2,1,0:T(8,128)S(1)} all-to-all(f32[48,4,8,128]{3,2,1,0:T(8,128)S(1)} %mixing.1), channel_id=1, replica_groups=mesh['mem'=48,'slab'=16] {'mem'}, dimensions={0} | all-to-all | bytes 1572864 | tf_op jit(solution)/shard_map/all_to_all | solution.py:292
  159.9 1.5 add.33
  (21 shorter events, 0.1 us)
Async XLA Ops:
  0.0 13.3 %copy-start = (f32[8,64,384]{2,1,0:T(8,128)S(1)}, f32[8,64,384]{2,1,0:T(8,128)}, u32[]{:S(2)}) copy-start(f32[8,64,384]{2,1,0:T(8,128)} %h_ref.1) | copy-start | bytes 2359300
  0.0 13.3 %copy-start.1 = (f32[64,384]{1,0:T(8,128)S(1)}, f32[64,384]{1,0:T(8,128)}, u32[]{:S(2)}) copy-start(f32[64,384]{1,0:T(8,128)} %v_ref.3) | copy-start | bytes 294916
  0.0 13.3 %copy-start.2 = (f32[64,384]{1,0:T(8,128)S(1)}, f32[64,384]{1,0:T(8,128)}, u32[]{:S(2)}) copy-start(f32[64,384]{1,0:T(8,128)} %u_ref.1) | copy-start | bytes 294916
  1.1 7.0 %collective-permute-start = (f32[2,8,384]{2,1,0:T(8,128)S(1)}, f32[2,8,384]{2,1,0:T(8,128)S(1)}, u32[]{:S(2)}, u32[]{:S(2)}) collective-permute-start(f32[2,8,384]{2,1,0:T(8,128)S(1)} %get-tuple-element.11), channel_id=1, source_target_pairs={{0,1},{1,2},{2,3},{3,4},{4,5},{5,6},{6,7},{7,8},{8,9},{9,10},{10,1... | collective-permute-start | bytes 73736 | tf_op jit(solution)/shard_map/ppermute | solution.py:240
  6.1 7.2 %collective-permute-start.1 = (f32[3,8,384]{2,1,0:T(8,128)S(1)}, f32[3,8,384]{2,1,0:T(8,128)S(1)}, u32[]{:S(2)}, u32[]{:S(2)}) collective-permute-start(f32[3,8,384]{2,1,0:T(8,128)S(1)} %get-tuple-element.12), channel_id=1, source_target_pairs={{1,0},{2,1},{3,2},{4,3},{5,4},{6,5},{7,6},{8,7},{9,8},{10,9},{11,1... | collective-permute-start | bytes 110600 | tf_op jit(solution)/shard_map/ppermute | solution.py:241
  7.4 0.7 copy-start.7
  13.3 0.7 copy-start.4
  13.3 0.7 copy-start.5
  13.3 0.7 copy-start.6
  19.4 56.8 %all-to-all-start = ((f32[48,5,8,128]{3,2,1,0:T(8,128)}), f32[48,5,8,128]{3,2,1,0:T(8,128)S(1)}, u32[]{:S(2)}, u32[]{:S(2)}) async-start(f32[48,5,8,128]{3,2,1,0:T(8,128)} %get-tuple-element.14), calls=%async_computation | async-start | bytes 1966080 | tf_op jit(solution)/shard_map/all_to_all | solution.py:257
  36.7 6.2 %collective-permute-start.2 = (f32[8,8,128]{2,1,0:T(8,128)S(1)}, f32[8,8,128]{2,1,0:T(8,128)S(1)}, u32[]{:S(2)}, u32[]{:S(2)}) collective-permute-start(f32[8,8,128]{2,1,0:T(8,128)S(1)} %get-tuple-element.16), channel_id=1, source_target_pairs={{0,12},{1,13},{2,14},{3,15},{4,8},{5,9},{6,10},{7,11},{8,4},{9,5},... | collective-permute-start | bytes 98312 | tf_op jit(solution)/shard_map/ppermute | solution.py:206
  42.9 4.8 %collective-permute-start.3 = (f32[4,8,128]{2,1,0:T(8,128)S(1)}, f32[4,8,128]{2,1,0:T(8,128)S(1)}, u32[]{:S(2)}, u32[]{:S(2)}) collective-permute-start(f32[4,8,128]{2,1,0:T(8,128)S(1)} %get-tuple-element.18), channel_id=1, source_target_pairs={{0,4},{1,5},{2,6},{3,7},{4,0},{5,1},{6,2},{7,3},{8,12},{9,13},{10,... | collective-permute-start | bytes 49160 | tf_op jit(solution)/shard_map/ppermute | solution.py:206
  47.6 7.5 %collective-permute-start.4 = (f32[2,8,128]{2,1,0:T(8,128)S(1)}, f32[2,8,128]{2,1,0:T(8,128)S(1)}, u32[]{:S(2)}, u32[]{:S(2)}) collective-permute-start(f32[2,8,128]{2,1,0:T(8,128)S(1)} %get-tuple-element.20), channel_id=1, source_target_pairs={{0,3},{1,2},{2,1},{3,0},{4,7},{5,6},{6,5},{7,4},{8,11},{9,10},{10,... | collective-permute-start | bytes 24584 | tf_op jit(solution)/shard_map/ppermute | solution.py:206
  55.1 21.1 %copy-start.3 = (s32[16,16]{1,0:T(8,128)S(1)}, s32[16,16]{1,0:T(8,128)}, u32[]{:S(2)}) copy-start(s32[16,16]{1,0:T(8,128)} %mask_ref.1) | copy-start | bytes 3076
  55.1 6.5 %collective-permute-start.5 = (f32[1,8,128]{2,1,0:T(8,128)S(1)}, f32[1,8,128]{2,1,0:T(8,128)S(1)}, u32[]{:S(2)}, u32[]{:S(2)}) collective-permute-start(f32[1,8,128]{2,1,0:T(8,128)S(1)} %get-tuple-element.21), channel_id=1, source_target_pairs={{0,1},{1,0},{2,3},{3,2},{4,5},{5,4},{6,7},{7,6},{8,9},{9,8},{10,11... | collective-permute-start | bytes 12296 | tf_op jit(solution)/shard_map/ppermute | solution.py:206

commit v7 on v6

--- a/solution.py
+++ b/solution.py
@@ -41,22 +41,17 @@
     up_ref[2] = jnp.broadcast_to(v_ref[0:1, :], up_ref.shape[1:])
 
 
-def forecast_kernel(
-    slab_ref, spot0_ref, spot1_ref, spot2_ref, spot3_ref, h_ref, low_ref, high_ref, u_ref, v_ref, weights_ref,
-    values_ref, noise_ref, cov_hbm,
-    f_ref, pieces_ref, near_ref, far_ref, stack_ref, cov_ref, cov_sem,
-):
-    cov_copy = pltpu.make_async_copy(cov_hbm, cov_ref, cov_sem)
-    cov_copy.start()
-    members = noise_ref.shape[0]
-    rows, cols = u_ref.shape
+def row_flux(v, h_low, half_low, h_high, half_high):
+    return jnp.maximum(v, 0.0) * (h_low + half_low) + jnp.minimum(v, 0.0) * (h_high - half_high)
+
+
+def inner_kernel(h_ref, u_ref, v_ref, f_ref, rim_ref):
+    members, rows, cols = h_ref.shape
     per_row = cols // LANES
-    mems, tiles = pieces_ref.shape[0], pieces_ref.shape[1] - 1
     batch = 8
     lane = lax.broadcasted_iota(jnp.int32, (members * batch, cols), 1)
     at_first = lane == 0
     at_last = lane == cols - 1
-
     blocks = {}
 
     def row(r):
@@ -74,39 +69,68 @@
         flux_next = jnp.where(at_last, 0.0, pltpu.roll(flux, cols - 1, 1))
         return flux_next - flux
 
-    def row_flux(v, h_low, half_low, h_high, half_high):
-        return jnp.maximum(v, 0.0) * (h_low + half_low) + jnp.minimum(v, 0.0) * (h_high - half_high)
-
-    low2, low1 = low_ref[0], low_ref[1]
-    h0, h1 = row(0), row(1)
-    d0, d1 = h0 - low1, h1 - h0
-    half_low = 0.5 * minmod(low1 - low2, d0)
-    half0 = 0.5 * minmod(d0, d1)
-    flux0 = row_flux(v_ref[0:1, :], low1, half_low, h0, half0)
-    carry = (h0, h1, d1, half0, flux0)
+    h, h_up = row(2), row(3)
+    d_up = h_up - h
+    half1 = 0.5 * minmod(row(1) - row(0), h - row(1))
+    half = 0.5 * minmod(h - row(1), d_up)
+    carry = (h, h_up, d_up, half, row_flux(v_ref[2:3, :], row(1), half1, h, half))
     for r in range(rows):
-        h, h_up, d_up, half, flux = carry
-        if r + 2 < rows:
-            h_up2 = row(r + 2)
-        else:
-            h_up2 = high_ref[r + 2 - rows]
-        v = v_ref[r + 1 : r + 2, :] if r + 1 < rows else high_ref[2, 0:1, :]
-        d_up2 = h_up2 - h_up
-        half_up = 0.5 * minmod(d_up, d_up2)
-        flux_up = row_flux(v, h, half, h_up, half_up)
         if r % batch == 0:
             inside = range(r, r + batch)
             term = columns_term(
                 jnp.concatenate([row(i) for i in inside], 0),
                 jnp.concatenate([jnp.broadcast_to(u_ref[i : i + 1, :], (members, cols)) for i in inside], 0),
             )
-        f = h - term[r % batch * members : (r % batch + 1) * members] - (flux_up - flux)
+        f = row(r) - term[r % batch * members : (r % batch + 1) * members]
+        if 2 <= r < rows - 2:
+            h, h_up, d_up, half, flux = carry
+            h_up2 = row(r + 2)
+            d_up2 = h_up2 - h_up
+            half_up = 0.5 * minmod(d_up, d_up2)
+            flux_up = row_flux(v_ref[r + 1 : r + 2, :], h, half, h_up, half_up)
+            f = f - (flux_up - flux)
+            carry = (h_up, h_up2, d_up2, half_up, flux_up)
+        for t in range(per_row):
+            f_ref[r * per_row + t] = f[:, t * LANES : (t + 1) * LANES]
+    for i in range(4):
+        rim_ref[i] = row(i)
+        rim_ref[4 + i] = row(rows - 4 + i)
+
+
+def forecast_kernel(
+    slab_ref, spot0_ref, spot1_ref, spot2_ref, spot3_ref, inner_ref, rim_ref, low_ref, high_ref, v_ref, weights_ref,
+    values_ref, noise_ref, cov_hbm,
+    f_ref, pieces_ref, near_ref, far_ref, stack_ref, cov_ref, cov_sem,
+):
+    cov_copy = pltpu.make_async_copy(cov_hbm, cov_ref, cov_sem)
+    cov_copy.start()
+    members = noise_ref.shape[0]
+    rows, cols = v_ref.shape
+    per_row = cols // LANES
+    mems, tiles = pieces_ref.shape[0], pieces_ref.shape[1] - 1
+
+    def edge_terms(h, v):
+        half = [0.5 * minmod(h[i] - h[i - 1], h[i + 1] - h[i]) for i in range(1, 5)]
+        flux = [row_flux(v[i], h[i + 1], half[i], h[i + 2], half[i + 1]) for i in range(3)]
+        return flux[1] - flux[0], flux[2] - flux[1]
+
+    lows = edge_terms(
+        [low_ref[0], low_ref[1], rim_ref[0], rim_ref[1], rim_ref[2], rim_ref[3]],
+        [v_ref[i : i + 1, :] for i in range(3)],
+    )
+    highs = edge_terms(
+        [rim_ref[4], rim_ref[5], rim_ref[6], rim_ref[7], high_ref[0], high_ref[1]],
+        [v_ref[rows - 2 : rows - 1, :], v_ref[rows - 1 : rows, :], high_ref[2, 0:1, :]],
+    )
+    late = {0: lows[0], 1: lows[1], rows - 2: highs[0], rows - 1: highs[1]}
+    for r in range(rows):
         for t in range(per_row):
             at = r * per_row + t
-            tile = f[:, t * LANES : (t + 1) * LANES]
+            tile = inner_ref[at]
+            if r in late:
+                tile = tile - late[r][:, t * LANES : (t + 1) * LANES]
             f_ref[at] = tile
             pieces_ref[at // tiles, at % tiles] = tile
-        carry = (h_up, h_up2, d_up2, half_up, flux_up)
 
     spots = (spot0_ref, spot1_ref, spot2_ref, spot3_ref)
     foot, count = weights_ref.shape
@@ -160,15 +184,25 @@
         out_ref[z] = e
 
 
+def two_parts(x):
+    high = x.astype(jnp.bfloat16)
+    return high, (x - high.astype(jnp.float32)).astype(jnp.bfloat16)
+
+
+def product(a, b):
+    return jnp.dot(a, b, preferred_element_type=jnp.float32)
+
+
 def mixing_kernel(x_ref, e_ref, out_ref):
     mems, tiles, members, width = out_ref.shape
     total = mems * members
-    e = e_ref[...]
+    e_high, e_low = two_parts(e_ref[...])
     depth = mems // PLANE
     for t in range(tiles):
         x = x_ref[:, t].reshape(total, width)
-        x = x - jnp.mean(x, axis=0, keepdims=True)
-        u = jnp.dot(e, x, precision=HIGHEST, preferred_element_type=jnp.float32) / (total - 1)
+        x_high, x_low = two_parts(x - jnp.mean(x, axis=0, keepdims=True))
+        u = product(e_high, x_high) + (product(e_high, x_low) + product(e_low, x_high))
+        u = u / (total - 1)
         for q in range(PLANE):
             for z in range(depth):
                 at = (q * depth + z) * members
@@ -239,6 +273,15 @@
     )(away(thickness), away(thickness), away(face_v))
     low = lax.ppermute(down, "slab", [(i, i + 1) for i in range(slabs - 1)])
     high = lax.ppermute(up, "slab", [(i + 1, i) for i in range(slabs - 1)])
+    speed = near(face_v)
+    inner, rim = pl.pallas_call(
+        inner_kernel,
+        in_specs=[vspec() for _ in range(3)],
+        out_specs=[vspec() for _ in range(2)],
+        out_shape=[v32(mems * tiles, members, LANES), v32(8, members, cols)],
+        compiler_params=ROOM,
+        name="inner",
+    )(near(thickness), near(face_u), speed)
 
     forecast, pieces, white, white_far = pl.pallas_call(
         forecast_kernel,
@@ -250,8 +293,8 @@
         compiler_params=ROOM,
         name="forecast",
     )(
-        slab, spots[0], spots[1], spots[2], spots[3], near(thickness), near(low), near(high), near(face_u),
-        near(face_v), near(obs_weights.T), near(obs_values.reshape(1, -1)), near(obs_noise), away(cov_inverse),
+        slab, spots[0], spots[1], spots[2], spots[3], near(inner), near(rim), near(low), near(high), speed,
+        near(obs_weights.T), near(obs_values.reshape(1, -1)), near(obs_noise), away(cov_inverse),
     )
 
     cell_state = lax.all_to_all(pieces, "mem", 0, 0, tiled=True)

time: 162 us -> 159 us (0.981)
  waiting for transfers between devices: 27 us -> 24.8 us
    ppermute x1, waiting for transfers between devices: 5.15 us -> 3.11 us  [local(): high = lax.ppermute(up, 'slab', [(i + 1, i) for i in range(slabs - 1)])]
    pallas_call x0 -> x1, Pallas kernels: none -> 2.01 us  [local(): pl.pallas_call(inner_kernel, in_specs=[vspec() for _ in range(3)], out_sp...]
    pallas_call x1, Pallas kernels: 5.4 us -> 3.47 us  [local(): pl.pallas_call(forecast_kernel, in_specs=[sspec() for _ in range(5)] + [v...]
  transfers between devices with their start and end apart: 7 -> 7, of which waited for: 6 -> 6; matrix products, arithmetic and copies ran while one was open for 0% -> 0% of each run, Pallas kernels for 0% -> 1%
where the time goes in v7:
time: 159 us
  blocking collectives  80.6 us (51%)
  starting transfers between devices  41.4 us (26%)
  waiting for transfers between devices  24.8 us (16%)
  Pallas kernels  10.3 us (6%)
    all_to_all x1, blocking collectives, local(): returned = lax.all_to_all(update, 'mem', 0, 0, tiled=True)  37.6 us
    all_to_all x1, blocking collectives, local(): parts = lax.all_to_all(parts, 'slab', 0, 0, tiled=True)  19.5 us
    ppermute x4, starting transfers between devices, swapped(): lax.ppermute(x, axis, [(i, i ^ k) for i in range(lax.axis_size(axis))])  17.7 us
    all_to_all x1, starting transfers between devices, local(): cell_state = lax.all_to_all(pieces, 'mem', 0, 0, tiled=True)  17.3 us
    all_to_all x1, waiting for transfers between devices, local(): cell_state = lax.all_to_all(pieces, 'mem', 0, 0, tiled=True)  14.6 us
    all_to_all x1, blocking collectives, local(): lax.all_to_all(copies, 'mem', 0, 0, tiled=True, axis_index_groups=columns)  14.3 us
    all_gather x1, blocking collectives, local(): lax.all_gather(over_z.reshape(depth * members, mems * members), 'mem', ax...  9.24 us
    ppermute x4, waiting for transfers between devices, swapped(): lax.ppermute(x, axis, [(i, i ^ k) for i in range(lax.axis_size(axis))])  7.13 us
  transfers between devices with their start and end apart: 7, of which 6 were waited for; matrix products, arithmetic and copies ran while one was open for 0% of the time, Pallas kernels for 1%

profile of v7, /device:TPU:1, one launch (start us, length us, event | category | flops | bytes accessed | tf_op | source)
XLA Modules:
  0.0 158.6 jit_solution(15946973420541019387)
XLA Ops:
  0.0 1.0 edges.1
  1.1 5.0 %collective-permute-start = (f32[2,8,384]{2,1,0:T(8,128)S(1)}, f32[2,8,384]{2,1,0:T(8,128)S(1)}, u32[]{:S(2)}, u32[]{:S(2)}) collective-permute-start(f32[2,8,384]{2,1,0:T(8,128)S(1)} %get-tuple-element.15), channel_id=1, source_target_pairs={{0,1},{1,2},{2,3},{3,4},{4,5},{5,6},{6,7},{7,8},{8,9},{9,10},{10,1... | collective-permute-start | bytes 73736 | tf_op jit(solution)/shard_map/ppermute | solution.py:274
  6.1 1.3 collective-permute-start.1
  8.1 2.0 %inner.1 = (f32[192,8,128]{2,1,0:T(8,128)S(1)}, f32[8,8,384]{2,1,0:T(8,128)S(1)}) custom-call(f32[8,64,384]{2,1,0:T(8,128)S(1)} %copy-done, f32[64,384]{1,0:T(8,128)S(1)} %copy-done.2, f32[64,384]{1,0:T(8,128)S(1)} %copy-done.1), custom_call_target="tpu_custom_call" | custom-call | tf_op jit(solution)/shard_map/inner/pallas_call | solution.py:277
  10.2 3.1 %collective-permute-done.1.high_ref = f32[3,8,384]{2,1,0:T(8,128)S(1)} collective-permute-done((f32[3,8,384]{2,1,0:T(8,128)S(1)}, f32[3,8,384]{2,1,0:T(8,128)S(1)}, u32[]{:S(2)}, u32[]{:S(2)}) %collective-permute-start.1) | collective-permute-done | bytes 36896 | tf_op jit(solution)/shard_map/ppermute | solution.py:275
  13.3 0.7 copy-done.4
  14.0 3.5 %forecast.1 = (f32[192,8,128]{2,1,0:T(8,128)S(1)}, f32[48,5,8,128]{3,2,1,0:T(8,128)}, f32[8,8,128]{2,1,0:T(8,128)S(1)}, f32[8,8,128]{2,1,0:T(8,128)S(1)}) custom-call(s32[1]{0:T(128)} %bitcast.slab_ref, s32[128]{0:T(128)S(1)} %get-tuple-element.30.spot0_ref, s32[128]{0:T(128)S(1)} %get-tuple-element.29.spot1_ref, s32[128]{0:T(128)S(1)} %get-tuple-element.28.spot2_ref, ...), custom_call_target="tpu_custom_call" | custom-call | tf_op jit(solution)/shard_map/forecast/pallas_call | solution.py:286
  17.4 17.3 %all-to-all-start = ((f32[48,5,8,128]{3,2,1,0:T(8,128)}), f32[48,5,8,128]{3,2,1,0:T(8,128)S(1)}, u32[]{:S(2)}, u32[]{:S(2)}) async-start(f32[48,5,8,128]{3,2,1,0:T(8,128)} %get-tuple-element.18), calls=%async_computation | async-start | bytes 1966080 | tf_op jit(solution)/shard_map/all_to_all | solution.py:300
  34.8 4.5 %collective-permute-start.2 = (f32[8,8,128]{2,1,0:T(8,128)S(1)}, f32[8,8,128]{2,1,0:T(8,128)S(1)}, u32[]{:S(2)}, u32[]{:S(2)}) collective-permute-start(f32[8,8,128]{2,1,0:T(8,128)S(1)} %get-tuple-element.20), channel_id=1, source_target_pairs={{0,12},{1,13},{2,14},{3,15},{4,8},{5,9},{6,10},{7,11},{8,4},{9,5},... | collective-permute-start | bytes 98312 | tf_op jit(solution)/shard_map/ppermute | solution.py:240
  39.3 1.7 %collective-permute-done.2 = f32[8,8,128]{2,1,0:T(8,128)S(1)} collective-permute-done((f32[8,8,128]{2,1,0:T(8,128)S(1)}, f32[8,8,128]{2,1,0:T(8,128)S(1)}, u32[]{:S(2)}, u32[]{:S(2)}) %collective-permute-start.2) | collective-permute-done | bytes 32800 | tf_op jit(solution)/shard_map/ppermute | solution.py:240
  40.9 1.9 %collective-permute-start.3 = (f32[4,8,128]{2,1,0:T(8,128)S(1)}, f32[4,8,128]{2,1,0:T(8,128)S(1)}, u32[]{:S(2)}, u32[]{:S(2)}) collective-permute-start(f32[4,8,128]{2,1,0:T(8,128)S(1)} %get-tuple-element.22), channel_id=1, source_target_pairs={{0,4},{1,5},{2,6},{3,7},{4,0},{5,1},{6,2},{7,3},{8,12},{9,13},{10,... | collective-permute-start | bytes 49160 | tf_op jit(solution)/shard_map/ppermute | solution.py:240
  42.9 2.8 %collective-permute-done.3 = f32[4,8,128]{2,1,0:T(8,128)S(1)} collective-permute-done((f32[4,8,128]{2,1,0:T(8,128)S(1)}, f32[4,8,128]{2,1,0:T(8,128)S(1)}, u32[]{:S(2)}, u32[]{:S(2)}) %collective-permute-start.3) | collective-permute-done | bytes 16416 | tf_op jit(solution)/shard_map/ppermute | solution.py:240
  45.7 6.1 %collective-permute-start.4 = (f32[2,8,128]{2,1,0:T(8,128)S(1)}, f32[2,8,128]{2,1,0:T(8,128)S(1)}, u32[]{:S(2)}, u32[]{:S(2)}) collective-permute-start(f32[2,8,128]{2,1,0:T(8,128)S(1)} %get-tuple-element.24), channel_id=1, source_target_pairs={{0,3},{1,2},{2,1},{3,0},{4,7},{5,6},{6,5},{7,4},{8,11},{9,10},{10,... | collective-permute-start | bytes 24584 | tf_op jit(solution)/shard_map/ppermute | solution.py:240
  51.8 1.3 collective-permute-done.4
  53.2 5.2 %collective-permute-start.5 = (f32[1,8,128]{2,1,0:T(8,128)S(1)}, f32[1,8,128]{2,1,0:T(8,128)S(1)}, u32[]{:S(2)}, u32[]{:S(2)}) collective-permute-start(f32[1,8,128]{2,1,0:T(8,128)S(1)} %get-tuple-element.25), channel_id=1, source_target_pairs={{0,1},{1,0},{2,3},{3,2},{4,5},{5,4},{6,7},{7,6},{8,9},{9,8},{10,11... | collective-permute-start | bytes 12296 | tf_op jit(solution)/shard_map/ppermute | solution.py:240
  58.4 1.3 collective-permute-done.5
  59.7 14.6 %all-to-all-done.x_ref = f32[48,5,8,128]{3,2,1,0:T(8,128)S(1)} async-done(((f32[48,5,8,128]{3,2,1,0:T(8,128)}), f32[48,5,8,128]{3,2,1,0:T(8,128)S(1)}, u32[]{:S(2)}, u32[]{:S(2)}) %all-to-all-start) | async-done | bytes 983072 | tf_op jit(solution)/shard_map/all_to_all | solution.py:300
  74.3 1.1 products.1
  75.3 19.5 %all_to_all.20.x_ref = f32[16,8,384]{2,1,0:T(8,128)S(1)} all-to-all(f32[16,8,384]{2,1,0:T(8,128)S(1)} %products.1), channel_id=1, replica_groups=mesh['mem'=48,'slab'=16] {'slab'}, dimensions={0} | all-to-all | bytes 393216 | tf_op jit(solution)/shard_map/all_to_all | solution.py:314
  94.8 14.3 %all_to_all.21 = f32[12,8,384]{2,1,0:T(8,128)S(1)} all-to-all(f32[12,8,384]{2,1,0:T(8,128)S(1)} %summed.1), channel_id=1, replica_groups={{0,64,128,192,256,320,384,448,512,576,640,704},{16,80,144,208,272,336,4..., dimensions={0} | all-to-all | bytes 294912 | tf_op jit(solution)/shard_map/all_to_all | solution.py:323
  109.1 9.2 %all_gather.3.e_ref = f32[384,384]{1,0:T(8,128)S(1)} all-gather(f32[96,384]{1,0:T(8,128)S(1)} %bitcast.30), channel_id=1, replica_groups={{0,16,32,48},{64,80,96,112},{128,144,160,176},{192,208,224,240},{256,27..., dimensions={0}, use_global_device_ids=true | all-gather | bytes 737280 | tf_op jit(solution)/shard_map/all_gather | solution.py:324
  118.4 1.1 mixing.1
  119.5 37.6 %all_to_all.22 = f32[48,4,8,128]{3,2,1,0:T(8,128)S(1)} all-to-all(f32[48,4,8,128]{3,2,1,0:T(8,128)S(1)} %mixing.1), channel_id=1, replica_groups=mesh['mem'=48,'slab'=16] {'mem'}, dimensions={0} | all-to-all | bytes 1572864 | tf_op jit(solution)/shard_map/all_to_all | solution.py:335
  157.1 1.5 add.33
  (22 shorter events, 0.8 us)
Async XLA Ops:
  0.0 8.1 %copy-start.1 = (f32[64,384]{1,0:T(8,128)S(1)}, f32[64,384]{1,0:T(8,128)}, u32[]{:S(2)}) copy-start(f32[64,384]{1,0:T(8,128)} %v_ref.5) | copy-start | bytes 294916
  0.0 8.1 %copy-start = (f32[8,64,384]{2,1,0:T(8,128)S(1)}, f32[8,64,384]{2,1,0:T(8,128)}, u32[]{:S(2)}) copy-start(f32[8,64,384]{2,1,0:T(8,128)} %last_ref.1) | copy-start | bytes 2359300
  0.0 8.1 %copy-start.2 = (f32[64,384]{1,0:T(8,128)S(1)}, f32[64,384]{1,0:T(8,128)}, u32[]{:S(2)}) copy-start(f32[64,384]{1,0:T(8,128)} %u_ref.1) | copy-start | bytes 294916
  1.1 9.1 %collective-permute-start = (f32[2,8,384]{2,1,0:T(8,128)S(1)}, f32[2,8,384]{2,1,0:T(8,128)S(1)}, u32[]{:S(2)}, u32[]{:S(2)}) collective-permute-start(f32[2,8,384]{2,1,0:T(8,128)S(1)} %get-tuple-element.15), channel_id=1, source_target_pairs={{0,1},{1,2},{2,3},{3,4},{4,5},{5,6},{6,7},{7,8},{8,9},{9,10},{10,1... | collective-permute-start | bytes 73736 | tf_op jit(solution)/shard_map/ppermute | solution.py:274
  6.1 7.2 %collective-permute-start.1 = (f32[3,8,384]{2,1,0:T(8,128)S(1)}, f32[3,8,384]{2,1,0:T(8,128)S(1)}, u32[]{:S(2)}, u32[]{:S(2)}) collective-permute-start(f32[3,8,384]{2,1,0:T(8,128)S(1)} %get-tuple-element.16), channel_id=1, source_target_pairs={{1,0},{2,1},{3,2},{4,3},{5,4},{6,5},{7,6},{8,7},{9,8},{10,9},{11,1... | collective-permute-start | bytes 110600 | tf_op jit(solution)/shard_map/ppermute | solution.py:275
  7.4 0.7 copy-start.7
  13.3 0.7 copy-start.4
  13.3 0.7 copy-start.5
  13.3 0.7 copy-start.6
  17.4 56.8 %all-to-all-start = ((f32[48,5,8,128]{3,2,1,0:T(8,128)}), f32[48,5,8,128]{3,2,1,0:T(8,128)S(1)}, u32[]{:S(2)}, u32[]{:S(2)}) async-start(f32[48,5,8,128]{3,2,1,0:T(8,128)} %get-tuple-element.18), calls=%async_computation | async-start | bytes 1966080 | tf_op jit(solution)/shard_map/all_to_all | solution.py:300
  34.8 6.2 %collective-permute-start.2 = (f32[8,8,128]{2,1,0:T(8,128)S(1)}, f32[8,8,128]{2,1,0:T(8,128)S(1)}, u32[]{:S(2)}, u32[]{:S(2)}) collective-permute-start(f32[8,8,128]{2,1,0:T(8,128)S(1)} %get-tuple-element.20), channel_id=1, source_target_pairs={{0,12},{1,13},{2,14},{3,15},{4,8},{5,9},{6,10},{7,11},{8,4},{9,5},... | collective-permute-start | bytes 98312 | tf_op jit(solution)/shard_map/ppermute | solution.py:240
  40.9 4.8 %collective-permute-start.3 = (f32[4,8,128]{2,1,0:T(8,128)S(1)}, f32[4,8,128]{2,1,0:T(8,128)S(1)}, u32[]{:S(2)}, u32[]{:S(2)}) collective-permute-start(f32[4,8,128]{2,1,0:T(8,128)S(1)} %get-tuple-element.22), channel_id=1, source_target_pairs={{0,4},{1,5},{2,6},{3,7},{4,0},{5,1},{6,2},{7,3},{8,12},{9,13},{10,... | collective-permute-start | bytes 49160 | tf_op jit(solution)/shard_map/ppermute | solution.py:240
  45.7 7.5 %collective-permute-start.4 = (f32[2,8,128]{2,1,0:T(8,128)S(1)}, f32[2,8,128]{2,1,0:T(8,128)S(1)}, u32[]{:S(2)}, u32[]{:S(2)}) collective-permute-start(f32[2,8,128]{2,1,0:T(8,128)S(1)} %get-tuple-element.24), channel_id=1, source_target_pairs={{0,3},{1,2},{2,1},{3,0},{4,7},{5,6},{6,5},{7,4},{8,11},{9,10},{10,... | collective-permute-start | bytes 24584 | tf_op jit(solution)/shard_map/ppermute | solution.py:240
  53.2 21.1 %copy-start.3 = (s32[16,16]{1,0:T(8,128)S(1)}, s32[16,16]{1,0:T(8,128)}, u32[]{:S(2)}) copy-start(s32[16,16]{1,0:T(8,128)} %mask_ref.1) | copy-start | bytes 3076
  53.2 6.5 %collective-permute-start.5 = (f32[1,8,128]{2,1,0:T(8,128)S(1)}, f32[1,8,128]{2,1,0:T(8,128)S(1)}, u32[]{:S(2)}, u32[]{:S(2)}) collective-permute-start(f32[1,8,128]{2,1,0:T(8,128)S(1)} %get-tuple-element.25), channel_id=1, source_target_pairs={{0,1},{1,0},{2,3},{3,2},{4,5},{5,4},{6,7},{7,6},{8,9},{9,8},{10,11... | collective-permute-start | bytes 12296 | tf_op jit(solution)/shard_map/ppermute | solution.py:240

commit v8 on v7

--- a/solution.py
+++ b/solution.py
@@ -45,7 +45,7 @@
     return jnp.maximum(v, 0.0) * (h_low + half_low) + jnp.minimum(v, 0.0) * (h_high - half_high)
 
 
-def inner_kernel(h_ref, u_ref, v_ref, f_ref, rim_ref):
+def inner_kernel(h_ref, u_ref, v_ref, values_ref, noise_ref, weights_ref, f_ref, rim_ref, seen_ref, share_ref):
     members, rows, cols = h_ref.shape
     per_row = cols // LANES
     batch = 8
@@ -92,6 +92,8 @@
             carry = (h_up, h_up2, d_up2, half_up, flux_up)
         for t in range(per_row):
             f_ref[r * per_row + t] = f[:, t * LANES : (t + 1) * LANES]
+    seen_ref[...] = values_ref[...] + noise_ref[...]
+    share_ref[...] = weights_ref[...].astype(jnp.float32)
     for i in range(4):
         rim_ref[i] = row(i)
         rim_ref[4 + i] = row(rows - 4 + i)
@@ -99,12 +101,12 @@
 
 def forecast_kernel(
     slab_ref, spot0_ref, spot1_ref, spot2_ref, spot3_ref, inner_ref, rim_ref, low_ref, high_ref, v_ref, weights_ref,
-    values_ref, noise_ref, cov_hbm,
+    seen_ref, cov_hbm,
     f_ref, pieces_ref, near_ref, far_ref, stack_ref, cov_ref, cov_sem,
 ):
     cov_copy = pltpu.make_async_copy(cov_hbm, cov_ref, cov_sem)
     cov_copy.start()
-    members = noise_ref.shape[0]
+    members = seen_ref.shape[0]
     rows, cols = v_ref.shape
     per_row = cols // LANES
     mems, tiles = pieces_ref.shape[0], pieces_ref.shape[1] - 1
@@ -147,14 +149,14 @@
 
     zero = jnp.zeros((members, LANES), jnp.float32)
     picked = lax.fori_loop(0, count, observe, (zero,) * foot, unroll=8)
-    weights = weights_ref[...].astype(jnp.float32)
+    weights = weights_ref[...]
     obs = picked[0] * weights[0:1]
     for k in range(1, foot):
         obs = obs + picked[k] * weights[k : k + 1]
     obs = obs / jnp.sum(weights, axis=0, keepdims=True)
     for p in range(mems):
         pieces_ref[p, tiles] = obs
-    innovation = values_ref[...] + noise_ref[...] - obs
+    innovation = seen_ref[...] - obs
     cov_copy.wait()
     white = jnp.dot(innovation, cov_ref[...], precision=HIGHEST, preferred_element_type=jnp.float32)
     order = swap_order(SLAB_SWAPS)
@@ -274,18 +276,23 @@
     low = lax.ppermute(down, "slab", [(i, i + 1) for i in range(slabs - 1)])
     high = lax.ppermute(up, "slab", [(i + 1, i) for i in range(slabs - 1)])
     speed = near(face_v)
-    inner, rim = pl.pallas_call(
+    inner, rim, seen, share = pl.pallas_call(
         inner_kernel,
-        in_specs=[vspec() for _ in range(3)],
-        out_specs=[vspec() for _ in range(2)],
-        out_shape=[v32(mems * tiles, members, LANES), v32(8, members, cols)],
+        in_specs=[vspec() for _ in range(6)],
+        out_specs=[vspec() for _ in range(4)],
+        out_shape=[
+            v32(mems * tiles, members, LANES),
+            v32(8, members, cols),
+            v32(members, LANES),
+            v32(*obs_weights.T.shape),
+        ],
         compiler_params=ROOM,
         name="inner",
-    )(near(thickness), near(face_u), speed)
+    )(near(thickness), near(face_u), speed, obs_values.reshape(1, -1), obs_noise, obs_weights.T)
 
     forecast, pieces, white, white_far = pl.pallas_call(
         forecast_kernel,
-        in_specs=[sspec() for _ in range(5)] + [vspec() for _ in range(8)] + [pl.BlockSpec(memory_space=pltpu.HBM)],
+        in_specs=[sspec() for _ in range(5)] + [vspec() for _ in range(7)] + [pl.BlockSpec(memory_space=pltpu.HBM)],
         out_specs=[vspec() for _ in range(4)],
         out_shape=[v32(mems * tiles, members, LANES), v32(mems, tiles + 1, members, LANES)]
         + [v32(slabs // 2, members, LANES) for _ in range(2)],
@@ -294,7 +301,7 @@
         name="forecast",
     )(
         slab, spots[0], spots[1], spots[2], spots[3], near(inner), near(rim), near(low), near(high), speed,
-        near(obs_weights.T), near(obs_values.reshape(1, -1)), near(obs_noise), away(cov_inverse),
+        near(share), near(seen), away(cov_inverse),
     )
 
     cell_state = lax.all_to_all(pieces, "mem", 0, 0, tiled=True)

time: 159 us -> 159 us (level)
  no operation moved by 1% of the time
where the time goes in v8:
time: 159 us; the launch traced here: 158 us
  blocking collectives  81.2 us (51%)
  starting transfers between devices  41.4 us (26%)
  waiting for transfers between devices  24.1 us (15%)
  Pallas kernels  10.2 us (6%)
    all_to_all x1, blocking collectives, local(): returned = lax.all_to_all(update, 'mem', 0, 0, tiled=True)  37.6 us
    all_to_all x1, blocking collectives, local(): parts = lax.all_to_all(parts, 'slab', 0, 0, tiled=True)  20.1 us
    ppermute x4, starting transfers between devices, swapped(): lax.ppermute(x, axis, [(i, i ^ k) for i in range(lax.axis_size(axis))])  17.8 us
    all_to_all x1, starting transfers between devices, local(): cell_state = lax.all_to_all(pieces, 'mem', 0, 0, tiled=True)  17.3 us
    all_to_all x1, waiting for transfers between devices, local(): cell_state = lax.all_to_all(pieces, 'mem', 0, 0, tiled=True)  14.6 us
    all_to_all x1, blocking collectives, local(): lax.all_to_all(copies, 'mem', 0, 0, tiled=True, axis_index_groups=columns)  14.3 us
    all_gather x1, blocking collectives, local(): lax.all_gather(over_z.reshape(depth * members, mems * members), 'mem', ax...  9.24 us
    ppermute x4, waiting for transfers between devices, swapped(): lax.ppermute(x, axis, [(i, i ^ k) for i in range(lax.axis_size(axis))])  7.05 us
  transfers between devices with their start and end apart: 7, of which 6 were waited for; matrix products, arithmetic and copies ran while one was open for 0% of the time, Pallas kernels for 1%

profile of v8, /device:TPU:1, one launch (start us, length us, event | category | flops | bytes accessed | tf_op | source)
XLA Modules:
  0.0 158.5 jit_solution(8781634837137851872)
XLA Ops:
  0.0 1.0 edges.1
  1.1 5.0 %collective-permute-start = (f32[2,8,384]{2,1,0:T(8,128)S(1)}, f32[2,8,384]{2,1,0:T(8,128)S(1)}, u32[]{:S(2)}, u32[]{:S(2)}) collective-permute-start(f32[2,8,384]{2,1,0:T(8,128)S(1)} %get-tuple-element.17), channel_id=1, source_target_pairs={{0,1},{1,2},{2,3},{3,4},{4,5},{5,6},{6,7},{7,8},{8,9},{9,10},{10,1... | collective-permute-start | bytes 73736 | tf_op jit(solution)/shard_map/ppermute | solution.py:276
  6.1 1.3 collective-permute-start.1
  7.4 0.7 copy-done.7
  8.8 2.0 %inner.1 = (f32[192,8,128]{2,1,0:T(8,128)S(1)}, f32[8,8,384]{2,1,0:T(8,128)S(1)}, f32[8,128]{1,0:T(8,128)S(1)}, f32[4,128]{1,0:T(4,128)S(1)}) custom-call(f32[8,64,384]{2,1,0:T(8,128)S(1)} %copy-done, f32[64,384]{1,0:T(8,128)S(1)} %copy-done.2, f32[64,384]{1,0:T(8,128)S(1)} %copy-done.1, f32[1,128]{1,0:T(1,128)S(1)} %bitcast.29, f32[8,128]{1,0:T(8,128)S(1)} %copy-done.4, ...), custom_call_target="tpu_custom_call" | custom-call | tf_op jit(solution)/shard_map/inner/pallas_call | solution.py:279
  10.8 2.4 %collective-permute-done.1.high_ref = f32[3,8,384]{2,1,0:T(8,128)S(1)} collective-permute-done((f32[3,8,384]{2,1,0:T(8,128)S(1)}, f32[3,8,384]{2,1,0:T(8,128)S(1)}, u32[]{:S(2)}, u32[]{:S(2)}) %collective-permute-start.1) | collective-permute-done | bytes 36896 | tf_op jit(solution)/shard_map/ppermute | solution.py:277
  13.3 3.5 %forecast.1 = (f32[192,8,128]{2,1,0:T(8,128)S(1)}, f32[48,5,8,128]{3,2,1,0:T(8,128)}, f32[8,8,128]{2,1,0:T(8,128)S(1)}, f32[8,8,128]{2,1,0:T(8,128)S(1)}) custom-call(s32[1]{0:T(128)} %bitcast.slab_ref, s32[128]{0:T(128)S(1)} %get-tuple-element.34.spot0_ref, s32[128]{0:T(128)S(1)} %get-tuple-element.33.spot1_ref, s32[128]{0:T(128)S(1)} %get-tuple-element.32.spot2_ref, ...), custom_call_target="tpu_custom_call" | custom-call | tf_op jit(solution)/shard_map/forecast/pallas_call | solution.py:293
  16.7 17.3 %all-to-all-start = ((f32[48,5,8,128]{3,2,1,0:T(8,128)}), f32[48,5,8,128]{3,2,1,0:T(8,128)S(1)}, u32[]{:S(2)}, u32[]{:S(2)}) async-start(f32[48,5,8,128]{3,2,1,0:T(8,128)} %get-tuple-element.22), calls=%async_computation | async-start | bytes 1966080 | tf_op jit(solution)/shard_map/all_to_all | solution.py:307
  34.1 5.2 %collective-permute-start.2 = (f32[8,8,128]{2,1,0:T(8,128)S(1)}, f32[8,8,128]{2,1,0:T(8,128)S(1)}, u32[]{:S(2)}, u32[]{:S(2)}) collective-permute-start(f32[8,8,128]{2,1,0:T(8,128)S(1)} %get-tuple-element.24), channel_id=1, source_target_pairs={{0,12},{1,13},{2,14},{3,15},{4,8},{5,9},{6,10},{7,11},{8,4},{9,5},... | collective-permute-start | bytes 98312 | tf_op jit(solution)/shard_map/ppermute | solution.py:242
  39.2 1.6 collective-permute-done.2
  40.8 1.9 %collective-permute-start.3 = (f32[4,8,128]{2,1,0:T(8,128)S(1)}, f32[4,8,128]{2,1,0:T(8,128)S(1)}, u32[]{:S(2)}, u32[]{:S(2)}) collective-permute-start(f32[4,8,128]{2,1,0:T(8,128)S(1)} %get-tuple-element.26), channel_id=1, source_target_pairs={{0,4},{1,5},{2,6},{3,7},{4,0},{5,1},{6,2},{7,3},{8,12},{9,13},{10,... | collective-permute-start | bytes 49160 | tf_op jit(solution)/shard_map/ppermute | solution.py:242
  42.8 2.8 %collective-permute-done.3 = f32[4,8,128]{2,1,0:T(8,128)S(1)} collective-permute-done((f32[4,8,128]{2,1,0:T(8,128)S(1)}, f32[4,8,128]{2,1,0:T(8,128)S(1)}, u32[]{:S(2)}, u32[]{:S(2)}) %collective-permute-start.3) | collective-permute-done | bytes 16416 | tf_op jit(solution)/shard_map/ppermute | solution.py:242
  45.6 5.5 %collective-permute-start.4 = (f32[2,8,128]{2,1,0:T(8,128)S(1)}, f32[2,8,128]{2,1,0:T(8,128)S(1)}, u32[]{:S(2)}, u32[]{:S(2)}) collective-permute-start(f32[2,8,128]{2,1,0:T(8,128)S(1)} %get-tuple-element.28), channel_id=1, source_target_pairs={{0,3},{1,2},{2,1},{3,0},{4,7},{5,6},{6,5},{7,4},{8,11},{9,10},{10,... | collective-permute-start | bytes 24584 | tf_op jit(solution)/shard_map/ppermute | solution.py:242
  51.1 1.3 collective-permute-done.4
  52.5 5.2 %collective-permute-start.5 = (f32[1,8,128]{2,1,0:T(8,128)S(1)}, f32[1,8,128]{2,1,0:T(8,128)S(1)}, u32[]{:S(2)}, u32[]{:S(2)}) collective-permute-start(f32[1,8,128]{2,1,0:T(8,128)S(1)} %get-tuple-element.29), channel_id=1, source_target_pairs={{0,1},{1,0},{2,3},{3,2},{4,5},{5,4},{6,7},{7,6},{8,9},{9,8},{10,11... | collective-permute-start | bytes 12296 | tf_op jit(solution)/shard_map/ppermute | solution.py:242
  57.7 1.3 collective-permute-done.5
  59.0 14.6 %all-to-all-done.x_ref = f32[48,5,8,128]{3,2,1,0:T(8,128)S(1)} async-done(((f32[48,5,8,128]{3,2,1,0:T(8,128)}), f32[48,5,8,128]{3,2,1,0:T(8,128)S(1)}, u32[]{:S(2)}, u32[]{:S(2)}) %all-to-all-start) | async-done | bytes 983072 | tf_op jit(solution)/shard_map/all_to_all | solution.py:307
  73.6 1.1 products.1
  74.6 20.1 %all_to_all.20.x_ref = f32[16,8,384]{2,1,0:T(8,128)S(1)} all-to-all(f32[16,8,384]{2,1,0:T(8,128)S(1)} %products.1), channel_id=1, replica_groups=mesh['mem'=48,'slab'=16] {'slab'}, dimensions={0} | all-to-all | bytes 393216 | tf_op jit(solution)/shard_map/all_to_all | solution.py:321
  94.7 14.3 %all_to_all.21 = f32[12,8,384]{2,1,0:T(8,128)S(1)} all-to-all(f32[12,8,384]{2,1,0:T(8,128)S(1)} %summed.1), channel_id=1, replica_groups={{0,64,128,192,256,320,384,448,512,576,640,704},{16,80,144,208,272,336,4..., dimensions={0} | all-to-all | bytes 294912 | tf_op jit(solution)/shard_map/all_to_all | solution.py:330
  109.0 9.2 %all_gather.3.e_ref = f32[384,384]{1,0:T(8,128)S(1)} all-gather(f32[96,384]{1,0:T(8,128)S(1)} %bitcast.30), channel_id=1, replica_groups={{0,16,32,48},{64,80,96,112},{128,144,160,176},{192,208,224,240},{256,27..., dimensions={0}, use_global_device_ids=true | all-gather | bytes 737280 | tf_op jit(solution)/shard_map/all_gather | solution.py:331
  118.3 1.1 mixing.1
  119.4 37.6 %all_to_all.22 = f32[48,4,8,128]{3,2,1,0:T(8,128)S(1)} all-to-all(f32[48,4,8,128]{3,2,1,0:T(8,128)S(1)} %mixing.1), channel_id=1, replica_groups=mesh['mem'=48,'slab'=16] {'mem'}, dimensions={0} | all-to-all | bytes 1572864 | tf_op jit(solution)/shard_map/all_to_all | solution.py:342
  157.0 1.5 add.33
  (22 shorter events, 0.7 us)
Async XLA Ops:
  0.0 8.1 %copy-start.1 = (f32[64,384]{1,0:T(8,128)S(1)}, f32[64,384]{1,0:T(8,128)}, u32[]{:S(2)}) copy-start(f32[64,384]{1,0:T(8,128)} %v_ref.5) | copy-start | bytes 294916
  0.0 8.1 %copy-start = (f32[8,64,384]{2,1,0:T(8,128)S(1)}, f32[8,64,384]{2,1,0:T(8,128)}, u32[]{:S(2)}) copy-start(f32[8,64,384]{2,1,0:T(8,128)} %last_ref.1) | copy-start | bytes 2359300
  0.0 8.1 %copy-start.2 = (f32[64,384]{1,0:T(8,128)S(1)}, f32[64,384]{1,0:T(8,128)}, u32[]{:S(2)}) copy-start(f32[64,384]{1,0:T(8,128)} %u_ref.1) | copy-start | bytes 294916
  1.1 9.8 %collective-permute-start = (f32[2,8,384]{2,1,0:T(8,128)S(1)}, f32[2,8,384]{2,1,0:T(8,128)S(1)}, u32[]{:S(2)}, u32[]{:S(2)}) collective-permute-start(f32[2,8,384]{2,1,0:T(8,128)S(1)} %get-tuple-element.17), channel_id=1, source_target_pairs={{0,1},{1,2},{2,3},{3,4},{4,5},{5,6},{6,7},{7,8},{8,9},{9,10},{10,1... | collective-permute-start | bytes 73736 | tf_op jit(solution)/shard_map/ppermute | solution.py:276
  6.1 7.2 %collective-permute-start.1 = (f32[3,8,384]{2,1,0:T(8,128)S(1)}, f32[3,8,384]{2,1,0:T(8,128)S(1)}, u32[]{:S(2)}, u32[]{:S(2)}) collective-permute-start(f32[3,8,384]{2,1,0:T(8,128)S(1)} %get-tuple-element.18), channel_id=1, source_target_pairs={{1,0},{2,1},{3,2},{4,3},{5,4},{6,5},{7,6},{8,7},{9,8},{10,9},{11,1... | collective-permute-start | bytes 110600 | tf_op jit(solution)/shard_map/ppermute | solution.py:277
  7.4 0.7 copy-start.7
  8.1 0.7 copy-start.4
  8.1 0.7 copy-start.5
  8.1 0.7 copy-start.6
  16.7 56.8 %all-to-all-start = ((f32[48,5,8,128]{3,2,1,0:T(8,128)}), f32[48,5,8,128]{3,2,1,0:T(8,128)S(1)}, u32[]{:S(2)}, u32[]{:S(2)}) async-start(f32[48,5,8,128]{3,2,1,0:T(8,128)} %get-tuple-element.22), calls=%async_computation | async-start | bytes 1966080 | tf_op jit(solution)/shard_map/all_to_all | solution.py:307
  34.1 6.8 %collective-permute-start.2 = (f32[8,8,128]{2,1,0:T(8,128)S(1)}, f32[8,8,128]{2,1,0:T(8,128)S(1)}, u32[]{:S(2)}, u32[]{:S(2)}) collective-permute-start(f32[8,8,128]{2,1,0:T(8,128)S(1)} %get-tuple-element.24), channel_id=1, source_target_pairs={{0,12},{1,13},{2,14},{3,15},{4,8},{5,9},{6,10},{7,11},{8,4},{9,5},... | collective-permute-start | bytes 98312 | tf_op jit(solution)/shard_map/ppermute | solution.py:242
  40.8 4.8 %collective-permute-start.3 = (f32[4,8,128]{2,1,0:T(8,128)S(1)}, f32[4,8,128]{2,1,0:T(8,128)S(1)}, u32[]{:S(2)}, u32[]{:S(2)}) collective-permute-start(f32[4,8,128]{2,1,0:T(8,128)S(1)} %get-tuple-element.26), channel_id=1, source_target_pairs={{0,4},{1,5},{2,6},{3,7},{4,0},{5,1},{6,2},{7,3},{8,12},{9,13},{10,... | collective-permute-start | bytes 49160 | tf_op jit(solution)/shard_map/ppermute | solution.py:242
  45.6 6.9 %collective-permute-start.4 = (f32[2,8,128]{2,1,0:T(8,128)S(1)}, f32[2,8,128]{2,1,0:T(8,128)S(1)}, u32[]{:S(2)}, u32[]{:S(2)}) collective-permute-start(f32[2,8,128]{2,1,0:T(8,128)S(1)} %get-tuple-element.28), channel_id=1, source_target_pairs={{0,3},{1,2},{2,1},{3,0},{4,7},{5,6},{6,5},{7,4},{8,11},{9,10},{10,... | collective-permute-start | bytes 24584 | tf_op jit(solution)/shard_map/ppermute | solution.py:242
  52.5 21.1 %copy-start.3 = (s32[16,16]{1,0:T(8,128)S(1)}, s32[16,16]{1,0:T(8,128)}, u32[]{:S(2)}) copy-start(s32[16,16]{1,0:T(8,128)} %mask_ref.1) | copy-start | bytes 3076
  52.5 6.5 %collective-permute-start.5 = (f32[1,8,128]{2,1,0:T(8,128)S(1)}, f32[1,8,128]{2,1,0:T(8,128)S(1)}, u32[]{:S(2)}, u32[]{:S(2)}) collective-permute-start(f32[1,8,128]{2,1,0:T(8,128)S(1)} %get-tuple-element.29), channel_id=1, source_target_pairs={{0,1},{1,0},{2,3},{3,2},{4,5},{5,4},{6,7},{7,6},{8,9},{9,8},{10,11... | collective-permute-start | bytes 12296 | tf_op jit(solution)/shard_map/ppermute | solution.py:242
